TPU v7x, 768 devices: a whole 4x8x12 slice. The times are simulated.
768 devices in a mesh: dp: 32 (over x, y), seq: 24 (over z, core).
Axes of the slice: x: 4, y: 8, z: 12, core: 2. Of those that a mesh axis runs over, the one named last changes fastest.
Arguments:
- grad_rows: bfloat16 [32, 1920, 4, 1280], P('dp', 'seq'), may hold values from -6 to 6
- row_owner: int32 [32, 1920, 1], P('dp', 'seq'), may hold values from 0 to 23; in each aligned block of 80 rows (0 to 79, 80 to 159, ..., all dimensions but the last counted through in order) at most 4 rows name the same one
- acts: bfloat16 [32, 24, 96, 4, 1280], P('dp', 'seq'), may hold values from -6 to 6
- xact: bfloat16 [32, 24, 96, 4, 1280], P('dp', 'seq'), may hold values from -72 to 72
- gamma: float32 [1280], replicated, may hold values from 0.25 to 1.75
- w_out: bfloat16 [1280, 1280], replicated, may hold values from -0.15625 to 0.15625
Outputs:
- attn_grad: bfloat16 [32, 24, 96, 4, 1280], P('dp', 'seq')
- weight_grad: float32 [1280, 1280], P('dp')
- gain_grad: float32 [1280], replicated
Inputs may be any that keep to these rules, and one draw needn't show every extreme that they name: `row_owner`: within the rows of one device (each aligned block of 80 rows) no owner is named more than 4 times, a bound that some block reaches.
All inputs are finite; a program needn't handle non-finite values.
Results may differ from a plain program's by a relative error of at most 0.0049.
Values may be sent and summed in bfloat16 or wider, within the bound.
No kernel may reach another device: no remote copies, remote signals or barrier semaphores. Data moves between devices by JAX's collectives and lax.ppermute only.
A program may use at most 64 MiB of HBM per device.

v0:
```python
import jax
import jax.numpy as jnp
from jax import lax
from jax.sharding import Mesh
from jax.sharding import PartitionSpec as P

DP = ("dp_0", "dp_1")


epsilon = 1e-06


def summed_rows(total, axes):
    for axis in axes:
        total = lax.psum_scatter(total, axis, scatter_dimension=0, tiled=True)
    return total


def over_pieces(array, axis):
    return lax.all_gather(array, axis).sum(0)


def copy_for_each(array, axis):
    length = lax.axis_size(axis)
    return lax.all_to_all(
        jnp.broadcast_to(array[None], (length, *array.shape)), axis, 0, 0, tiled=True
    )


def over_copies(array, axis):
    return copy_for_each(array, axis).sum(axis=0)


def in_one(arrays, axis):
    ends = [0]
    for a in arrays:
        ends.append(ends[-1] + a.size)
    total = over_copies(jnp.concatenate([a.ravel() for a in arrays]), axis)
    return tuple((total[b:e].reshape(a.shape) for a, b, e in zip(arrays, ends, ends[1:])))


def slot_table(owners, buckets, capacity):
    picked = (owners[:, None] == jnp.arange(buckets, dtype=jnp.int32)[None, :]).astype(jnp.int32)
    before = jnp.cumsum(picked, axis=0) - picked
    ranking = jnp.sum(before * picked, axis=1)
    target = owners * capacity + ranking
    places = jnp.arange(buckets * capacity, dtype=jnp.int32)
    return (places[:, None] == target[None, :]).astype(jnp.bfloat16)


def norm_backward(upstream, inputs, gamma):
    values = inputs.astype(jnp.float32)
    inverse = lax.rsqrt(jnp.mean(values * values, axis=1, keepdims=True) + epsilon)
    normed = values * inverse
    gradient = upstream.astype(jnp.float32)
    gain_part = jnp.sum(gradient * normed, axis=0)
    scaled = gamma * gradient
    centre = jnp.mean(scaled * normed, axis=1, keepdims=True)
    patch_grad = (inverse * (scaled - normed * centre)).astype(jnp.bfloat16)
    return (patch_grad, gain_part)


def project_back(patch_grad, w_out):
    return lax.dot_general(
        patch_grad, w_out, (((1,), (1,)), ((), ())), preferred_element_type=jnp.float32
    ).astype(jnp.bfloat16)


def on_device(grad_rows, row_owner, acts, xact, gamma, w_out):
    seq_count = lax.axis_size("seq")
    slot_count = acts.shape[2]
    capacity = slot_count // seq_count
    patches = acts.shape[3]
    features = acts.shape[4]
    tok_rows = grad_rows.shape[1]
    placing = slot_table(row_owner[0, :, 0], seq_count, capacity)
    outgoing = jnp.dot(
        placing, grad_rows.reshape(tok_rows, patches * features), preferred_element_type=jnp.float32
    ).astype(jnp.bfloat16)
    received = lax.all_to_all(
        outgoing.reshape(seq_count, capacity, patches, features),
        "seq",
        split_axis=0,
        concat_axis=0,
        tiled=True,
    )
    upstream = received.reshape(slot_count * patches, features)
    act_rows = acts.reshape(slot_count * patches, features)
    patch_grad, gain_part = norm_backward(
        upstream, xact.reshape(slot_count * patches, features), gamma
    )
    attn_grad = project_back(patch_grad, w_out).reshape(acts.shape)
    weight_part = summed_rows(
        lax.dot_general(
            act_rows, patch_grad, (((0,), (0,)), ((), ())), preferred_element_type=jnp.float32
        ),
        DP,
    )
    weight_sum, gain_seq = (over_pieces(weight_part, "seq"), over_pieces(gain_part, "seq"))
    square_total, gain_sum = in_one((jnp.sum(weight_sum * weight_sum), gain_seq), DP)
    norm_total = jnp.sqrt(square_total + jnp.sum(gain_sum * gain_sum) + epsilon)
    factor = jnp.float32(features) / norm_total
    return (attn_grad, weight_sum * factor, gain_sum * factor)


def solution(mesh):
    finer = Mesh(mesh.devices.reshape(4, 8, mesh.shape["seq"]), ("dp_0", "dp_1", "seq"))
    placed = (
        P(DP, "seq", None, None),
        P(DP, "seq", None),
        P(DP, "seq", None, None, None),
        P(DP, "seq", None, None, None),
        P(),
        P(),
    )
    return jax.shard_map(
        on_device,
        mesh=finer,
        in_specs=placed,
        out_specs=(P(DP, "seq", None, None, None), P(DP, None), P()),
        check_vma=False,
    )
```

profile of v0, /device:TPU:1, one launch (start us, length us, event | category | flops | bytes accessed | tf_op | source)
XLA Modules:
  0.0 313.2 jit_solution(1764706199901293244)
XLA Ops:
  7.2 0.0 copy-start
  7.2 0.9 fusion.3
  8.1 0.1 reduce_window_sum.11
  8.2 0.8 select_reduce_fusion
  9.0 0.7 multiply_add_fusion
  9.7 1.2 copy.21
  10.9 1.3 convolution_convert_fusion
  12.3 3.0 reshape.119
  15.2 16.7 %all-to-all-start = ((bf16[24,4,4,1280]{3,2,1,0:T(4,128)(2,1)}), bf16[24,4,4,1280]{3,2,1,0:T(4,128)(2,1)}, u32[]{:S(2)}, u32[]{:S(2)}) async-start(bf16[24,4,4,1280]{3,2,1,0:T(4,128)(2,1)} %reshape.119), calls=%async_computation | async-start | bytes 1966080 | tf_op jit(solution)/shard_map/all_to_all | solution.py:80
  31.9 0.0 reduce-scatter.7.cloned.1.call-start
  32.0 2.5 reshape.121
  34.5 2.8 convert_element_type.46
  37.3 0.0 copy-done.2
  37.3 0.6 multiply_reduce_fusion.2
  37.9 30.8 %all-to-all-done = bf16[24,4,4,1280]{3,2,1,0:T(4,128)(2,1)} async-done(((bf16[24,4,4,1280]{3,2,1,0:T(4,128)(2,1)}), bf16[24,4,4,1280]{3,2,1,0:T(4,128)(2,1)}, u32[]{:S(2)}, u32[]{:S(2)}) %all-to-all-start) | async-done | bytes 983072 | tf_op jit(solution)/shard_map/all_to_all | solution.py:80
  68.7 0.0 copy-done.3
  68.7 3.5 %multiply_reduce_fusion = (f32[1280]{0:T(1024)S(1)}, f32[24,4,4]{2,1,0:T(4,128)S(1)}) fusion(f32[24,4,4,1280]{3,2,1,0:T(4,128)} %bitcast.18, bf16[24,4,4,1280]{3,2,1,0:T(4,128)(2,1)} %all-to-all-done, f32[24,4,4]{2,1,0:T(4,128)S(1)} %bitcast.23, f32[1280]{0:T(1024)S(1)} %copy-done.3), kind=kLoop, calls=%fused_computation.3 | loop fusion | flops 3438976 | bytes 2962432 | tf_op jit(solution)/shard_map/reduce_sum | solution.py:56
  72.3 3.1 multiply_convert_fusion
  75.4 2.5 convert_element_type.59
  77.9 6.1 %convolution_bitcast_fusion = f32[1280,1280]{0,1:T(8,128)} fusion(bf16[384,1280]{1,0:T(8,128)(2,1)} %convert_element_type.59, bf16[384,1280]{1,0:T(8,128)(2,1)} %reshape.121), kind=kOutput, calls=%fused_computation | convolution fusion | flops 1258291200 | bytes 8519680 | tf_op jit(solution)/shard_map/dot_general | solution.py:94
  84.0 8.2 %copy.14 = f32[1280,1280]{1,0:T(8,128)} copy(f32[1280,1280]{0,1:T(8,128)} %convolution_bitcast_fusion) | data formatting | bytes 13107200
  92.2 0.0 reduce-scatter.7.cloned.1.call-update
  92.2 0.0 reduce-scatter.9.cloned.1.call-start
  92.2 71.4 %reduce-scatter.7.cloned.1.call-done = f32[320,1280]{1,0:T(8,128)} async-done(((f32[1280,1280]{1,0:T(8,128)}), f32[320,1280]{1,0:T(8,128)}) %reduce-scatter.7.cloned.1.call-update) | async-done | bytes 1638416
  163.6 0.0 reduce-scatter.9.cloned.1.call-update
  163.6 0.0 all-gather.5.cloned.1.call-start
  163.7 45.0 %reduce-scatter.9.cloned.1.call-done = f32[40,1280]{1,0:T(8,128)} async-done(((f32[320,1280]{1,0:T(8,128)}), f32[40,1280]{1,0:T(8,128)}) %reduce-scatter.9.cloned.1.call-update) | async-done | bytes 204816 | tf_op jit(solution)/shard_map/reduce_scatter | solution.py:15
  208.7 0.0 all-gather.5.cloned.1.call-update
  208.8 0.1 rsqrt.17
  208.9 2.7 reshape.125
  211.5 0.1 div.13
  211.6 29.9 %all-gather.2 = f32[24,1,1280]{2,1,0:T(1,128)S(1)} all-gather(f32[1,1,1280]{2,1,0:T(1,128)S(1)} %reshape.129), channel_id=3, replica_groups=mesh['dp_0'=4,'dp_1'=8,'seq'=24] {'seq'}, dimensions={0}, use_global_device_ids=true | all-gather | bytes 128000 | tf_op jit(solution)/shard_map/all_gather | solution.py:20
  241.5 0.1 reduce_sum.87
  241.6 2.7 reshape.124
  244.3 34.0 %all-gather.5.cloned.1.call-done = f32[960,1280]{1,0:T(8,128)} async-done(((f32[40,1280]{1,0:T(8,128)}), f32[960,1280]{1,0:T(8,128)}) %all-gather.5.cloned.1.call-update) | async-done | bytes 4915216 | tf_op jit(solution)/shard_map/all_gather | solution.py:20
  278.3 2.6 reduce_sum.84
  281.0 0.7 multiply_reduce_fusion.3
  281.6 0.7 pad_maximum_fusion
  282.3 0.8 broadcast_in_dim.2
  283.1 9.5 %all-to-all-start.1 = ((f32[32,1,1281]{2,1,0:T(1,128)}), f32[32,1,1281]{2,1,0:T(1,128)}, u32[]{:S(2)}, u32[]{:S(2)}) async-start(f32[32,1,1281]{2,1,0:T(1,128)} %broadcast_in_dim.2), calls=%async_computation.1 | async-start | bytes 360448 | tf_op jit(solution)/shard_map/all_to_all | solution.py:25
  292.6 4.7 %convolution_convert_fusion.1 = bf16[384,1280]{1,0:T(8,128)(2,1)} fusion(bf16[1280,1280]{1,0:T(8,128)(2,1)S(1)} %copy-done, f32[384,1280]{1,0:T(8,128)} %reshape.125, f32[384,1280]{1,0:T(8,128)} %reshape.124, f32[384]{0:T(512)S(1)} %div.13, f32[1280]{0:T(1024)S(1)} %copy-done.3, f32[384]{0:T(512)S(1)} %rsqrt.17), kind=kOutput, calls=%fused_computation.2 | convolution fusion | flops 1261731840 | bytes 8200192 | tf_op jit(solution)/shard_map/dot_general | solution.py:64
  297.2 2.6 reshape.120
  299.8 1.9 all-to-all-done.1
  301.7 1.0 reduce_sum.88
  302.7 0.7 multiply_reduce_fusion.4
  303.4 0.5 slice.8
  305.3 0.7 slice_multiply_fusion
  305.9 0.7 broadcast_multiply_fusion
  (8 shorter events, 0.0 us)
Async XLA Ops:
  7.2 285.4 %copy-start = (bf16[1280,1280]{1,0:T(8,128)(2,1)S(1)}, bf16[1280,1280]{1,0:T(8,128)(2,1)}, u32[]{:S(2)}) copy-start(bf16[1280,1280]{1,0:T(8,128)(2,1)} %param.11) | copy-start | bytes 9830404
  15.2 53.5 %all-to-all-start = ((bf16[24,4,4,1280]{3,2,1,0:T(4,128)(2,1)}), bf16[24,4,4,1280]{3,2,1,0:T(4,128)(2,1)}, u32[]{:S(2)}, u32[]{:S(2)}) async-start(bf16[24,4,4,1280]{3,2,1,0:T(4,128)(2,1)} %reshape.119), calls=%async_computation | async-start | bytes 1966080 | tf_op jit(solution)/shard_map/all_to_all | solution.py:80
  31.9 131.7 %reduce-scatter.7.cloned.1.call-start = ((), (), s32[]{:S(2)}) async-start(), calls=%async_computation.5 | async-start | bytes 8192000
  34.4 2.8 copy-start.2
  34.4 34.2 %copy-start.3 = (f32[1280]{0:T(1024)S(1)}, f32[1280]{0:T(1024)}, u32[]{:S(2)}) copy-start(f32[1280]{0:T(1024)} %param.10) | copy-start | bytes 15364
  68.7 3.6 %copy-start.1 = (f32[1,1,96,4,1280]{4,3,2,1,0:T(4,128)S(1)}, f32[1,1,96,4,1280]{4,3,2,1,0:T(4,128)}, u32[]{:S(2)}) copy-start(f32[1,1,96,4,1280]{4,3,2,1,0:T(4,128)} %convert_element_type.46) | copy-start | bytes 5898244
  92.2 116.5 %reduce-scatter.9.cloned.1.call-start = ((), (), s32[]{:S(2)}) async-start(), calls=%async_computation.6 | async-start | bytes 1843200 | tf_op jit(solution)/shard_map/reduce_scatter | solution.py:15
  163.6 114.7 %all-gather.5.cloned.1.call-start = ((), (), s32[]{:S(2)}) async-start(), calls=%async_computation.4 | async-start | bytes 5120000 | tf_op jit(solution)/shard_map/all_gather | solution.py:20
  283.1 18.6 %all-to-all-start.1 = ((f32[32,1,1281]{2,1,0:T(1,128)}), f32[32,1,1281]{2,1,0:T(1,128)}, u32[]{:S(2)}, u32[]{:S(2)}) async-start(f32[32,1,1281]{2,1,0:T(1,128)} %broadcast_in_dim.2), calls=%async_computation.1 | async-start | bytes 360448 | tf_op jit(solution)/shard_map/all_to_all | solution.py:25
Sparse Core Ops, SparseCore 0:
  92.3 71.2 reduce-scatter.6
  166.8 41.9 reduce-scatter.8
  211.2 67.1 all-gather.4
where the time goes:
time: 315 us; the launch traced here: 313 us
  waiting for transfers between devices  183 us (58%)
  blocking collectives  29.9 us (9%)
  local copies, waits for them, and re-layouts  26.8 us (9%)
  starting transfers between devices  26.3 us (8%)
  other arithmetic  19.7 us (6%)
  between operations  15.2 us (5%)
  matrix products  12.2 us (4%)
    unnamed x4, waiting for transfers between devices  71.4 us
    reduce_scatter x1, waiting for transfers between devices, summed_rows(): total = lax.psum_scatter(total, axis, scatter_dimension=0, tiled=True)  45 us
    all_gather x1, waiting for transfers between devices, over_pieces(): return lax.all_gather(array, axis).sum(0)  34 us
    all_to_all x1, waiting for transfers between devices, on_device(): lax.all_to_all(outgoing.reshape(seq_count, capacity, patches, features),...  30.8 us
    all_gather x1, blocking collectives, over_pieces(): return lax.all_gather(array, axis).sum(0)  29.9 us
    all_to_all x1, starting transfers between devices, on_device(): lax.all_to_all(outgoing.reshape(seq_count, capacity, patches, features),...  16.7 us
    all_to_all x1, starting transfers between devices, copy_for_each(): lax.all_to_all(jnp.broadcast_to(array[None], (length, *array.shape)), axi...  9.46 us
    unnamed x11, local copies, waits for them, and re-layouts  9.43 us
  transfers between devices with their start and end apart: 5, of which 5 were waited for; matrix products, arithmetic and copies ran while one was open for 6% of the time, Pallas kernels for 0%

commit v1 on v0

v1 whole, which is shorter than its diff:
```python
import functools

import jax
import jax.numpy as jnp
from jax import lax
from jax.experimental import pallas as pl
from jax.experimental.pallas import tpu as pltpu
from jax.sharding import Mesh
from jax.sharding import PartitionSpec as P

DP = ("dp_0", "dp_1")
SEQ = ("z", "core")

epsilon = 1e-06


def copies(array, axes):
    count = lax.axis_size(axes)
    sent = jnp.broadcast_to(array[None], (count, *array.shape))
    return lax.all_to_all(sent, axes, 0, 0, tiled=True)


def summed_blocks(total, axis):
    count = lax.axis_size(axis)
    blocks = total.reshape(count, total.shape[0] // count, *total.shape[1:])
    return lax.all_to_all(blocks, axis, 0, 0, tiled=True).astype(jnp.float32).sum(0)


def slot_targets(owners, buckets, capacity):
    picked = (owners[:, None] == jnp.arange(buckets, dtype=jnp.int32)[None, :]).astype(jnp.int32)
    before = jnp.cumsum(picked, axis=0) - picked
    ranking = jnp.sum(before * picked, axis=1)
    return owners * capacity + ranking


def norm_kernel(step, core_ref, recv_ref, xact_ref, gamma_ref, grad_ref, keep_ref, send_ref, gain_ref):
    rows, features = recv_ref.shape
    half = features // 2
    mine = pl.multiple_of(core_ref[0] * half, half)
    other = pl.multiple_of((1 - core_ref[0]) * half, half)
    gain_ref[...] = jnp.zeros_like(gain_ref)
    gamma = gamma_ref[...]

    def body(i, carry):
        at = pl.ds(pl.multiple_of(i * step, step), step)
        values = xact_ref[at, :].astype(jnp.float32)
        gradient = recv_ref[at, :].astype(jnp.float32)
        inverse = lax.rsqrt(jnp.mean(values * values, axis=1, keepdims=True) + epsilon)
        normed = values * inverse
        gain_ref[...] += (gradient * normed).reshape(step // 8, 8, features).sum(0)
        scaled = gamma * gradient
        centre = jnp.mean(scaled * normed, axis=1, keepdims=True)
        grad_ref[at, :] = (inverse * (scaled - normed * centre)).astype(jnp.bfloat16)
        keep_ref[at, :] = grad_ref[at, pl.ds(mine, half)]
        send_ref[at, :] = grad_ref[at, pl.ds(other, half)]
        return carry

    lax.fori_loop(0, rows // step, body, 0)


def norm_backward(core, upstream, inputs, gamma):
    rows, features = upstream.shape
    whole = pl.BlockSpec(memory_space=pltpu.VMEM)
    return pl.pallas_call(
        functools.partial(norm_kernel, 16),
        out_shape=(
            jax.ShapeDtypeStruct((rows, features), jnp.bfloat16),
            jax.ShapeDtypeStruct((rows, features // 2), jnp.bfloat16),
            jax.ShapeDtypeStruct((rows, features // 2), jnp.bfloat16),
            jax.ShapeDtypeStruct((8, features), jnp.float32),
        ),
        in_specs=[pl.BlockSpec(memory_space=pltpu.SMEM), whole, whole, whole],
        out_specs=(whole, whole, whole, whole),
        name="norm_backward",
        compiler_params=pltpu.CompilerParams(vmem_limit_bytes=12 * 1024 * 1024),
        cost_estimate=pl.CostEstimate(flops=14 * rows * features, bytes_accessed=8 * rows * features, transcendentals=rows),
    )(core, upstream, inputs, gamma.reshape(1, features))


def on_device(grad_rows, row_owner, acts, xact, gamma, w_out):
    seq_count = lax.axis_size(SEQ)
    slot_count, patches, features = acts.shape[2:]
    capacity = slot_count // seq_count
    rows = slot_count * patches
    core = lax.axis_index("core")
    swap = [(0, 1), (1, 0)]

    target = slot_targets(row_owner[0, :, 0], seq_count, capacity)
    places = (target[:, None] * patches + jnp.arange(patches, dtype=jnp.int32)[None, :]).reshape(-1)
    placing = (jnp.arange(rows, dtype=jnp.int32)[:, None] == places[None, :]).astype(jnp.bfloat16)
    outgoing = jnp.dot(
        placing, grad_rows.reshape(-1, features), preferred_element_type=jnp.float32
    ).astype(jnp.bfloat16)
    received = lax.all_to_all(
        outgoing.reshape(seq_count, capacity * patches, features), SEQ, 0, 0, tiled=True
    ).reshape(rows, features)

    act_rows = acts.reshape(rows, features)
    act_pair = lax.ppermute(act_rows, "core", swap)
    xact_rows = xact.reshape(rows, features)

    grad, grad_keep, grad_send, gain_part = norm_backward(
        jnp.reshape(core, (1,)).astype(jnp.int32), received, xact_rows, gamma
    )
    grad_pair = lax.ppermute(grad_send, "core", swap)

    def outer(left, right):
        return lax.dot_general(left, right, (((0,), (0,)), ((), ())), preferred_element_type=jnp.float32)

    weight_pair = (outer(act_rows, grad_keep) + outer(act_pair, grad_pair)).astype(jnp.bfloat16)
    weight_x = summed_blocks(weight_pair, "dp_0").astype(jnp.bfloat16)
    attn_grad = lax.dot_general(
        grad, w_out, (((1,), (1,)), ((), ())), preferred_element_type=jnp.float32
    ).astype(jnp.bfloat16).reshape(acts.shape)
    weight_y = summed_blocks(weight_x, "dp_1")

    z_count = lax.axis_size("z")
    out_rows, half = weight_y.shape
    padded = -(-out_rows // z_count) * z_count
    weight_y = jnp.pad(weight_y, ((0, padded - out_rows), (0, 0))).astype(jnp.bfloat16)
    piece = summed_blocks(weight_y, "z")

    gain_seq = copies(gain_part.sum(0), SEQ).sum(0)
    squares = jnp.sum(piece * piece)
    pieces = copies(piece, SEQ).reshape(z_count, 2, padded // z_count, half)
    weight_sum = pieces.transpose(0, 2, 1, 3).reshape(padded, features)[:out_rows]
    squares = jnp.sum(weight_sum * weight_sum)
    both = copies(jnp.concatenate([gain_seq, jnp.full((128,), squares)]), DP).sum(0)
    gain_sum, square_total = both[:features], both[features]
    norm_total = jnp.sqrt(square_total + jnp.sum(gain_sum * gain_sum) + epsilon)
    factor = jnp.float32(features) / norm_total
    return (attn_grad, weight_sum * factor, gain_sum * factor)


def solution(mesh):
    finer = Mesh(mesh.devices.reshape(4, 8, mesh.shape["seq"] // 2, 2), (*DP, *SEQ))
    placed = (
        P(DP, SEQ, None, None),
        P(DP, SEQ, None),
        P(DP, SEQ, None, None, None),
        P(DP, SEQ, None, None, None),
        P(),
        P(),
    )
    return jax.shard_map(
        on_device,
        mesh=finer,
        in_specs=placed,
        out_specs=(P(DP, SEQ, None, None, None), P(DP, None), P()),
        check_vma=False,
    )
```

time: 315 us -> 211 us (0.67)
  waiting for transfers between devices: 183 us -> 68 us
  starting transfers between devices: 26.3 us -> 43.2 us
  blocking collectives: 29.9 us -> 46.6 us
  between operations: 15.2 us -> 2.16 us
  other arithmetic: 19.7 us -> 10.2 us
  local copies, waits for them, and re-layouts: 26.8 us -> 20.4 us
  Pallas kernels: 0 us -> 6.2 us
    unnamed x4 -> x0, waiting for transfers between devices: 71.4 us -> none
    all_to_all x0 -> x2, blocking collectives: none -> 46.6 us  [summed_blocks(): lax.all_to_all(blocks, axis, 0, 0, tiled=True).astype(jnp.float32).sum(0)]
    reduce_scatter x1 -> x0, waiting for transfers between devices: 45 us -> none  [summed_rows(): total = lax.psum_scatter(total, axis, scatter_dimension=0, tiled=True)]
    all_to_all x2 -> x5, waiting for transfers between devices: 32.7 us -> 68 us  [the longest x1 29.7 us: on_device(): lax.all_to_all(outgoing.reshape(seq_count, capacity * patches, features),...]
    all_gather x1 -> x0, waiting for transfers between devices: 34 us -> none  [over_pieces(): return lax.all_gather(array, axis).sum(0)]
    all_gather x1 -> x0, blocking collectives: 29.9 us -> none  [over_pieces(): return lax.all_gather(array, axis).sum(0)]
    all_to_all x2 -> x5, starting transfers between devices: 26.2 us -> 36.5 us  [the longest x1 16.7 us: on_device(): lax.all_to_all(outgoing.reshape(seq_count, capacity * patches, features),...]
    ppermute x0 -> x2, starting transfers between devices: none -> 6.68 us  [the longest x1 4.54 us: on_device(): grad_pair = lax.ppermute(grad_send, 'core', swap)]
  transfers between devices with their start and end apart: 5 -> 7, of which waited for: 5 -> 5; matrix products, arithmetic and copies ran while one was open for 6% -> 7% of each run, Pallas kernels for 0% -> 3%
where the time goes in v1:
time: 211 us; the launch traced here: 209 us
  waiting for transfers between devices  68 us (32%)
  blocking collectives  46.6 us (22%)
  starting transfers between devices  43.2 us (20%)
  local copies, waits for them, and re-layouts  20.4 us (10%)
  matrix products  12.1 us (6%)
  other arithmetic  10.2 us (5%)
  Pallas kernels  6.2 us (3%)
  between operations  2.16 us (1%)
    all_to_all x2, blocking collectives, summed_blocks(): lax.all_to_all(blocks, axis, 0, 0, tiled=True).astype(jnp.float32).sum(0)  46.6 us
    all_to_all x1, waiting for transfers between devices, on_device(): lax.all_to_all(outgoing.reshape(seq_count, capacity * patches, features),...  29.7 us
    all_to_all x3, waiting for transfers between devices, copies(): return lax.all_to_all(sent, axes, 0, 0, tiled=True)  28.6 us
    all_to_all x1, starting transfers between devices, on_device(): lax.all_to_all(outgoing.reshape(seq_count, capacity * patches, features),...  16.7 us
    all_to_all x3, starting transfers between devices, copies(): return lax.all_to_all(sent, axes, 0, 0, tiled=True)  16.3 us
    all_to_all x1, waiting for transfers between devices, summed_blocks(): lax.all_to_all(blocks, axis, 0, 0, tiled=True).astype(jnp.float32).sum(0)  9.77 us
    pallas_call x1, Pallas kernels, norm_backward(): pl.pallas_call(functools.partial(norm_kernel, 16), out_shape=(jax.ShapeDt...  6.2 us
    dot_general x2, matrix products, outer(): lax.dot_general(left, right, (((0,), (0,)), ((), ())), preferred_element_...  5.75 us
  transfers between devices with their start and end apart: 7, of which 5 were waited for; matrix products, arithmetic and copies ran while one was open for 7% of the time, Pallas kernels for 3%

profile of v1, /device:TPU:1, one launch (start us, length us, event | category | flops | bytes accessed | tf_op | source)
XLA Modules:
  0.0 208.9 jit_solution(297745275986873967)
XLA Ops:
  0.6 0.0 copy-start
  0.6 0.9 fusion.3
  1.5 0.1 reduce_window_sum.11
  1.6 0.8 select_reduce_fusion
  2.5 0.7 add_multiply_fusion
  3.2 0.1 iota_add_fusion
  3.2 0.1 add.45
  3.3 2.3 %reshape.85 = bf16[320,1280]{1,0:T(8,128)(2,1)} reshape(bf16[1,80,4,1280]{3,2,1,0:T(4,128)(2,1)} %param.6) | data formatting | bytes 1638400 | tf_op jit(solution)/shard_map/reshape | solution.py:92
  5.6 2.8 %convolution_convert_fusion = bf16[384,1280]{1,0:T(8,128)(2,1)} fusion(bf16[320,1280]{1,0:T(8,128)(2,1)} %reshape.85, s32[320]{0:T(512)S(1)} %add.45), kind=kOutput, calls=%fused_computation.3 | convolution fusion | flops 315187200 | bytes 1803520 | tf_op jit(solution)/shard_map/dot_general | solution.py:91
  8.4 16.7 %all-to-all-start = ((bf16[24,16,1280]{2,1,0:T(8,128)(2,1)}), bf16[24,16,1280]{2,1,0:T(8,128)(2,1)}, u32[]{:S(2)}, u32[]{:S(2)}) async-start(bf16[24,16,1280]{2,1,0:T(8,128)(2,1)} %bitcast.27), calls=%async_computation | async-start | bytes 1966080 | tf_op jit(solution)/shard_map/all_to_all | solution.py:94
  25.1 2.4 %reshape.91 = bf16[384,1280]{1,0:T(8,128)(2,1)} reshape(bf16[1,1,96,4,1280]{4,3,2,1,0:T(4,128)(2,1)} %param.8) | data formatting | bytes 1966080 | tf_op jit(solution)/shard_map/reshape | solution.py:98
  27.5 2.1 %collective-permute-start.1 = (bf16[384,1280]{1,0:T(8,128)(2,1)}, bf16[384,1280]{1,0:T(8,128)(2,1)}, u32[]{:S(2)}, u32[]{:S(2)}) collective-permute-start(bf16[384,1280]{1,0:T(8,128)(2,1)} %reshape.91), channel_id=1, source_target_pairs={{0,1},{1,0},{2,3},{3,2},{4,5},{5,4},{6,7},{7,6},{8,9},{9,8},{10,11... | collective-permute-start | bytes 2949128 | tf_op jit(solution)/shard_map/ppermute | solution.py:99
  29.7 2.5 %reshape.88.xact_ref = bf16[384,1280]{1,0:T(8,128)(2,1)} reshape(bf16[1,1,96,4,1280]{4,3,2,1,0:T(4,128)(2,1)} %param.9) | data formatting | bytes 1966080 | tf_op jit(solution)/shard_map/reshape | solution.py:100
  32.2 29.7 %all-to-all-done = bf16[24,16,1280]{2,1,0:T(8,128)(2,1)} async-done(((bf16[24,16,1280]{2,1,0:T(8,128)(2,1)}), bf16[24,16,1280]{2,1,0:T(8,128)(2,1)}, u32[]{:S(2)}, u32[]{:S(2)}) %all-to-all-start) | async-done | bytes 983072 | tf_op jit(solution)/shard_map/all_to_all | solution.py:94
  61.9 1.2 copy-done.1
  63.1 6.2 %norm_backward.1 = (bf16[384,1280]{1,0:T(8,128)(2,1)S(1)}, bf16[384,640]{1,0:T(8,128)(2,1)S(1)}, bf16[384,640]{1,0:T(8,128)(2,1)S(1)}, f32[8,1280]{1,0:T(8,128)S(1)}) custom-call(s32[1]{0:T(128)} %bitcast.core_ref, bf16[384,1280]{1,0:T(8,128)(2,1)} %bitcast.3.recv_ref, bf16[384,1280]{1,0:T(8,128)(2,1)S(1)} %copy-done.1, f32[1,1280]{1,0:T(1,128)S(1)} %reshape.89.gamma_ref), custom_call_target="tpu_custom_call" | custom-call | flops 6881280 | bytes 3932160 | tf_op jit(solution)/shard_map/norm_backward/pallas_call | solution.py:64
  69.3 0.9 copy-done.2
  70.2 4.5 %collective-permute-start = (bf16[384,640]{1,0:T(8,128)(2,1)S(1)}, bf16[384,640]{1,0:T(8,128)(2,1)S(1)}, u32[]{:S(2)}, u32[]{:S(2)}) collective-permute-start(bf16[384,640]{1,0:T(8,128)(2,1)S(1)} %get-tuple-element.9), channel_id=1, source_target_pairs={{0,1},{1,0},{2,3},{3,2},{4,5},{5,4},{6,7},{7,6},{8,9},{9,8},{10,11... | collective-permute-start | bytes 1474568 | tf_op jit(solution)/shard_map/ppermute | solution.py:105
  74.7 2.2 %fusion.4 = f32[640,1280]{1,0:T(8,128)S(1)} fusion(bf16[384,640]{1,0:T(8,128)(2,1)S(1)} %get-tuple-element.8, bf16[384,1280]{1,0:T(8,128)(2,1)} %reshape.91), kind=kOutput, calls=%fused_computation.17 | convolution fusion | flops 629145600 | bytes 4751360 | tf_op jit(solution)/shard_map/dot_general | solution.py:108
  77.0 3.5 %fusion.1 = bf16[1280,640]{0,1:T(8,128)(2,1)} fusion(f32[640,1280]{1,0:T(8,128)S(1)} %fusion.4, bf16[384,640]{1,0:T(8,128)(2,1)S(1)} %collective-permute-done, bf16[384,1280]{1,0:T(8,128)(2,1)} %collective-permute-done.1), kind=kOutput, calls=%fused_computation.2 | convolution fusion | flops 630784000 | bytes 6389760 | tf_op jit(solution)/shard_map/dot_general | solution.py:108
  80.5 3.5 %copy.14 = bf16[1280,640]{1,0:T(8,128)(2,1)} copy(bf16[1280,640]{0,1:T(8,128)(2,1)} %fusion.1) | data formatting | bytes 3276800 | tf_op jit(solution)/shard_map/convert_element_type | solution.py:110
  84.0 25.9 %all_to_all.37 = bf16[4,320,640]{2,1,0:T(8,128)(2,1)} all-to-all(bf16[4,320,640]{2,1,0:T(8,128)(2,1)} %bitcast.23), channel_id=1, replica_groups=mesh['dp_0'=4,'dp_1'=8,'z'=12,'core'=2] {'dp_0'}, dimensions={0} | all-to-all | bytes 3276800 | tf_op jit(solution)/shard_map/all_to_all | solution.py:26
  109.9 2.5 %reduce_sum.85 = bf16[320,640]{1,0:T(8,128)(2,1)} reduce(bf16[4,320,640]{2,1,0:T(8,128)(2,1)} %all_to_all.37, bf16[]{:T(256)} %constant.19.clone.1), dimensions={0}, to_apply=%region_2.3 | reduce | flops 614400 | bytes 2048002 | tf_op jit(solution)/shard_map/reduce_sum | solution.py:26
  112.5 20.7 %all_to_all.38 = bf16[8,40,640]{2,1,0:T(8,128)(2,1)} all-to-all(bf16[8,40,640]{2,1,0:T(8,128)(2,1)} %bitcast.26), channel_id=1, replica_groups=mesh['dp_0'=4,'dp_1'=8,'z'=12,'core'=2] {'dp_1'}, dimensions={0} | all-to-all | bytes 819200 | tf_op jit(solution)/shard_map/all_to_all | solution.py:26
  133.2 1.1 reduce.4
  134.3 0.6 reshape.94
  134.9 3.5 %all-to-all-start.3 = ((bf16[12,4,640]{2,1,0:T(4,128)(2,1)}), bf16[12,4,640]{2,1,0:T(4,128)(2,1)S(1)}, u32[]{:S(2)}, u32[]{:S(2)}) async-start(bf16[12,4,640]{2,1,0:T(4,128)(2,1)} %reshape.94), calls=%async_computation.3 | async-start | bytes 122880 | tf_op jit(solution)/shard_map/all_to_all | solution.py:26
  138.4 9.8 %all-to-all-done.3 = bf16[12,4,640]{2,1,0:T(4,128)(2,1)S(1)} async-done(((bf16[12,4,640]{2,1,0:T(4,128)(2,1)}), bf16[12,4,640]{2,1,0:T(4,128)(2,1)S(1)}, u32[]{:S(2)}, u32[]{:S(2)}) %all-to-all-start.3) | async-done | bytes 61472 | tf_op jit(solution)/shard_map/all_to_all | solution.py:26
  148.2 0.7 broadcast_in_dim.7
  148.9 7.1 %all-to-all-start.5 = ((f32[24,1,1280]{2,1,0:T(1,128)}), f32[24,1,1280]{2,1,0:T(1,128)S(1)}, u32[]{:S(2)}, u32[]{:S(2)}) async-start(f32[24,1,1280]{2,1,0:T(1,128)} %broadcast_in_dim.7), calls=%async_computation.5 | async-start | bytes 245760 | tf_op jit(solution)/shard_map/all_to_all | solution.py:20
  156.1 11.4 %all-to-all-done.5 = f32[24,1,1280]{2,1,0:T(1,128)S(1)} async-done(((f32[24,1,1280]{2,1,0:T(1,128)}), f32[24,1,1280]{2,1,0:T(1,128)S(1)}, u32[]{:S(2)}, u32[]{:S(2)}) %all-to-all-start.5) | async-done | bytes 122912 | tf_op jit(solution)/shard_map/all_to_all | solution.py:20
  167.5 0.7 broadcast_in_dim.6
  168.2 4.6 %all-to-all-start.4 = ((f32[24,4,640]{2,1,0:T(4,128)}), f32[24,4,640]{2,1,0:T(4,128)S(1)}, u32[]{:S(2)}, u32[]{:S(2)}) async-start(f32[24,4,640]{2,1,0:T(4,128)} %broadcast_in_dim.6), calls=%async_computation.4 | async-start | bytes 491520 | tf_op jit(solution)/shard_map/all_to_all | solution.py:20
  172.8 1.0 reduce_sum.89
  173.8 14.0 %all-to-all-done.4 = f32[24,4,640]{2,1,0:T(4,128)S(1)} async-done(((f32[24,4,640]{2,1,0:T(4,128)}), f32[24,4,640]{2,1,0:T(4,128)S(1)}, u32[]{:S(2)}, u32[]{:S(2)}) %all-to-all-start.4) | async-done | bytes 245792 | tf_op jit(solution)/shard_map/all_to_all | solution.py:20
  187.9 0.7 multiply_reduce_fusion
  188.6 0.6 concatenate.3
  189.2 0.8 broadcast_in_dim.8
  190.0 4.6 %all-to-all-start.6 = ((f32[32,1,1408]{2,1,0:T(1,128)}), f32[32,1,1408]{2,1,0:T(1,128)}, u32[]{:S(2)}, u32[]{:S(2)}) async-start(f32[32,1,1408]{2,1,0:T(1,128)} %broadcast_in_dim.8), calls=%async_computation.6 | async-start | bytes 360448 | tf_op jit(solution)/shard_map/all_to_all | solution.py:20
  194.6 3.6 %convolution_convert_fusion.1 = bf16[384,1280]{1,0:T(8,128)(2,1)} fusion(bf16[384,1280]{1,0:T(8,128)(2,1)} %copy-done.2, bf16[1280,1280]{1,0:T(8,128)(2,1)S(1)} %copy-done), kind=kOutput, calls=%fused_computation.4 | convolution fusion | flops 1258782720 | bytes 5242880 | tf_op jit(solution)/shard_map/dot_general | solution.py:112
  198.2 2.6 %reshape.90 = bf16[1,1,96,4,1280]{4,3,2,1,0:T(4,128)(2,1)} reshape(bf16[384,1280]{1,0:T(8,128)(2,1)} %convolution_convert_fusion.1) | data formatting | bytes 1966080 | tf_op jit(solution)/shard_map/reshape | solution.py:114
  200.8 3.1 %all-to-all-done.6 = f32[32,1,1408]{2,1,0:T(1,128)} async-done(((f32[32,1,1408]{2,1,0:T(1,128)}), f32[32,1,1408]{2,1,0:T(1,128)}, u32[]{:S(2)}, u32[]{:S(2)}) %all-to-all-start.6) | async-done | bytes 180256 | tf_op jit(solution)/shard_map/all_to_all | solution.py:20
  203.9 1.0 reduce_sum.91
  205.0 0.6 multiply_reduce_fusion.1
  205.6 0.5 slice.14
  207.5 0.6 slice_multiply_fusion.1
  208.1 0.1 copy.17
  208.2 0.7 copy.22
  (14 shorter events, 0.1 us)
Async XLA Ops:
  0.6 193.9 %copy-start = (bf16[1280,1280]{1,0:T(8,128)(2,1)S(1)}, bf16[1280,1280]{1,0:T(8,128)(2,1)}, u32[]{:S(2)}) copy-start(bf16[1280,1280]{1,0:T(8,128)(2,1)} %param.11) | copy-start | bytes 9830404
  5.6 24.1 %copy-start.4 = (f32[1280]{0:T(1024)S(1)}, f32[1280]{0:T(1024)}, u32[]{:S(2)}) copy-start(f32[1280]{0:T(1024)} %param.10) | copy-start | bytes 15364
  8.4 53.5 %all-to-all-start = ((bf16[24,16,1280]{2,1,0:T(8,128)(2,1)}), bf16[24,16,1280]{2,1,0:T(8,128)(2,1)}, u32[]{:S(2)}, u32[]{:S(2)}) async-start(bf16[24,16,1280]{2,1,0:T(8,128)(2,1)} %bitcast.27), calls=%async_computation | async-start | bytes 1966080 | tf_op jit(solution)/shard_map/all_to_all | solution.py:94
  27.5 49.5 %collective-permute-start.1 = (bf16[384,1280]{1,0:T(8,128)(2,1)}, bf16[384,1280]{1,0:T(8,128)(2,1)}, u32[]{:S(2)}, u32[]{:S(2)}) collective-permute-start(bf16[384,1280]{1,0:T(8,128)(2,1)} %reshape.91), channel_id=1, source_target_pairs={{0,1},{1,0},{2,3},{3,2},{4,5},{5,4},{6,7},{7,6},{8,9},{9,8},{10,11... | collective-permute-start | bytes 2949128 | tf_op jit(solution)/shard_map/ppermute | solution.py:99
  61.9 1.2 copy-start.1
  69.3 0.9 copy-start.2
  70.2 6.8 %collective-permute-start = (bf16[384,640]{1,0:T(8,128)(2,1)S(1)}, bf16[384,640]{1,0:T(8,128)(2,1)S(1)}, u32[]{:S(2)}, u32[]{:S(2)}) collective-permute-start(bf16[384,640]{1,0:T(8,128)(2,1)S(1)} %get-tuple-element.9), channel_id=1, source_target_pairs={{0,1},{1,0},{2,3},{3,2},{4,5},{5,4},{6,7},{7,6},{8,9},{9,8},{10,11... | collective-permute-start | bytes 1474568 | tf_op jit(solution)/shard_map/ppermute | solution.py:105
  134.9 13.3 %all-to-all-start.3 = ((bf16[12,4,640]{2,1,0:T(4,128)(2,1)}), bf16[12,4,640]{2,1,0:T(4,128)(2,1)S(1)}, u32[]{:S(2)}, u32[]{:S(2)}) async-start(bf16[12,4,640]{2,1,0:T(4,128)(2,1)} %reshape.94), calls=%async_computation.3 | async-start | bytes 122880 | tf_op jit(solution)/shard_map/all_to_all | solution.py:26
  148.9 18.6 %all-to-all-start.5 = ((f32[24,1,1280]{2,1,0:T(1,128)}), f32[24,1,1280]{2,1,0:T(1,128)S(1)}, u32[]{:S(2)}, u32[]{:S(2)}) async-start(f32[24,1,1280]{2,1,0:T(1,128)} %broadcast_in_dim.7), calls=%async_computation.5 | async-start | bytes 245760 | tf_op jit(solution)/shard_map/all_to_all | solution.py:20
  167.5 0.7 copy-start.3
  168.2 19.6 %all-to-all-start.4 = ((f32[24,4,640]{2,1,0:T(4,128)}), f32[24,4,640]{2,1,0:T(4,128)S(1)}, u32[]{:S(2)}, u32[]{:S(2)}) async-start(f32[24,4,640]{2,1,0:T(4,128)} %broadcast_in_dim.6), calls=%async_computation.4 | async-start | bytes 491520 | tf_op jit(solution)/shard_map/all_to_all | solution.py:20
  190.0 13.9 %all-to-all-start.6 = ((f32[32,1,1408]{2,1,0:T(1,128)}), f32[32,1,1408]{2,1,0:T(1,128)}, u32[]{:S(2)}, u32[]{:S(2)}) async-start(f32[32,1,1408]{2,1,0:T(1,128)} %broadcast_in_dim.8), calls=%async_computation.6 | async-start | bytes 360448 | tf_op jit(solution)/shard_map/all_to_all | solution.py:20

commit v2 on v1

v2 whole, which is shorter than its diff:
```python
import functools

import jax
import jax.numpy as jnp
from jax import lax
from jax.experimental import pallas as pl
from jax.experimental.pallas import tpu as pltpu
from jax.sharding import Mesh
from jax.sharding import PartitionSpec as P

DP = ("dp_0", "dp_1")
SEQ = ("z", "core")
LANES = 128

epsilon = 1e-06
f32 = jnp.float32
bf16 = jnp.bfloat16
VMEM = pl.BlockSpec(memory_space=pltpu.VMEM)
SMEM = pl.BlockSpec(memory_space=pltpu.SMEM)


def call(kernel, name, outs, ins, flops=0, limit=24):
    specs = [SMEM if a.shape == (1,) else VMEM for a in ins]
    moved = sum(a.size * a.dtype.itemsize for a in (*ins, *outs))
    return pl.pallas_call(
        kernel,
        name=name,
        out_shape=outs,
        in_specs=specs,
        out_specs=tuple(VMEM for _ in outs),
        compiler_params=pltpu.CompilerParams(vmem_limit_bytes=limit * 1024 * 1024),
        cost_estimate=pl.CostEstimate(flops=max(flops, 1000000), bytes_accessed=moved, transcendentals=0),
    )(*ins)


def exchange(blocks, axes):
    return lax.all_to_all(blocks, axes, 0, 0, tiled=True)


def iota(shape, dim):
    return lax.broadcasted_iota(jnp.int32, shape, dim)


def gather_kernel(buckets, capacity, patches, owner_ref, rows_ref, out_ref):
    count = owner_ref.shape[1]
    owner = owner_ref[...]
    picked = (iota((buckets, count), 0) == owner).astype(f32)
    earlier = (iota((count, count), 0) < iota((count, count), 1)).astype(f32)
    before = jnp.dot(picked.astype(bf16), earlier.astype(bf16), preferred_element_type=f32)
    ranking = jnp.sum(before * picked, axis=0, keepdims=True)
    target = owner.astype(f32) * capacity + ranking
    spread = (iota((count, count * patches), 0) == iota((count, count * patches), 1) // patches).astype(bf16)
    wide = jnp.dot(jnp.broadcast_to(target, (8, count)).astype(bf16), spread, preferred_element_type=f32)[:1]
    place = wide.astype(jnp.int32) * patches + iota((1, count * patches), 1) % patches
    total = out_ref.shape[0]
    placing = (iota((total, count * patches), 0) == place).astype(bf16)
    out_ref[...] = jnp.dot(placing, rows_ref[...], preferred_element_type=f32).astype(bf16)


def norm_kernel(step, core_ref, recv_ref, xact_ref, gamma_ref, grad_ref, keep_ref, send_ref, gain_ref, sum_ref):
    rows, features = recv_ref.shape
    half = features // 2
    mine = pl.multiple_of(core_ref[0] * half, half)
    other = pl.multiple_of((1 - core_ref[0]) * half, half)
    sum_ref[...] = jnp.zeros_like(sum_ref)
    gamma = gamma_ref[...]

    def body(i, carry):
        at = pl.ds(pl.multiple_of(i * step, step), step)
        values = xact_ref[at, :].astype(f32)
        gradient = recv_ref[at, :].astype(f32)
        inverse = lax.rsqrt(jnp.mean(values * values, axis=1, keepdims=True) + epsilon)
        normed = values * inverse
        sum_ref[...] += (gradient * normed).reshape(step // 8, 8, features).sum(0)
        scaled = gamma * gradient
        centre = jnp.mean(scaled * normed, axis=1, keepdims=True)
        grad_ref[at, :] = (inverse * (scaled - normed * centre)).astype(bf16)
        keep_ref[at, :] = grad_ref[at, pl.ds(mine, half)]
        send_ref[at, :] = grad_ref[at, pl.ds(other, half)]
        return carry

    lax.fori_loop(0, rows // step, body, 0)
    gain_ref[...] = jnp.sum(sum_ref[...], axis=0, keepdims=True)


def weight_kernel(left_ref, left_pair_ref, right_ref, right_pair_ref, gain_ref, out_ref):
    blocks, height, _ = out_ref.shape
    rows = height - 8
    gain = gain_ref[...]
    chunks = gain.shape[1] // LANES
    for b in range(blocks):
        at = slice(b * rows, (b + 1) * rows)
        out_ref[b, :rows, :] = (
            jnp.dot(left_ref[at, :], right_ref[...], preferred_element_type=f32)
            + jnp.dot(left_pair_ref[at, :], right_pair_ref[...], preferred_element_type=f32)
        ).astype(bf16)
        out_ref[b, rows:, :] = jnp.zeros((8, out_ref.shape[2]), bf16)
        lines = [
            gain[:, n * LANES:(n + 1) * LANES] if n < chunks else jnp.zeros((1, LANES), f32)
            for n in range(b * 8, b * 8 + 8)
        ]
        if b * 8 < chunks:
            out_ref[b, rows:, :LANES] = jnp.concatenate(lines, axis=0).astype(bf16)


def first_sum_kernel(in_ref, out_ref):
    blocks, height, width = out_ref.shape
    rows = height - 8
    lines = in_ref[:, blocks * rows:, :].astype(f32).sum(0)
    for b in range(blocks):
        out_ref[b, :rows, :] = in_ref[:, b * rows:(b + 1) * rows, :].astype(f32).sum(0).astype(bf16)
        own = jnp.where(iota((8, width), 0) == 0, lines[b:b + 1, :], 0.0)
        out_ref[b, rows:, :] = own.astype(bf16)


def second_sum_kernel(in_ref, out_ref):
    total = in_ref[...].astype(f32).sum(0)
    pieces, height, _ = out_ref.shape
    for b in range(pieces):
        out_ref[b] = total[b * height:(b + 1) * height, :].astype(bf16)


def third_sum_kernel(in_ref, out_ref):
    total = in_ref[...].astype(f32).sum(0)
    for b in range(out_ref.shape[0]):
        out_ref[b] = total


def joined_kernel(in_ref, weight_ref, note_ref):
    pieces, height, half = in_ref.shape
    rows = weight_ref.shape[0]
    squares = jnp.zeros((height, half), f32)
    for p in range(pieces):
        at = (p // 2) * height
        if at < rows:
            block = in_ref[p]
            squares += block * block
            weight_ref[at:at + height, (p % 2) * half:(p % 2 + 1) * half] = block
    p = 2 * (rows // height)
    gain = in_ref[p, :1, :LANES] + in_ref[p + 1, :1, :LANES]
    line = jnp.concatenate([gain, jnp.full((1, LANES), jnp.sum(squares), f32)], axis=1)
    for d in range(note_ref.shape[0]):
        note_ref[d] = line


def scale_kernel(features, note_ref, weight_ref, weight_out_ref, gain_out_ref):
    chunks = features // LANES
    notes = note_ref[...]
    squares = jnp.sum(jnp.max(notes[:, :, LANES:], axis=2))
    gain = notes[:chunks, :, :LANES]
    total = squares + jnp.sum(gain * gain)
    factor = f32(features) * lax.rsqrt(jnp.full((1, LANES), total + epsilon, f32))
    for n in range(chunks):
        gain_out_ref[:, n * LANES:(n + 1) * LANES] = gain[n] * factor
        at = slice(n * LANES, (n + 1) * LANES)
        weight_out_ref[:, at] = weight_ref[:, at] * factor


def on_device(grad_rows, row_owner, acts, xact, gamma, w_out):
    seq_count = lax.axis_size(SEQ)
    x_count, y_count, z_count = (lax.axis_size(a) for a in ("dp_0", "dp_1", "z"))
    tokens = row_owner.shape[1]
    slot_count, patches, features = acts.shape[2:]
    capacity = slot_count // seq_count
    rows = slot_count * patches
    half = features // 2
    core = jnp.reshape(lax.axis_index("core"), (1,)).astype(jnp.int32)
    swap = [(0, 1), (1, 0)]

    def shaped(dtype, *shape):
        return jax.ShapeDtypeStruct(shape, dtype)

    (outgoing,) = call(
        functools.partial(gather_kernel, seq_count, capacity, patches),
        "gather_rows",
        (shaped(bf16, rows, features),),
        (row_owner.reshape(1, tokens), grad_rows.reshape(tokens * patches, features)),
    )
    received = exchange(outgoing.reshape(seq_count, capacity * patches, features), SEQ)

    act_rows = acts.reshape(rows, features)
    act_pair = lax.ppermute(act_rows, "core", swap)
    left, left_pair, xact_rows = lax.optimization_barrier(
        (act_rows.T, act_pair.T, xact.reshape(rows, features))
    )

    grad, grad_keep, grad_send, gain_part, _ = call(
        functools.partial(norm_kernel, 16),
        "norm_backward",
        (
            shaped(bf16, rows, features),
            shaped(bf16, rows, half),
            shaped(bf16, rows, half),
            shaped(f32, 1, features),
            shaped(f32, 8, features),
        ),
        (core, received.reshape(rows, features), xact_rows, gamma.reshape(1, features)),
    )
    grad_pair = lax.ppermute(grad_send, "core", swap)

    x_rows = features // x_count
    y_rows = x_rows // y_count
    z_rows = (y_rows + 8) // z_count
    (weight_pair,) = call(
        weight_kernel,
        "weight_pair",
        (shaped(bf16, x_count, x_rows + 8, half),),
        (left, left_pair, grad_keep, grad_pair, gain_part),
        flops=4 * features * half * rows,
    )
    (weight_x,) = call(
        first_sum_kernel,
        "sum_first",
        (shaped(bf16, y_count, y_rows + 8, half),),
        (exchange(weight_pair, "dp_0"),),
    )
    (weight_y,) = call(
        second_sum_kernel,
        "sum_second",
        (shaped(bf16, z_count, z_rows, half),),
        (exchange(weight_x, "dp_1"),),
    )
    (pieces,) = call(
        third_sum_kernel,
        "sum_third",
        (shaped(f32, seq_count, z_rows, half),),
        (exchange(weight_y, "z"),),
    )
    weight_sum, note = call(
        joined_kernel,
        "joined",
        (shaped(f32, y_rows, features), shaped(f32, x_count * y_count, 1, 2 * LANES)),
        (exchange(pieces, SEQ),),
    )
    attn_grad = lax.dot_general(
        grad, w_out, (((1,), (1,)), ((), ())), preferred_element_type=f32
    ).astype(bf16).reshape(acts.shape)
    weight_grad, gain_grad = call(
        functools.partial(scale_kernel, features),
        "scaled",
        (shaped(f32, y_rows, features), shaped(f32, 1, features)),
        (exchange(note, DP), weight_sum),
    )
    return (attn_grad, weight_grad, gain_grad.reshape(features))


def solution(mesh):
    finer = Mesh(mesh.devices.reshape(4, 8, mesh.shape["seq"] // 2, 2), (*DP, *SEQ))
    placed = (
        P(DP, SEQ, None, None),
        P(DP, SEQ, None),
        P(DP, SEQ, None, None, None),
        P(DP, SEQ, None, None, None),
        P(),
        P(),
    )
    return jax.shard_map(
        on_device,
        mesh=finer,
        in_specs=placed,
        out_specs=(P(DP, SEQ, None, None, None), P(DP, None), P()),
        check_vma=False,
    )
```

time: 211 us -> 178 us (0.84)
  waiting for transfers between devices: 68 us -> 31.4 us
  blocking collectives: 46.6 us -> 81.6 us
  starting transfers between devices: 43.2 us -> 27.4 us
  other arithmetic: 10.2 us -> 0.62 us
  matrix products: 12.1 us -> 3.63 us
  Pallas kernels: 6.2 us -> 13 us
    all_to_all x5 -> x2, waiting for transfers between devices: 68 us -> 29.8 us  [exchange(): return lax.all_to_all(blocks, axes, 0, 0, tiled=True)]
    all_to_all x2 -> x4, blocking collectives: 46.6 us -> 81.6 us  [exchange(): return lax.all_to_all(blocks, axes, 0, 0, tiled=True)]
    all_to_all x5 -> x2, starting transfers between devices: 36.5 us -> 20.7 us  [exchange(): return lax.all_to_all(blocks, axes, 0, 0, tiled=True)]
    dot_general x3 -> x0, matrix products: 8.51 us -> none  [the longest x2 5.75 us: outer(): lax.dot_general(left, right, (((0,), (0,)), ((), ())), preferred_element_...]
    reduce_sum x9 -> x0, other arithmetic: 7.83 us -> none  [the longest x3 3.64 us: summed_blocks(): lax.all_to_all(blocks, axis, 0, 0, tiled=True).astype(jnp.float32).sum(0)]
    pallas_call x1 -> x8, Pallas kernels: 6.2 us -> 13 us  [call(): pl.pallas_call(kernel, name=name, out_shape=outs, in_specs=specs, out_spe...]
    convert_element_type x1 -> x0, local copies, waits for them, and re-layouts: 3.51 us -> none  [on_device(): (outer(act_rows, grad_keep) + outer(act_pair, grad_pair)).astype(jnp.bflo...]
    unnamed x11 -> x16, local copies, waits for them, and re-layouts: 2.85 us -> 6.1 us
  transfers between devices with their start and end apart: 7 -> 4, of which waited for: 5 -> 4; matrix products, arithmetic and copies ran while one was open for 7% -> 8% of each run, Pallas kernels for 3% -> 0%
where the time goes in v2:
time: 178 us; the launch traced here: 177 us
  blocking collectives  81.6 us (46%)
  waiting for transfers between devices  31.4 us (18%)
  starting transfers between devices  27.4 us (15%)
  local copies, waits for them, and re-layouts  18.3 us (10%)
  Pallas kernels  13 us (7%)
  matrix products  3.63 us (2%)
    all_to_all x4, blocking collectives, exchange(): return lax.all_to_all(blocks, axes, 0, 0, tiled=True)  81.6 us
    all_to_all x2, waiting for transfers between devices, exchange(): return lax.all_to_all(blocks, axes, 0, 0, tiled=True)  29.8 us
    all_to_all x2, starting transfers between devices, exchange(): return lax.all_to_all(blocks, axes, 0, 0, tiled=True)  20.7 us
    pallas_call x8, Pallas kernels, call(): pl.pallas_call(kernel, name=name, out_shape=outs, in_specs=specs, out_spe...  13 us
    unnamed x16, local copies, waits for them, and re-layouts  6.1 us
    reshape x2, local copies, waits for them, and re-layouts, on_device(): act_rows = acts.reshape(rows, features)  4.71 us
    ppermute x1, starting transfers between devices, on_device(): grad_pair = lax.ppermute(grad_send, 'core', swap)  4.54 us
    dot_general x1, matrix products, on_device(): lax.dot_general(grad, w_out, (((1,), (1,)), ((), ())), preferred_element_...  3.63 us
  transfers between devices with their start and end apart: 4, of which 4 were waited for; matrix products, arithmetic and copies ran while one was open for 8% of the time, Pallas kernels for 0%

profile of v2, /device:TPU:1, one launch (start us, length us, event | category | flops | bytes accessed | tf_op | source)
XLA Modules:
  0.0 176.6 jit_solution(10477946925923986295)
XLA Ops:
  0.6 0.0 copy-start
  0.6 2.4 %reshape.38.rows_ref = bf16[320,1280]{1,0:T(8,128)(2,1)} reshape(bf16[1,80,4,1280]{3,2,1,0:T(4,128)(2,1)} %param.6) | data formatting | bytes 1638400 | tf_op jit(solution)/shard_map/reshape | solution.py:177
  3.1 0.0 copy-start.3
  3.1 1.1 copy-done.3
  4.2 0.0 copy-start.5
  4.2 0.7 copy-done.5
  4.9 0.9 gather_rows.1
  5.8 0.0 copy-start.1
  5.8 0.9 copy-done.1
  6.8 0.0 copy-start.7
  6.8 16.8 %all-to-all-start = ((bf16[24,16,1280]{2,1,0:T(8,128)(2,1)}), bf16[24,16,1280]{2,1,0:T(8,128)(2,1)}, u32[]{:S(2)}, u32[]{:S(2)}) async-start(bf16[24,16,1280]{2,1,0:T(8,128)(2,1)} %bitcast.8), calls=%async_computation | async-start | bytes 1966080 | tf_op jit(solution)/shard_map/all_to_all | solution.py:37
  23.6 2.5 %reshape.41 = bf16[384,1280]{1,0:T(8,128)(2,1)} reshape(bf16[1,1,96,4,1280]{4,3,2,1,0:T(4,128)(2,1)} %param.8) | data formatting | bytes 1966080 | tf_op jit(solution)/shard_map/reshape | solution.py:181
  26.1 2.3 %copy.10 = bf16[384,1280]{0,1:T(8,128)(2,1)} copy(bf16[384,1280]{1,0:T(8,128)(2,1)} %reshape.41) | data formatting | bytes 1966080 | tf_op jit(solution)/shard_map/reshape | solution.py:181
  28.3 2.1 %collective-permute-start = (bf16[384,1280]{0,1:T(8,128)(2,1)}, bf16[384,1280]{0,1:T(8,128)(2,1)}, u32[]{:S(2)}, u32[]{:S(2)}) collective-permute-start(bf16[384,1280]{0,1:T(8,128)(2,1)} %copy.10), channel_id=1, source_target_pairs={{0,1},{1,0},{2,3},{3,2},{4,5},{5,4},{6,7},{7,6},{8,9},{9,8},{10,11... | collective-permute-start | bytes 2949128 | tf_op jit(solution)/shard_map/ppermute | solution.py:182
  30.5 0.0 copy-done.7
  30.5 2.5 %reshape.42.xact_ref = bf16[384,1280]{1,0:T(8,128)(2,1)} reshape(bf16[1,1,96,4,1280]{4,3,2,1,0:T(4,128)(2,1)} %param.9) | data formatting | bytes 1966080 | tf_op jit(solution)/shard_map/reshape | solution.py:184
  33.0 0.1 collective-permute-done
  33.1 27.2 %all-to-all-done = bf16[24,16,1280]{2,1,0:T(8,128)(2,1)} async-done(((bf16[24,16,1280]{2,1,0:T(8,128)(2,1)}), bf16[24,16,1280]{2,1,0:T(8,128)(2,1)}, u32[]{:S(2)}, u32[]{:S(2)}) %all-to-all-start) | async-done | bytes 983072 | tf_op jit(solution)/shard_map/all_to_all | solution.py:37
  60.3 0.0 copy-start.2
  60.3 1.2 copy-done.2
  61.5 6.7 %norm_backward.1 = (bf16[384,1280]{1,0:T(8,128)(2,1)S(1)}, bf16[384,640]{1,0:T(8,128)(2,1)S(1)}, bf16[384,640]{1,0:T(8,128)(2,1)S(1)}, f32[1,1280]{1,0:T(1,128)S(1)}, f32[8,1280]{1,0:T(8,128)}) custom-call(s32[1]{0:T(128)} %bitcast.core_ref, bf16[384,1280]{1,0:T(8,128)(2,1)} %bitcast.3.recv_ref, bf16[384,1280]{1,0:T(8,128)(2,1)S(1)} %copy-done.2, ...), custom_call_target="tpu_custom_call" | custom-call | flops 1000000 | bytes 3983364 | tf_op jit(solution)/shard_map/norm_backward/pallas_call | solution.py:25
  68.3 0.0 copy-start.6
  68.3 0.9 copy-done.6
  69.2 4.5 %collective-permute-start.1 = (bf16[384,640]{1,0:T(8,128)(2,1)S(1)}, bf16[384,640]{1,0:T(8,128)(2,1)S(1)}, u32[]{:S(2)}, u32[]{:S(2)}) collective-permute-start(bf16[384,640]{1,0:T(8,128)(2,1)S(1)} %get-tuple-element.19), channel_id=1, source_target_pairs={{0,1},{1,0},{2,3},{3,2},{4,5},{5,4},{6,7},{7,6},{8,9},{9,8},{10,11... | collective-permute-start | bytes 1474568 | tf_op jit(solution)/shard_map/ppermute | solution.py:199
  73.8 1.5 collective-permute-done.1.right_pair_ref
  75.2 0.0 copy-start.4
  75.3 1.2 copy-done.4
  76.5 3.3 %weight_pair.1 = bf16[4,328,640]{2,1,0:T(8,128)(2,1)S(1)} custom-call(bf16[1280,384]{1,0:T(8,128)(2,1)S(1)} %bitcast.9, bf16[1280,384]{1,0:T(8,128)(2,1)} %bitcast.5.left_pair_ref, bf16[384,640]{1,0:T(8,128)(2,1)S(1)} %get-tuple-element.18.right_ref, bf16[384,640]{1,0:T(8,128)(2,1)S(1)} %collective-permute-done.1.right_pair_ref, ...), custom_call_target="tpu_custom_call" | custom-call | flops 1258291200 | bytes 4633600 | tf_op jit(solution)/shard_map/weight_pair/pallas_call | solution.py:25
  79.7 24.8 %all_to_all.30.in_ref = bf16[4,328,640]{2,1,0:T(8,128)(2,1)S(1)} all-to-all(bf16[4,328,640]{2,1,0:T(8,128)(2,1)S(1)} %weight_pair.1), channel_id=1, replica_groups=mesh['dp_0'=4,'dp_1'=8,'z'=12,'core'=2] {'dp_0'}, dimensions={0} | all-to-all | bytes 3358720 | tf_op jit(solution)/shard_map/all_to_all | solution.py:37
  104.5 0.2 sum_first.1
  104.8 20.6 %all_to_all.31.in_ref = bf16[8,48,640]{2,1,0:T(8,128)(2,1)S(1)} all-to-all(bf16[8,48,640]{2,1,0:T(8,128)(2,1)S(1)} %sum_first.1), channel_id=1, replica_groups=mesh['dp_0'=4,'dp_1'=8,'z'=12,'core'=2] {'dp_1'}, dimensions={0} | all-to-all | bytes 983040 | tf_op jit(solution)/shard_map/all_to_all | solution.py:37
  125.4 0.1 sum_second.1
  125.4 13.8 %all_to_all.32.in_ref = bf16[12,4,640]{2,1,0:T(4,128)(2,1)S(1)} all-to-all(bf16[12,4,640]{2,1,0:T(4,128)(2,1)S(1)} %sum_second.1), channel_id=1, replica_groups=mesh['dp_0'=4,'dp_1'=8,'z'=12,'core'=2] {'z'}, dimensions={0} | all-to-all | bytes 122880 | tf_op jit(solution)/shard_map/all_to_all | solution.py:37
  139.2 22.4 %all_to_all.33.in_ref = f32[24,4,640]{2,1,0:T(4,128)S(1)} all-to-all(f32[24,4,640]{2,1,0:T(4,128)S(1)} %sum_third.1), channel_id=1, replica_groups=mesh['dp_0'=4,'dp_1'=8,'z'=12,'core'=2] {'z','core'}, dimensions={0} | all-to-all | bytes 491520 | tf_op jit(solution)/shard_map/all_to_all | solution.py:37
  161.6 0.8 joined.1
  162.4 3.9 %all-to-all-start.5 = ((f32[32,1,256]{2,1,0:T(1,128)}), f32[32,1,256]{2,1,0:T(1,128)S(1)}, u32[]{:S(2)}, u32[]{:S(2)}) async-start(f32[32,1,256]{2,1,0:T(1,128)} %get-tuple-element.21), calls=%async_computation.5 | async-start | bytes 65536 | tf_op jit(solution)/shard_map/all_to_all | solution.py:37
  166.3 0.0 copy-done
  166.3 3.6 %convolution_convert_fusion = bf16[384,1280]{1,0:T(8,128)(2,1)} fusion(bf16[384,1280]{1,0:T(8,128)(2,1)} %copy-done.6, bf16[1280,1280]{1,0:T(8,128)(2,1)S(1)} %copy-done), kind=kOutput, calls=%fused_computation | convolution fusion | flops 1258782720 | bytes 5242880 | tf_op jit(solution)/shard_map/dot_general | solution.py:235
  169.9 2.6 %reshape.44 = bf16[1,1,96,4,1280]{4,3,2,1,0:T(4,128)(2,1)} reshape(bf16[384,1280]{1,0:T(8,128)(2,1)} %convolution_convert_fusion) | data formatting | bytes 1966080 | tf_op jit(solution)/shard_map/reshape | solution.py:237
  172.5 2.6 %all-to-all-done.5.note_ref = f32[32,1,256]{2,1,0:T(1,128)S(1)} async-done(((f32[32,1,256]{2,1,0:T(1,128)}), f32[32,1,256]{2,1,0:T(1,128)S(1)}, u32[]{:S(2)}, u32[]{:S(2)}) %all-to-all-start.5) | async-done | bytes 32800 | tf_op jit(solution)/shard_map/all_to_all | solution.py:37
  175.1 0.9 scaled.1
  176.0 0.6 reduce
  (2 shorter events, 0.0 us)
Async XLA Ops:
  0.6 165.6 %copy-start = (bf16[1280,1280]{1,0:T(8,128)(2,1)S(1)}, bf16[1280,1280]{1,0:T(8,128)(2,1)}, u32[]{:S(2)}) copy-start(bf16[1280,1280]{1,0:T(8,128)(2,1)} %param.11) | copy-start | bytes 9830404
  3.1 1.1 copy-start.3
  4.2 0.7 copy-start.5
  5.8 0.9 copy-start.1
  6.8 23.7 %copy-start.7 = (f32[1280]{0:T(1024)S(1)}, f32[1280]{0:T(1024)}, u32[]{:S(2)}) copy-start(f32[1280]{0:T(1024)} %param.10) | copy-start | bytes 15364
  6.8 53.6 %all-to-all-start = ((bf16[24,16,1280]{2,1,0:T(8,128)(2,1)}), bf16[24,16,1280]{2,1,0:T(8,128)(2,1)}, u32[]{:S(2)}, u32[]{:S(2)}) async-start(bf16[24,16,1280]{2,1,0:T(8,128)(2,1)} %bitcast.8), calls=%async_computation | async-start | bytes 1966080 | tf_op jit(solution)/shard_map/all_to_all | solution.py:37
  28.3 4.8 %collective-permute-start = (bf16[384,1280]{0,1:T(8,128)(2,1)}, bf16[384,1280]{0,1:T(8,128)(2,1)}, u32[]{:S(2)}, u32[]{:S(2)}) collective-permute-start(bf16[384,1280]{0,1:T(8,128)(2,1)} %copy.10), channel_id=1, source_target_pairs={{0,1},{1,0},{2,3},{3,2},{4,5},{5,4},{6,7},{7,6},{8,9},{9,8},{10,11... | collective-permute-start | bytes 2949128 | tf_op jit(solution)/shard_map/ppermute | solution.py:182
  60.3 1.2 copy-start.2
  68.3 0.9 copy-start.6
  69.2 6.0 %collective-permute-start.1 = (bf16[384,640]{1,0:T(8,128)(2,1)S(1)}, bf16[384,640]{1,0:T(8,128)(2,1)S(1)}, u32[]{:S(2)}, u32[]{:S(2)}) collective-permute-start(bf16[384,640]{1,0:T(8,128)(2,1)S(1)} %get-tuple-element.19), channel_id=1, source_target_pairs={{0,1},{1,0},{2,3},{3,2},{4,5},{5,4},{6,7},{7,6},{8,9},{9,8},{10,11... | collective-permute-start | bytes 1474568 | tf_op jit(solution)/shard_map/ppermute | solution.py:199
  75.2 1.2 copy-start.4
  162.4 12.6 %all-to-all-start.5 = ((f32[32,1,256]{2,1,0:T(1,128)}), f32[32,1,256]{2,1,0:T(1,128)S(1)}, u32[]{:S(2)}, u32[]{:S(2)}) async-start(f32[32,1,256]{2,1,0:T(1,128)} %get-tuple-element.21), calls=%async_computation.5 | async-start | bytes 65536 | tf_op jit(solution)/shard_map/all_to_all | solution.py:37

commit v3 on v2

--- a/solution.py
+++ b/solution.py
@@ -17,17 +17,19 @@
 bf16 = jnp.bfloat16
 VMEM = pl.BlockSpec(memory_space=pltpu.VMEM)
 SMEM = pl.BlockSpec(memory_space=pltpu.SMEM)
-
-
-def call(kernel, name, outs, ins, flops=0, limit=24):
-    specs = [SMEM if a.shape == (1,) else VMEM for a in ins]
+FAR = pl.BlockSpec(memory_space=pltpu.HBM)
+
+
+def call(kernel, name, outs, ins, flops=0, limit=24, far_in=(), far_out=(), scratch=()):
+    specs = [SMEM if a.shape == (1,) else (FAR if n in far_in else VMEM) for n, a in enumerate(ins)]
     moved = sum(a.size * a.dtype.itemsize for a in (*ins, *outs))
     return pl.pallas_call(
         kernel,
         name=name,
         out_shape=outs,
         in_specs=specs,
-        out_specs=tuple(VMEM for _ in outs),
+        out_specs=tuple(FAR if n in far_out else VMEM for n in range(len(outs))),
+        scratch_shapes=scratch,
         compiler_params=pltpu.CompilerParams(vmem_limit_bytes=limit * 1024 * 1024),
         cost_estimate=pl.CostEstimate(flops=max(flops, 1000000), bytes_accessed=moved, transcendentals=0),
     )(*ins)
@@ -41,8 +43,9 @@
     return lax.broadcasted_iota(jnp.int32, shape, dim)
 
 
-def gather_kernel(buckets, capacity, patches, owner_ref, rows_ref, out_ref):
+def gather_kernel(buckets, capacity, patches, chunks, owner_ref, rows_ref, out_ref, hold_ref, sems):
     count = owner_ref.shape[1]
+    features = rows_ref.shape[2]
     owner = owner_ref[...]
     picked = (iota((buckets, count), 0) == owner).astype(f32)
     earlier = (iota((count, count), 0) < iota((count, count), 1)).astype(f32)
@@ -52,35 +55,81 @@
     spread = (iota((count, count * patches), 0) == iota((count, count * patches), 1) // patches).astype(bf16)
     wide = jnp.dot(jnp.broadcast_to(target, (8, count)).astype(bf16), spread, preferred_element_type=f32)[:1]
     place = wide.astype(jnp.int32) * patches + iota((1, count * patches), 1) % patches
-    total = out_ref.shape[0]
-    placing = (iota((total, count * patches), 0) == place).astype(bf16)
-    out_ref[...] = jnp.dot(placing, rows_ref[...], preferred_element_type=f32).astype(bf16)
-
-
-def norm_kernel(step, core_ref, recv_ref, xact_ref, gamma_ref, grad_ref, keep_ref, send_ref, gain_ref, sum_ref):
+    lines = rows_ref[...].reshape(count * patches, features)
+    step = out_ref.shape[0] // chunks
+    copies = []
+    for n in range(chunks):
+        placing = (iota((step, count * patches), 0) + n * step == place).astype(bf16)
+        at = pl.ds(n * step, step)
+        hold_ref[at, :] = jnp.dot(placing, lines, preferred_element_type=f32).astype(bf16)
+        copies.append(pltpu.make_async_copy(hold_ref.at[at, :], out_ref.at[at, :], sems.at[n]))
+        copies[-1].start()
+    for copy in copies:
+        copy.wait()
+
+
+def prepare_kernel(step, xact_ref, acts_ref, pair_ref, lines_ref, inverse_ref, left_ref, left_pair_ref):
+    slots, patches, features = xact_ref.shape
+    height = step * patches
+    for n in range(slots // step):
+        at = slice(n * height, (n + 1) * height)
+        lines = xact_ref[n * step:(n + 1) * step].reshape(height, features)
+        lines_ref[at, :] = lines
+        values = lines.astype(f32)
+        inverse_ref[at, :] = lax.rsqrt(jnp.mean(values * values, axis=1, keepdims=True) + epsilon)
+    for source, target in ((acts_ref, left_ref), (pair_ref, left_pair_ref)):
+        width = LANES
+        for n in range(slots * patches // width):
+            block = source[n * width // patches:(n + 1) * width // patches].reshape(width, features)
+            target[:, n * width:(n + 1) * width] = block.T
+
+
+def norm_kernel(
+    chunks, step, core_ref, recv_ref, lines_ref, inverse_ref, gamma_ref,
+    grad_ref, keep_ref, send_ref, gain_ref, hold_ref, values_ref, made_ref, in_sems, value_sems, out_sems,
+):
     rows, features = recv_ref.shape
     half = features // 2
-    mine = pl.multiple_of(core_ref[0] * half, half)
-    other = pl.multiple_of((1 - core_ref[0]) * half, half)
-    sum_ref[...] = jnp.zeros_like(sum_ref)
+    height = rows // chunks
+    first = core_ref[0] == 0
     gamma = gamma_ref[...]
-
-    def body(i, carry):
+    incoming = []
+    for n in range(chunks):
+        at = pl.ds(n * height, height)
+        incoming.append((
+            pltpu.make_async_copy(recv_ref.at[at, :], hold_ref.at[at, :], in_sems.at[n]),
+            pltpu.make_async_copy(lines_ref.at[at, :], values_ref.at[at, :], value_sems.at[n]),
+        ))
+        for copy in incoming[-1]:
+            copy.start()
+
+    def body(i, gain):
         at = pl.ds(pl.multiple_of(i * step, step), step)
-        values = xact_ref[at, :].astype(f32)
-        gradient = recv_ref[at, :].astype(f32)
-        inverse = lax.rsqrt(jnp.mean(values * values, axis=1, keepdims=True) + epsilon)
-        normed = values * inverse
-        sum_ref[...] += (gradient * normed).reshape(step // 8, 8, features).sum(0)
-        scaled = gamma * gradient
-        centre = jnp.mean(scaled * normed, axis=1, keepdims=True)
-        grad_ref[at, :] = (inverse * (scaled - normed * centre)).astype(bf16)
-        keep_ref[at, :] = grad_ref[at, pl.ds(mine, half)]
-        send_ref[at, :] = grad_ref[at, pl.ds(other, half)]
-        return carry
-
-    lax.fori_loop(0, rows // step, body, 0)
-    gain_ref[...] = jnp.sum(sum_ref[...], axis=0, keepdims=True)
+        inverse = inverse_ref[at, :]
+        normed = values_ref[at, :].astype(f32) * inverse
+        gradient = hold_ref[at, :].astype(f32)
+        both = gradient * normed
+        gain = gain + both.reshape(step // 8, 8, features).sum(0)
+        centre = jnp.mean(gamma * both, axis=1, keepdims=True)
+        made = (inverse * (gamma * gradient - normed * centre)).astype(bf16)
+        made_ref[at, :] = made
+        low, high = made[:, :half], made[:, half:]
+        keep_ref[at, :] = jnp.where(first, low, high)
+        send_ref[at, :] = jnp.where(first, high, low)
+        return gain
+
+    gain = jnp.zeros((8, features), f32)
+    outgoing = []
+    for n in range(chunks):
+        at = pl.ds(n * height, height)
+        for copy in incoming[n]:
+            copy.wait()
+        gain = lax.fori_loop(n * height // step, (n + 1) * height // step, body, gain, unroll=2)
+        outgoing.append(pltpu.make_async_copy(made_ref.at[at, :], grad_ref.at[at, :], out_sems.at[n]))
+        outgoing[-1].start()
+    gain_ref[...] = jnp.sum(gain, axis=0, keepdims=True)
+    for copy in outgoing:
+        copy.wait()
 
 
 def weight_kernel(left_ref, left_pair_ref, right_ref, right_pair_ref, gain_ref, out_ref):
@@ -122,6 +171,7 @@
 
 def third_sum_kernel(in_ref, out_ref):
     total = in_ref[...].astype(f32).sum(0)
+    total = total.astype(bf16)
     for b in range(out_ref.shape[0]):
         out_ref[b] = total
 
@@ -133,11 +183,11 @@
     for p in range(pieces):
         at = (p // 2) * height
         if at < rows:
-            block = in_ref[p]
+            block = in_ref[p].astype(f32)
             squares += block * block
             weight_ref[at:at + height, (p % 2) * half:(p % 2 + 1) * half] = block
     p = 2 * (rows // height)
-    gain = in_ref[p, :1, :LANES] + in_ref[p + 1, :1, :LANES]
+    gain = (in_ref[p].astype(f32) + in_ref[p + 1].astype(f32))[:1, :LANES]
     line = jnp.concatenate([gain, jnp.full((1, LANES), jnp.sum(squares), f32)], axis=1)
     for d in range(note_ref.shape[0]):
         note_ref[d] = line
@@ -170,31 +220,53 @@
     def shaped(dtype, *shape):
         return jax.ShapeDtypeStruct(shape, dtype)
 
+    chunks = 3
     (outgoing,) = call(
-        functools.partial(gather_kernel, seq_count, capacity, patches),
+        functools.partial(gather_kernel, seq_count, capacity, patches, chunks),
         "gather_rows",
         (shaped(bf16, rows, features),),
-        (row_owner.reshape(1, tokens), grad_rows.reshape(tokens * patches, features)),
+        (row_owner.reshape(1, tokens), grad_rows.reshape(tokens, patches, features)),
+        far_out=(0,),
+        limit=60,
+        scratch=[pltpu.VMEM((rows, features), bf16), pltpu.SemaphoreType.DMA((chunks,))],
     )
     received = exchange(outgoing.reshape(seq_count, capacity * patches, features), SEQ)
 
-    act_rows = acts.reshape(rows, features)
-    act_pair = lax.ppermute(act_rows, "core", swap)
-    left, left_pair, xact_rows = lax.optimization_barrier(
-        (act_rows.T, act_pair.T, xact.reshape(rows, features))
-    )
-
-    grad, grad_keep, grad_send, gain_part, _ = call(
-        functools.partial(norm_kernel, 16),
+    act_slots = acts.reshape(slot_count, patches, features)
+    act_pair = lax.ppermute(act_slots, "core", swap)
+    lines, inverse, left, left_pair = call(
+        functools.partial(prepare_kernel, 8),
+        "prepare",
+        (
+            shaped(bf16, rows, features),
+            shaped(f32, rows, 1),
+            shaped(bf16, features, rows),
+            shaped(bf16, features, rows),
+        ),
+        (xact.reshape(slot_count, patches, features), act_slots, act_pair),
+    )
+
+    chunks = 6
+    grad, grad_keep, grad_send, gain_part = call(
+        functools.partial(norm_kernel, chunks, 16),
         "norm_backward",
         (
             shaped(bf16, rows, features),
             shaped(bf16, rows, half),
             shaped(bf16, rows, half),
             shaped(f32, 1, features),
-            shaped(f32, 8, features),
         ),
-        (core, received.reshape(rows, features), xact_rows, gamma.reshape(1, features)),
+        (core, received.reshape(rows, features), lines, inverse, gamma.reshape(1, features)),
+        far_in=(1, 2),
+        far_out=(0,),
+        scratch=[
+            pltpu.VMEM((rows, features), bf16),
+            pltpu.VMEM((rows, features), bf16),
+            pltpu.VMEM((rows, features), bf16),
+            pltpu.SemaphoreType.DMA((chunks,)),
+            pltpu.SemaphoreType.DMA((chunks,)),
+            pltpu.SemaphoreType.DMA((chunks,)),
+        ],
     )
     grad_pair = lax.ppermute(grad_send, "core", swap)
 
@@ -223,7 +295,7 @@
     (pieces,) = call(
         third_sum_kernel,
         "sum_third",
-        (shaped(f32, seq_count, z_rows, half),),
+        (shaped(bf16, seq_count, z_rows, half),),
         (exchange(weight_y, "z"),),
     )
     weight_sum, note = call(

time: 178 us -> 169 us (0.949)
  local copies, waits for them, and re-layouts: 18.3 us -> 12.4 us
  blocking collectives: 81.6 us -> 78 us
    reshape x4 -> x0, local copies, waits for them, and re-layouts: 9.63 us -> none  [the longest x2 4.71 us: on_device(): act_rows = acts.reshape(rows, features)]
    unnamed x16 -> x22, local copies, waits for them, and re-layouts: 6.1 us -> 9.86 us
    all_to_all x4, blocking collectives: 81.6 us -> 78 us  [exchange(): return lax.all_to_all(blocks, axes, 0, 0, tiled=True)]
    all_to_all x2, waiting for transfers between devices: 29.8 us -> 27 us  [exchange(): return lax.all_to_all(blocks, axes, 0, 0, tiled=True)]
    ppermute x1, waiting for transfers between devices: 0.14 us -> 2.61 us  [on_device(): act_pair = lax.ppermute(act_slots, 'core', swap)]
    pallas_call x8 -> x9, Pallas kernels: 13 us -> 14.2 us  [call(): pl.pallas_call(kernel, name=name, out_shape=outs, in_specs=specs, out_spe...]
  transfers between devices with their start and end apart: 4 -> 4, of which waited for: 4 -> 4; matrix products, arithmetic and copies ran while one was open for 8% -> 4% of each run, Pallas kernels for 0% -> 1%
where the time goes in v3:
time: 169 us; the launch traced here: 168 us
  blocking collectives  78 us (46%)
  waiting for transfers between devices  31.1 us (18%)
  starting transfers between devices  27.3 us (16%)
  Pallas kernels  14.2 us (8%)
  local copies, waits for them, and re-layouts  12.4 us (7%)
  matrix products  3.64 us (2%)
    all_to_all x4, blocking collectives, exchange(): return lax.all_to_all(blocks, axes, 0, 0, tiled=True)  78 us
    all_to_all x2, waiting for transfers between devices, exchange(): return lax.all_to_all(blocks, axes, 0, 0, tiled=True)  27 us
    all_to_all x2, starting transfers between devices, exchange(): return lax.all_to_all(blocks, axes, 0, 0, tiled=True)  20.6 us
    pallas_call x9, Pallas kernels, call(): pl.pallas_call(kernel, name=name, out_shape=outs, in_specs=specs, out_spe...  14.2 us
    unnamed x22, local copies, waits for them, and re-layouts  9.86 us
    ppermute x1, starting transfers between devices, on_device(): grad_pair = lax.ppermute(grad_send, 'core', swap)  4.55 us
    dot_general x1, matrix products, on_device(): lax.dot_general(grad, w_out, (((1,), (1,)), ((), ())), preferred_element_...  3.64 us
  transfers between devices with their start and end apart: 4, of which 4 were waited for; matrix products, arithmetic and copies ran while one was open for 4% of the time, Pallas kernels for 1%

profile of v3, /device:TPU:1, one launch (start us, length us, event | category | flops | bytes accessed | tf_op | source)
XLA Modules:
  0.0 168.1 jit_solution(11088755570508535368)
XLA Ops:
  0.6 0.0 copy-start
  0.6 0.0 copy-start.10
  0.7 3.0 %gather_rows.1 = bf16[384,1280]{1,0:T(8,128)(2,1)} custom-call(s32[1,80]{1,0:T(1,128)} %bitcast.14, bf16[80,4,1280]{2,1,0:T(4,128)(2,1)} %bitcast.13), custom_call_target="tpu_custom_call" | custom-call | flops 1000000 | bytes 1802560 | tf_op jit(solution)/shard_map/gather_rows/pallas_call | solution.py:26
  3.6 16.7 %all-to-all-start = ((bf16[24,16,1280]{2,1,0:T(8,128)(2,1)}), bf16[24,16,1280]{2,1,0:T(8,128)(2,1)}, u32[]{:S(2)}, u32[]{:S(2)}) async-start(bf16[24,16,1280]{2,1,0:T(8,128)(2,1)} %bitcast.12), calls=%async_computation | async-start | bytes 1966080 | tf_op jit(solution)/shard_map/all_to_all | solution.py:39
  20.4 2.2 %collective-permute-start = (bf16[96,4,1280]{2,1,0:T(4,128)(2,1)}, bf16[96,4,1280]{2,1,0:T(4,128)(2,1)}, u32[]{:S(2)}, u32[]{:S(2)}) collective-permute-start(bf16[96,4,1280]{2,1,0:T(4,128)(2,1)} %bitcast.10), channel_id=1, source_target_pairs={{0,1},{1,0},{2,3},{3,2},{4,5},{5,4},{6,7},{7,6},{8,9},{9,8},{10,11... | collective-permute-start | bytes 2949128 | tf_op jit(solution)/shard_map/ppermute | solution.py:236
  22.5 0.0 copy-done.10
  22.6 2.6 %collective-permute-done.pair_ref = bf16[96,4,1280]{2,1,0:T(4,128)(2,1)} collective-permute-done((bf16[96,4,1280]{2,1,0:T(4,128)(2,1)}, bf16[96,4,1280]{2,1,0:T(4,128)(2,1)}, u32[]{:S(2)}, u32[]{:S(2)}) %collective-permute-start) | collective-permute-done | bytes 983072 | tf_op jit(solution)/shard_map/ppermute | solution.py:236
  25.2 0.0 copy-start.1
  25.2 1.2 copy-done.1
  26.4 0.0 copy-start.2
  26.4 1.2 copy-done.2
  27.6 2.1 %prepare.1 = (bf16[384,1280]{1,0:T(8,128)(2,1)S(1)}, f32[384,1]{1,0:T(8,128)S(1)}, bf16[1280,384]{1,0:T(8,128)(2,1)S(1)}, bf16[1280,384]{1,0:T(8,128)(2,1)S(1)}) custom-call(bf16[96,4,1280]{2,1,0:T(4,128)(2,1)S(1)} %bitcast.9, bf16[96,4,1280]{2,1,0:T(4,128)(2,1)S(1)} %bitcast.11, bf16[96,4,1280]{2,1,0:T(4,128)(2,1)} %collective-permute-done.pair_ref), custom_call_target="tpu_custom_call" | custom-call | flops 1000000 | bytes 5899776 | tf_op jit(solution)/shard_map/prepare/pallas_call | solution.py:26
  29.6 0.0 copy-start.3
  29.7 0.9 copy-done.3
  30.6 0.0 copy-start.6
  30.6 1.0 copy-done.6
  31.6 0.0 copy-start.8
  31.6 1.0 copy-done.8
  32.6 24.6 %all-to-all-done = bf16[24,16,1280]{2,1,0:T(8,128)(2,1)} async-done(((bf16[24,16,1280]{2,1,0:T(8,128)(2,1)}), bf16[24,16,1280]{2,1,0:T(8,128)(2,1)}, u32[]{:S(2)}, u32[]{:S(2)}) %all-to-all-start) | async-done | bytes 983072 | tf_op jit(solution)/shard_map/all_to_all | solution.py:39
  57.1 0.0 copy-start.4
  57.1 1.2 copy-done.4
  58.3 5.0 %norm_backward.1 = (bf16[384,1280]{1,0:T(8,128)(2,1)S(1)}, bf16[384,640]{1,0:T(8,128)(2,1)S(1)}, bf16[384,640]{1,0:T(8,128)(2,1)S(1)}, f32[1,1280]{1,0:T(1,128)S(1)}) custom-call(s32[1]{0:T(128)} %bitcast.core_ref, bf16[384,1280]{1,0:T(8,128)(2,1)} %bitcast.4.recv_ref, bf16[384,1280]{1,0:T(8,128)(2,1)S(1)} %copy-done.4, ...), custom_call_target="tpu_custom_call" | custom-call | flops 1000000 | bytes 3943940 | tf_op jit(solution)/shard_map/norm_backward/pallas_call | solution.py:26
  63.3 0.0 copy-start.5
  63.4 0.9 copy-done.5
  64.3 4.5 %collective-permute-start.1 = (bf16[384,640]{1,0:T(8,128)(2,1)S(1)}, bf16[384,640]{1,0:T(8,128)(2,1)S(1)}, u32[]{:S(2)}, u32[]{:S(2)}) collective-permute-start(bf16[384,640]{1,0:T(8,128)(2,1)S(1)} %get-tuple-element.21), channel_id=1, source_target_pairs={{0,1},{1,0},{2,3},{3,2},{4,5},{5,4},{6,7},{7,6},{8,9},{9,8},{10,11... | collective-permute-start | bytes 1474568 | tf_op jit(solution)/shard_map/ppermute | solution.py:271
  68.9 1.5 collective-permute-done.1.right_pair_ref
  70.3 0.0 copy-start.7
  70.3 1.2 copy-done.7
  71.5 0.0 copy-start.9
  71.5 1.2 copy-done.9
  72.7 2.0 %weight_pair.1 = bf16[4,328,640]{2,1,0:T(8,128)(2,1)S(1)} custom-call(bf16[1280,384]{1,0:T(8,128)(2,1)S(1)} %copy-done.7, bf16[1280,384]{1,0:T(8,128)(2,1)S(1)} %copy-done.9, bf16[384,640]{1,0:T(8,128)(2,1)S(1)} %get-tuple-element.20.right_ref, bf16[384,640]{1,0:T(8,128)(2,1)S(1)} %collective-permute-done.1.right_pair_ref, ...), custom_call_target="tpu_custom_call" | custom-call | flops 1258291200 | bytes 4633600 | tf_op jit(solution)/shard_map/weight_pair/pallas_call | solution.py:26
  74.8 24.8 %all_to_all.30.in_ref = bf16[4,328,640]{2,1,0:T(8,128)(2,1)S(1)} all-to-all(bf16[4,328,640]{2,1,0:T(8,128)(2,1)S(1)} %weight_pair.1), channel_id=1, replica_groups=mesh['dp_0'=4,'dp_1'=8,'z'=12,'core'=2] {'dp_0'}, dimensions={0} | all-to-all | bytes 3358720 | tf_op jit(solution)/shard_map/all_to_all | solution.py:39
  99.6 0.2 sum_first.1
  99.8 20.6 %all_to_all.31.in_ref = bf16[8,48,640]{2,1,0:T(8,128)(2,1)S(1)} all-to-all(bf16[8,48,640]{2,1,0:T(8,128)(2,1)S(1)} %sum_first.1), channel_id=1, replica_groups=mesh['dp_0'=4,'dp_1'=8,'z'=12,'core'=2] {'dp_1'}, dimensions={0} | all-to-all | bytes 983040 | tf_op jit(solution)/shard_map/all_to_all | solution.py:39
  120.5 0.1 sum_second.1
  120.5 13.7 %all_to_all.32.in_ref = bf16[12,4,640]{2,1,0:T(4,128)(2,1)S(1)} all-to-all(bf16[12,4,640]{2,1,0:T(4,128)(2,1)S(1)} %sum_second.1), channel_id=1, replica_groups=mesh['dp_0'=4,'dp_1'=8,'z'=12,'core'=2] {'z'}, dimensions={0} | all-to-all | bytes 122880 | tf_op jit(solution)/shard_map/all_to_all | solution.py:39
  134.3 18.9 %all_to_all.33.in_ref = bf16[24,4,640]{2,1,0:T(4,128)(2,1)S(1)} all-to-all(bf16[24,4,640]{2,1,0:T(4,128)(2,1)S(1)} %sum_third.1), channel_id=1, replica_groups=mesh['dp_0'=4,'dp_1'=8,'z'=12,'core'=2] {'z','core'}, dimensions={0} | all-to-all | bytes 245760 | tf_op jit(solution)/shard_map/all_to_all | solution.py:39
  153.2 0.8 joined.1
  154.0 3.9 %all-to-all-start.5 = ((f32[32,1,256]{2,1,0:T(1,128)}), f32[32,1,256]{2,1,0:T(1,128)S(1)}, u32[]{:S(2)}, u32[]{:S(2)}) async-start(f32[32,1,256]{2,1,0:T(1,128)} %get-tuple-element.23), calls=%async_computation.5 | async-start | bytes 65536 | tf_op jit(solution)/shard_map/all_to_all | solution.py:39
  157.8 0.0 copy-done
  157.8 3.6 %convolution_convert_fusion = bf16[384,1280]{1,0:T(8,128)(2,1)} fusion(bf16[384,1280]{1,0:T(8,128)(2,1)} %copy-done.5, bf16[1280,1280]{1,0:T(8,128)(2,1)S(1)} %copy-done), kind=kOutput, calls=%fused_computation | convolution fusion | flops 1258782720 | bytes 5242880 | tf_op jit(solution)/shard_map/dot_general | solution.py:307
  161.5 2.6 %reshape.44 = bf16[1,1,96,4,1280]{4,3,2,1,0:T(4,128)(2,1)} reshape(bf16[384,1280]{1,0:T(8,128)(2,1)} %convolution_convert_fusion) | data formatting | bytes 1966080 | tf_op jit(solution)/shard_map/reshape | solution.py:309
  164.0 2.5 %all-to-all-done.5.note_ref = f32[32,1,256]{2,1,0:T(1,128)S(1)} async-done(((f32[32,1,256]{2,1,0:T(1,128)}), f32[32,1,256]{2,1,0:T(1,128)S(1)}, u32[]{:S(2)}, u32[]{:S(2)}) %all-to-all-start.5) | async-done | bytes 32800 | tf_op jit(solution)/shard_map/all_to_all | solution.py:39
  166.5 0.9 scaled.1
  167.5 0.6 reduce
  (2 shorter events, 0.1 us)
Async XLA Ops:
  0.6 157.2 %copy-start = (bf16[1280,1280]{1,0:T(8,128)(2,1)S(1)}, bf16[1280,1280]{1,0:T(8,128)(2,1)}, u32[]{:S(2)}) copy-start(bf16[1280,1280]{1,0:T(8,128)(2,1)} %param.11) | copy-start | bytes 9830404
  0.6 21.9 %copy-start.10 = (f32[1280]{0:T(1024)S(1)}, f32[1280]{0:T(1024)}, u32[]{:S(2)}) copy-start(f32[1280]{0:T(1024)} %param.10) | copy-start | bytes 15364
  3.6 53.5 %all-to-all-start = ((bf16[24,16,1280]{2,1,0:T(8,128)(2,1)}), bf16[24,16,1280]{2,1,0:T(8,128)(2,1)}, u32[]{:S(2)}, u32[]{:S(2)}) async-start(bf16[24,16,1280]{2,1,0:T(8,128)(2,1)} %bitcast.12), calls=%async_computation | async-start | bytes 1966080 | tf_op jit(solution)/shard_map/all_to_all | solution.py:39
  20.4 4.8 %collective-permute-start = (bf16[96,4,1280]{2,1,0:T(4,128)(2,1)}, bf16[96,4,1280]{2,1,0:T(4,128)(2,1)}, u32[]{:S(2)}, u32[]{:S(2)}) collective-permute-start(bf16[96,4,1280]{2,1,0:T(4,128)(2,1)} %bitcast.10), channel_id=1, source_target_pairs={{0,1},{1,0},{2,3},{3,2},{4,5},{5,4},{6,7},{7,6},{8,9},{9,8},{10,11... | collective-permute-start | bytes 2949128 | tf_op jit(solution)/shard_map/ppermute | solution.py:236
  25.2 1.2 copy-start.1
  26.4 1.2 copy-start.2
  29.6 1.0 copy-start.3
  30.6 1.0 copy-start.6
  31.6 1.0 copy-start.8
  57.1 1.2 copy-start.4
  63.3 0.9 copy-start.5
  64.3 6.0 %collective-permute-start.1 = (bf16[384,640]{1,0:T(8,128)(2,1)S(1)}, bf16[384,640]{1,0:T(8,128)(2,1)S(1)}, u32[]{:S(2)}, u32[]{:S(2)}) collective-permute-start(bf16[384,640]{1,0:T(8,128)(2,1)S(1)} %get-tuple-element.21), channel_id=1, source_target_pairs={{0,1},{1,0},{2,3},{3,2},{4,5},{5,4},{6,7},{7,6},{8,9},{9,8},{10,11... | collective-permute-start | bytes 1474568 | tf_op jit(solution)/shard_map/ppermute | solution.py:271
  70.3 1.2 copy-start.7
  71.5 1.2 copy-start.9
  154.0 12.6 %all-to-all-start.5 = ((f32[32,1,256]{2,1,0:T(1,128)}), f32[32,1,256]{2,1,0:T(1,128)S(1)}, u32[]{:S(2)}, u32[]{:S(2)}) async-start(f32[32,1,256]{2,1,0:T(1,128)} %get-tuple-element.23), calls=%async_computation.5 | async-start | bytes 65536 | tf_op jit(solution)/shard_map/all_to_all | solution.py:39

commit v4 on v3

--- a/solution.py
+++ b/solution.py
@@ -85,8 +85,8 @@
 
 
 def norm_kernel(
-    chunks, step, core_ref, recv_ref, lines_ref, inverse_ref, gamma_ref,
-    grad_ref, keep_ref, send_ref, gain_ref, hold_ref, values_ref, made_ref, in_sems, value_sems, out_sems,
+    chunks, step, core_ref, recv_ref, lines_ref, left_ref, left_pair_ref, inverse_ref, gamma_ref,
+    keep_ref, send_ref, left_out_ref, left_pair_out_ref, gain_ref, hold_ref, values_ref, sems, left_sems,
 ):
     rows, features = recv_ref.shape
     half = features // 2
@@ -97,11 +97,17 @@
     for n in range(chunks):
         at = pl.ds(n * height, height)
         incoming.append((
-            pltpu.make_async_copy(recv_ref.at[at, :], hold_ref.at[at, :], in_sems.at[n]),
-            pltpu.make_async_copy(lines_ref.at[at, :], values_ref.at[at, :], value_sems.at[n]),
+            pltpu.make_async_copy(recv_ref.at[at, :], hold_ref.at[at, :], sems.at[2 * n]),
+            pltpu.make_async_copy(lines_ref.at[at, :], values_ref.at[at, :], sems.at[2 * n + 1]),
         ))
         for copy in incoming[-1]:
             copy.start()
+    lefts = (
+        pltpu.make_async_copy(left_ref, left_out_ref, left_sems.at[0]),
+        pltpu.make_async_copy(left_pair_ref, left_pair_out_ref, left_sems.at[1]),
+    )
+    for copy in lefts:
+        copy.start()
 
     def body(i, gain):
         at = pl.ds(pl.multiple_of(i * step, step), step)
@@ -112,24 +118,27 @@
         gain = gain + both.reshape(step // 8, 8, features).sum(0)
         centre = jnp.mean(gamma * both, axis=1, keepdims=True)
         made = (inverse * (gamma * gradient - normed * centre)).astype(bf16)
-        made_ref[at, :] = made
         low, high = made[:, :half], made[:, half:]
         keep_ref[at, :] = jnp.where(first, low, high)
         send_ref[at, :] = jnp.where(first, high, low)
         return gain
 
     gain = jnp.zeros((8, features), f32)
-    outgoing = []
     for n in range(chunks):
-        at = pl.ds(n * height, height)
         for copy in incoming[n]:
             copy.wait()
         gain = lax.fori_loop(n * height // step, (n + 1) * height // step, body, gain, unroll=2)
-        outgoing.append(pltpu.make_async_copy(made_ref.at[at, :], grad_ref.at[at, :], out_sems.at[n]))
-        outgoing[-1].start()
     gain_ref[...] = jnp.sum(gain, axis=0, keepdims=True)
-    for copy in outgoing:
+    for copy in lefts:
         copy.wait()
+
+
+def whole_kernel(core_ref, keep_ref, send_ref, grad_ref):
+    half = keep_ref.shape[1]
+    first = core_ref[0] == 0
+    keep, send = keep_ref[...], send_ref[...]
+    grad_ref[:, :half] = jnp.where(first, keep, send)
+    grad_ref[:, half:] = jnp.where(first, send, keep)
 
 
 def weight_kernel(left_ref, left_pair_ref, right_ref, right_pair_ref, gain_ref, out_ref):
@@ -201,7 +210,7 @@
     total = squares + jnp.sum(gain * gain)
     factor = f32(features) * lax.rsqrt(jnp.full((1, LANES), total + epsilon, f32))
     for n in range(chunks):
-        gain_out_ref[:, n * LANES:(n + 1) * LANES] = gain[n] * factor
+        gain_out_ref[n * LANES:(n + 1) * LANES] = (gain[n] * factor)[0]
         at = slice(n * LANES, (n + 1) * LANES)
         weight_out_ref[:, at] = weight_ref[:, at] * factor
 
@@ -246,29 +255,32 @@
         (xact.reshape(slot_count, patches, features), act_slots, act_pair),
     )
 
-    chunks = 6
-    grad, grad_keep, grad_send, gain_part = call(
+    chunks = 4
+    grad_keep, grad_send, left, left_pair, gain_part = call(
         functools.partial(norm_kernel, chunks, 16),
         "norm_backward",
         (
-            shaped(bf16, rows, features),
             shaped(bf16, rows, half),
             shaped(bf16, rows, half),
+            shaped(bf16, features, rows),
+            shaped(bf16, features, rows),
             shaped(f32, 1, features),
         ),
-        (core, received.reshape(rows, features), lines, inverse, gamma.reshape(1, features)),
-        far_in=(1, 2),
-        far_out=(0,),
+        (core, received.reshape(rows, features), lines, left, left_pair, inverse, gamma.reshape(1, features)),
+        far_in=(1, 2, 3, 4),
+        limit=50,
         scratch=[
             pltpu.VMEM((rows, features), bf16),
             pltpu.VMEM((rows, features), bf16),
-            pltpu.VMEM((rows, features), bf16),
-            pltpu.SemaphoreType.DMA((chunks,)),
-            pltpu.SemaphoreType.DMA((chunks,)),
-            pltpu.SemaphoreType.DMA((chunks,)),
+            pltpu.SemaphoreType.DMA((2 * chunks,)),
+            pltpu.SemaphoreType.DMA((2,)),
         ],
     )
     grad_pair = lax.ppermute(grad_send, "core", swap)
+    (grad,) = call(
+        whole_kernel, "whole_grad", (shaped(bf16, rows, features),), (core, grad_keep, grad_send), limit=52
+    )
+    grad, grad_keep = lax.optimization_barrier((grad, grad_keep))
 
     x_rows = features // x_count
     y_rows = x_rows // y_count
@@ -310,10 +322,10 @@
     weight_grad, gain_grad = call(
         functools.partial(scale_kernel, features),
         "scaled",
-        (shaped(f32, y_rows, features), shaped(f32, 1, features)),
+        (shaped(f32, y_rows, features), shaped(f32, features)),
         (exchange(note, DP), weight_sum),
     )
-    return (attn_grad, weight_grad, gain_grad.reshape(features))
+    return (attn_grad, weight_grad, gain_grad)
 
 
 def solution(mesh):

time: 169 us -> 162 us (0.959)
  local copies, waits for them, and re-layouts: 12.4 us -> 7.92 us
    unnamed x22 -> x16, local copies, waits for them, and re-layouts: 9.86 us -> 5.33 us
    pallas_call x9 -> x10, Pallas kernels: 14.2 us -> 12.7 us  [call(): pl.pallas_call(kernel, name=name, out_shape=outs, in_specs=specs, out_spe...]
where the time goes in v4:
time: 162 us; the launch traced here: 161 us
  blocking collectives  78 us (48%)
  waiting for transfers between devices  31 us (19%)
  starting transfers between devices  27.3 us (17%)
  Pallas kernels  12.7 us (8%)
  local copies, waits for them, and re-layouts  7.92 us (5%)
  matrix products  3.62 us (2%)
    all_to_all x4, blocking collectives, exchange(): return lax.all_to_all(blocks, axes, 0, 0, tiled=True)  78 us
    all_to_all x2, waiting for transfers between devices, exchange(): return lax.all_to_all(blocks, axes, 0, 0, tiled=True)  27 us
    all_to_all x2, starting transfers between devices, exchange(): return lax.all_to_all(blocks, axes, 0, 0, tiled=True)  20.6 us
    pallas_call x10, Pallas kernels, call(): pl.pallas_call(kernel, name=name, out_shape=outs, in_specs=specs, out_spe...  12.7 us
    unnamed x16, local copies, waits for them, and re-layouts  5.33 us
    ppermute x1, starting transfers between devices, on_device(): grad_pair = lax.ppermute(grad_send, 'core', swap)  4.56 us
    dot_general x1, matrix products, on_device(): lax.dot_general(grad, w_out, (((1,), (1,)), ((), ())), preferred_element_...  3.62 us
  transfers between devices with their start and end apart: 4, of which 4 were waited for; matrix products, arithmetic and copies ran while one was open for 4% of the time, Pallas kernels for 1%

profile of v4, /device:TPU:1, one launch (start us, length us, event | category | flops | bytes accessed | tf_op | source)
XLA Modules:
  0.0 161.4 jit_solution(11743696776085027668)
XLA Ops:
  0.6 0.0 copy-start
  0.6 0.0 copy-start.7
  0.7 3.0 %gather_rows.1 = bf16[384,1280]{1,0:T(8,128)(2,1)} custom-call(s32[1,80]{1,0:T(1,128)} %bitcast.14, bf16[80,4,1280]{2,1,0:T(4,128)(2,1)} %bitcast.13), custom_call_target="tpu_custom_call" | custom-call | flops 1000000 | bytes 1802560 | tf_op jit(solution)/shard_map/gather_rows/pallas_call | solution.py:26
  3.6 16.7 %all-to-all-start = ((bf16[24,16,1280]{2,1,0:T(8,128)(2,1)}), bf16[24,16,1280]{2,1,0:T(8,128)(2,1)}, u32[]{:S(2)}, u32[]{:S(2)}) async-start(bf16[24,16,1280]{2,1,0:T(8,128)(2,1)} %bitcast.12), calls=%async_computation | async-start | bytes 1966080 | tf_op jit(solution)/shard_map/all_to_all | solution.py:39
  20.4 2.2 %collective-permute-start = (bf16[96,4,1280]{2,1,0:T(4,128)(2,1)}, bf16[96,4,1280]{2,1,0:T(4,128)(2,1)}, u32[]{:S(2)}, u32[]{:S(2)}) collective-permute-start(bf16[96,4,1280]{2,1,0:T(4,128)(2,1)} %bitcast.10), channel_id=1, source_target_pairs={{0,1},{1,0},{2,3},{3,2},{4,5},{5,4},{6,7},{7,6},{8,9},{9,8},{10,11... | collective-permute-start | bytes 2949128 | tf_op jit(solution)/shard_map/ppermute | solution.py:245
  22.5 0.0 copy-done.7
  22.6 2.6 %collective-permute-done.pair_ref = bf16[96,4,1280]{2,1,0:T(4,128)(2,1)} collective-permute-done((bf16[96,4,1280]{2,1,0:T(4,128)(2,1)}, bf16[96,4,1280]{2,1,0:T(4,128)(2,1)}, u32[]{:S(2)}, u32[]{:S(2)}) %collective-permute-start) | collective-permute-done | bytes 983072 | tf_op jit(solution)/shard_map/ppermute | solution.py:245
  25.2 0.0 copy-start.1
  25.2 1.2 copy-done.1
  26.4 0.0 copy-start.2
  26.4 1.2 copy-done.2
  27.6 2.1 %prepare.1 = (bf16[384,1280]{1,0:T(8,128)(2,1)S(1)}, f32[384,1]{1,0:T(8,128)S(1)}, bf16[1280,384]{1,0:T(8,128)(2,1)S(1)}, bf16[1280,384]{1,0:T(8,128)(2,1)S(1)}) custom-call(bf16[96,4,1280]{2,1,0:T(4,128)(2,1)S(1)} %bitcast.9, bf16[96,4,1280]{2,1,0:T(4,128)(2,1)S(1)} %bitcast.11, bf16[96,4,1280]{2,1,0:T(4,128)(2,1)} %collective-permute-done.pair_ref), custom_call_target="tpu_custom_call" | custom-call | flops 1000000 | bytes 5899776 | tf_op jit(solution)/shard_map/prepare/pallas_call | solution.py:26
  29.6 0.0 copy-start.4
  29.7 1.0 copy-done.4
  30.6 0.0 copy-start.5
  30.6 1.0 copy-done.5
  31.6 0.0 copy-start.6
  31.6 1.0 copy-done.6
  32.6 24.5 %all-to-all-done = bf16[24,16,1280]{2,1,0:T(8,128)(2,1)} async-done(((bf16[24,16,1280]{2,1,0:T(8,128)(2,1)}), bf16[24,16,1280]{2,1,0:T(8,128)(2,1)}, u32[]{:S(2)}, u32[]{:S(2)}) %all-to-all-start) | async-done | bytes 983072 | tf_op jit(solution)/shard_map/all_to_all | solution.py:39
  57.1 3.5 %norm_backward.1 = (bf16[384,640]{1,0:T(8,128)(2,1)S(1)}, bf16[384,640]{1,0:T(8,128)(2,1)S(1)}, bf16[1280,384]{1,0:T(8,128)(2,1)S(1)}, bf16[1280,384]{1,0:T(8,128)(2,1)S(1)}, f32[1,1280]{1,0:T(1,128)S(1)}) custom-call(s32[1]{0:T(128)} %bitcast.core_ref, bf16[384,1280]{1,0:T(8,128)(2,1)} %bitcast.4.recv_ref, bf16[384,1280]{1,0:T(8,128)(2,1)} %copy-done.4, ...), custom_call_target="tpu_custom_call" | custom-call | flops 1000000 | bytes 6893060 | tf_op jit(solution)/shard_map/norm_backward/pallas_call | solution.py:26
  60.6 4.6 %collective-permute-start.1 = (bf16[384,640]{1,0:T(8,128)(2,1)S(1)}, bf16[384,640]{1,0:T(8,128)(2,1)S(1)}, u32[]{:S(2)}, u32[]{:S(2)}) collective-permute-start(bf16[384,640]{1,0:T(8,128)(2,1)S(1)} %get-tuple-element.23.send_ref), channel_id=1, source_target_pairs={{0,1},{1,0},{2,3},{3,2},{4,5},{5,4},{6,7},{7,6},{8,9},{9,8},{10,11... | collective-permute-start | bytes 1474568 | tf_op jit(solution)/shard_map/ppermute | solution.py:279
  65.2 0.1 whole_grad.1
  65.3 0.0 copy-start.3
  65.3 1.4 collective-permute-done.1.right_pair_ref
  66.7 2.0 %weight_pair.1 = bf16[4,328,640]{2,1,0:T(8,128)(2,1)S(1)} custom-call(bf16[1280,384]{1,0:T(8,128)(2,1)S(1)} %get-tuple-element.25.left_ref, bf16[1280,384]{1,0:T(8,128)(2,1)S(1)} %get-tuple-element.26.left_pair_ref, bf16[384,640]{1,0:T(8,128)(2,1)S(1)} %get-tuple-element.27.keep_ref.right_ref, bf16[384,640]{1,0:T(8,128)(2,1)S(1)} %collective-permute-done.1.right_pair_ref, ...), custom_call_target="tpu_custom_call" | custom-call | flops 1258291200 | bytes 4633600 | tf_op jit(solution)/shard_map/weight_pair/pallas_call | solution.py:26
  68.7 24.8 %all_to_all.30.in_ref = bf16[4,328,640]{2,1,0:T(8,128)(2,1)S(1)} all-to-all(bf16[4,328,640]{2,1,0:T(8,128)(2,1)S(1)} %weight_pair.1), channel_id=1, replica_groups=mesh['dp_0'=4,'dp_1'=8,'z'=12,'core'=2] {'dp_0'}, dimensions={0} | all-to-all | bytes 3358720 | tf_op jit(solution)/shard_map/all_to_all | solution.py:39
  93.5 0.0 copy-done.3
  93.5 0.2 sum_first.1
  93.8 20.6 %all_to_all.31.in_ref = bf16[8,48,640]{2,1,0:T(8,128)(2,1)S(1)} all-to-all(bf16[8,48,640]{2,1,0:T(8,128)(2,1)S(1)} %sum_first.1), channel_id=1, replica_groups=mesh['dp_0'=4,'dp_1'=8,'z'=12,'core'=2] {'dp_1'}, dimensions={0} | all-to-all | bytes 983040 | tf_op jit(solution)/shard_map/all_to_all | solution.py:39
  114.4 0.1 sum_second.1
  114.5 13.8 %all_to_all.32.in_ref = bf16[12,4,640]{2,1,0:T(4,128)(2,1)S(1)} all-to-all(bf16[12,4,640]{2,1,0:T(4,128)(2,1)S(1)} %sum_second.1), channel_id=1, replica_groups=mesh['dp_0'=4,'dp_1'=8,'z'=12,'core'=2] {'z'}, dimensions={0} | all-to-all | bytes 122880 | tf_op jit(solution)/shard_map/all_to_all | solution.py:39
  128.3 18.9 %all_to_all.33.in_ref = bf16[24,4,640]{2,1,0:T(4,128)(2,1)S(1)} all-to-all(bf16[24,4,640]{2,1,0:T(4,128)(2,1)S(1)} %sum_third.1), channel_id=1, replica_groups=mesh['dp_0'=4,'dp_1'=8,'z'=12,'core'=2] {'z','core'}, dimensions={0} | all-to-all | bytes 245760 | tf_op jit(solution)/shard_map/all_to_all | solution.py:39
  147.1 0.8 joined.1
  147.9 3.9 %all-to-all-start.5 = ((f32[32,1,256]{2,1,0:T(1,128)}), f32[32,1,256]{2,1,0:T(1,128)S(1)}, u32[]{:S(2)}, u32[]{:S(2)}) async-start(f32[32,1,256]{2,1,0:T(1,128)} %get-tuple-element.29), calls=%async_computation.5 | async-start | bytes 65536 | tf_op jit(solution)/shard_map/all_to_all | solution.py:39
  151.8 0.0 copy-done
  151.8 3.6 %convolution_convert_fusion = bf16[384,1280]{1,0:T(8,128)(2,1)} fusion(bf16[384,1280]{1,0:T(8,128)(2,1)} %copy-done.3, bf16[1280,1280]{1,0:T(8,128)(2,1)S(1)} %copy-done), kind=kOutput, calls=%fused_computation | convolution fusion | flops 1258782720 | bytes 5242880 | tf_op jit(solution)/shard_map/dot_general | solution.py:319
  155.4 2.6 %reshape.41 = bf16[1,1,96,4,1280]{4,3,2,1,0:T(4,128)(2,1)} reshape(bf16[384,1280]{1,0:T(8,128)(2,1)} %convolution_convert_fusion) | data formatting | bytes 1966080 | tf_op jit(solution)/shard_map/reshape | solution.py:321
  158.0 2.5 %all-to-all-done.5.note_ref = f32[32,1,256]{2,1,0:T(1,128)S(1)} async-done(((f32[32,1,256]{2,1,0:T(1,128)}), f32[32,1,256]{2,1,0:T(1,128)S(1)}, u32[]{:S(2)}, u32[]{:S(2)}) %all-to-all-start.5) | async-done | bytes 32800 | tf_op jit(solution)/shard_map/all_to_all | solution.py:39
  160.5 0.9 scaled.1
  (2 shorter events, 0.1 us)
Async XLA Ops:
  0.6 151.1 %copy-start = (bf16[1280,1280]{1,0:T(8,128)(2,1)S(1)}, bf16[1280,1280]{1,0:T(8,128)(2,1)}, u32[]{:S(2)}) copy-start(bf16[1280,1280]{1,0:T(8,128)(2,1)} %param.11) | copy-start | bytes 9830404
  0.6 21.9 %copy-start.7 = (f32[1280]{0:T(1024)S(1)}, f32[1280]{0:T(1024)}, u32[]{:S(2)}) copy-start(f32[1280]{0:T(1024)} %param.10) | copy-start | bytes 15364
  3.6 53.5 %all-to-all-start = ((bf16[24,16,1280]{2,1,0:T(8,128)(2,1)}), bf16[24,16,1280]{2,1,0:T(8,128)(2,1)}, u32[]{:S(2)}, u32[]{:S(2)}) async-start(bf16[24,16,1280]{2,1,0:T(8,128)(2,1)} %bitcast.12), calls=%async_computation | async-start | bytes 1966080 | tf_op jit(solution)/shard_map/all_to_all | solution.py:39
  20.4 4.8 %collective-permute-start = (bf16[96,4,1280]{2,1,0:T(4,128)(2,1)}, bf16[96,4,1280]{2,1,0:T(4,128)(2,1)}, u32[]{:S(2)}, u32[]{:S(2)}) collective-permute-start(bf16[96,4,1280]{2,1,0:T(4,128)(2,1)} %bitcast.10), channel_id=1, source_target_pairs={{0,1},{1,0},{2,3},{3,2},{4,5},{5,4},{6,7},{7,6},{8,9},{9,8},{10,11... | collective-permute-start | bytes 2949128 | tf_op jit(solution)/shard_map/ppermute | solution.py:245
  25.2 1.2 copy-start.1
  26.4 1.2 copy-start.2
  29.6 1.0 copy-start.4
  30.6 1.0 copy-start.5
  31.6 1.0 copy-start.6
  60.6 6.0 %collective-permute-start.1 = (bf16[384,640]{1,0:T(8,128)(2,1)S(1)}, bf16[384,640]{1,0:T(8,128)(2,1)S(1)}, u32[]{:S(2)}, u32[]{:S(2)}) collective-permute-start(bf16[384,640]{1,0:T(8,128)(2,1)S(1)} %get-tuple-element.23.send_ref), channel_id=1, source_target_pairs={{0,1},{1,0},{2,3},{3,2},{4,5},{5,4},{6,7},{7,6},{8,9},{9,8},{10,11... | collective-permute-start | bytes 1474568 | tf_op jit(solution)/shard_map/ppermute | solution.py:279
  65.3 28.2 %copy-start.3 = (bf16[384,1280]{1,0:T(8,128)(2,1)}, bf16[384,1280]{1,0:T(8,128)(2,1)S(1)}, u32[]{:S(2)}) copy-start(bf16[384,1280]{1,0:T(8,128)(2,1)S(1)} %whole_grad.1) | copy-start | bytes 2949124
  147.9 12.6 %all-to-all-start.5 = ((f32[32,1,256]{2,1,0:T(1,128)}), f32[32,1,256]{2,1,0:T(1,128)S(1)}, u32[]{:S(2)}, u32[]{:S(2)}) async-start(f32[32,1,256]{2,1,0:T(1,128)} %get-tuple-element.29), calls=%async_computation.5 | async-start | bytes 65536 | tf_op jit(solution)/shard_map/all_to_all | solution.py:39

commit v5 on v4

--- a/solution.py
+++ b/solution.py
@@ -8,7 +8,9 @@
 from jax.sharding import Mesh
 from jax.sharding import PartitionSpec as P
 
-DP = ("dp_0", "dp_1")
+DP = ("dp_0", "dp_1", "dp_2")
+FIRST = ("dp_0", "dp_2")
+SECOND = ("dp_1", "z")
 SEQ = ("z", "core")
 LANES = 128
 
@@ -141,44 +143,50 @@
     grad_ref[:, half:] = jnp.where(first, send, keep)
 
 
-def weight_kernel(left_ref, left_pair_ref, right_ref, right_pair_ref, gain_ref, out_ref):
-    blocks, height, _ = out_ref.shape
-    rows = height - 8
+def weight_kernel(shape, left_ref, left_pair_ref, right_ref, right_pair_ref, gain_ref, out_ref):
+    outer, middle, inner = shape
+    rows = (out_ref.shape[1] - 8) // middle
+    width = out_ref.shape[2]
     gain = gain_ref[...]
     chunks = gain.shape[1] // LANES
-    for b in range(blocks):
-        at = slice(b * rows, (b + 1) * rows)
-        out_ref[b, :rows, :] = (
+    for b in range(outer):
+        at = slice(b * middle * inner * rows, (b + 1) * middle * inner * rows)
+        block = (
             jnp.dot(left_ref[at, :], right_ref[...], preferred_element_type=f32)
             + jnp.dot(left_pair_ref[at, :], right_pair_ref[...], preferred_element_type=f32)
         ).astype(bf16)
-        out_ref[b, rows:, :] = jnp.zeros((8, out_ref.shape[2]), bf16)
-        lines = [
-            gain[:, n * LANES:(n + 1) * LANES] if n < chunks else jnp.zeros((1, LANES), f32)
-            for n in range(b * 8, b * 8 + 8)
-        ]
-        if b * 8 < chunks:
-            out_ref[b, rows:, :LANES] = jnp.concatenate(lines, axis=0).astype(bf16)
-
-
-def first_sum_kernel(in_ref, out_ref):
-    blocks, height, width = out_ref.shape
-    rows = height - 8
-    lines = in_ref[:, blocks * rows:, :].astype(f32).sum(0)
-    for b in range(blocks):
-        out_ref[b, :rows, :] = in_ref[:, b * rows:(b + 1) * rows, :].astype(f32).sum(0).astype(bf16)
-        own = jnp.where(iota((8, width), 0) == 0, lines[b:b + 1, :], 0.0)
-        out_ref[b, rows:, :] = own.astype(bf16)
+        for i in range(inner):
+            lines = []
+            for m in range(middle):
+                own = m * inner + i
+                out_ref[b * inner + i, m * rows:(m + 1) * rows, :] = block[own * rows:(own + 1) * rows, :]
+                n = b * middle * inner + own
+                if n < chunks:
+                    lines.append(gain[:, n * LANES:(n + 1) * LANES])
+            out_ref[b * inner + i, middle * rows:, :] = jnp.zeros((8, width), bf16)
+            if lines:
+                lines += [jnp.zeros((1, LANES), f32)] * (8 - len(lines))
+                out_ref[b * inner + i, middle * rows:, :LANES] = jnp.concatenate(lines, axis=0).astype(bf16)
+
+
+def first_sum_kernel(middle, in_ref, out_ref):
+    pieces, height, width = out_ref.shape
+    pieces //= middle
+    rows = (in_ref.shape[1] - 8) // middle
+    lines = in_ref[:, middle * rows:, :].astype(f32).sum(0)
+    for m in range(middle):
+        total = in_ref[:, m * rows:(m + 1) * rows, :].astype(f32).sum(0)
+        for p in range(pieces):
+            if p * height < rows:
+                piece = total[p * height:(p + 1) * height, :]
+            elif p * height == rows:
+                piece = jnp.where(iota((height, width), 0) == 0, lines[m:m + 1, :], 0.0)
+            else:
+                piece = jnp.zeros((height, width), f32)
+            out_ref[m * pieces + p] = piece.astype(bf16)
 
 
 def second_sum_kernel(in_ref, out_ref):
-    total = in_ref[...].astype(f32).sum(0)
-    pieces, height, _ = out_ref.shape
-    for b in range(pieces):
-        out_ref[b] = total[b * height:(b + 1) * height, :].astype(bf16)
-
-
-def third_sum_kernel(in_ref, out_ref):
     total = in_ref[...].astype(f32).sum(0)
     total = total.astype(bf16)
     for b in range(out_ref.shape[0]):
@@ -217,7 +225,7 @@
 
 def on_device(grad_rows, row_owner, acts, xact, gamma, w_out):
     seq_count = lax.axis_size(SEQ)
-    x_count, y_count, z_count = (lax.axis_size(a) for a in ("dp_0", "dp_1", "z"))
+    outer, middle, inner, z_count = (lax.axis_size(a) for a in (*DP, "z"))
     tokens = row_owner.shape[1]
     slot_count, patches, features = acts.shape[2:]
     capacity = slot_count // seq_count
@@ -282,38 +290,31 @@
     )
     grad, grad_keep = lax.optimization_barrier((grad, grad_keep))
 
-    x_rows = features // x_count
-    y_rows = x_rows // y_count
-    z_rows = (y_rows + 8) // z_count
+    out_rows = features // (outer * middle * inner)
+    z_rows = (out_rows + 8) // z_count
     (weight_pair,) = call(
-        weight_kernel,
+        functools.partial(weight_kernel, (outer, middle, inner)),
         "weight_pair",
-        (shaped(bf16, x_count, x_rows + 8, half),),
+        (shaped(bf16, outer * inner, middle * out_rows + 8, half),),
         (left, left_pair, grad_keep, grad_pair, gain_part),
         flops=4 * features * half * rows,
     )
-    (weight_x,) = call(
-        first_sum_kernel,
+    (weight_some,) = call(
+        functools.partial(first_sum_kernel, middle),
         "sum_first",
-        (shaped(bf16, y_count, y_rows + 8, half),),
-        (exchange(weight_pair, "dp_0"),),
-    )
-    (weight_y,) = call(
+        (shaped(bf16, middle * z_count, z_rows, half),),
+        (exchange(weight_pair, FIRST),),
+    )
+    (pieces,) = call(
         second_sum_kernel,
         "sum_second",
-        (shaped(bf16, z_count, z_rows, half),),
-        (exchange(weight_x, "dp_1"),),
-    )
-    (pieces,) = call(
-        third_sum_kernel,
-        "sum_third",
         (shaped(bf16, seq_count, z_rows, half),),
-        (exchange(weight_y, "z"),),
+        (exchange(weight_some, SECOND),),
     )
     weight_sum, note = call(
         joined_kernel,
         "joined",
-        (shaped(f32, y_rows, features), shaped(f32, x_count * y_count, 1, 2 * LANES)),
+        (shaped(f32, out_rows, features), shaped(f32, outer * middle * inner, 1, 2 * LANES)),
         (exchange(pieces, SEQ),),
     )
     attn_grad = lax.dot_general(
@@ -322,14 +323,14 @@
     weight_grad, gain_grad = call(
         functools.partial(scale_kernel, features),
         "scaled",
-        (shaped(f32, y_rows, features), shaped(f32, features)),
+        (shaped(f32, out_rows, features), shaped(f32, features)),
         (exchange(note, DP), weight_sum),
     )
     return (attn_grad, weight_grad, gain_grad)
 
 
 def solution(mesh):
-    finer = Mesh(mesh.devices.reshape(4, 8, mesh.shape["seq"] // 2, 2), (*DP, *SEQ))
+    finer = Mesh(mesh.devices.reshape(4, 4, 2, mesh.shape["seq"] // 2, 2), (*DP, *SEQ))
     placed = (
         P(DP, SEQ, None, None),
         P(DP, SEQ, None),

time: 162 us -> 155 us (0.957)
  blocking collectives: 78 us -> 70.9 us
    all_to_all x4 -> x3, blocking collectives: 78 us -> 70.9 us  [exchange(): return lax.all_to_all(blocks, axes, 0, 0, tiled=True)]
    pallas_call x10 -> x9, Pallas kernels: 12.7 us -> 12.8 us  [call(): pl.pallas_call(kernel, name=name, out_shape=outs, in_specs=specs, out_spe...]
where the time goes in v5:
time: 155 us; the launch traced here: 154 us
  blocking collectives  70.9 us (46%)
  waiting for transfers between devices  31 us (20%)
  starting transfers between devices  27.3 us (18%)
  Pallas kernels  12.8 us (8%)
  local copies, waits for them, and re-layouts  7.92 us (5%)
  matrix products  3.62 us (2%)
    all_to_all x3, blocking collectives, exchange(): return lax.all_to_all(blocks, axes, 0, 0, tiled=True)  70.9 us
    all_to_all x2, waiting for transfers between devices, exchange(): return lax.all_to_all(blocks, axes, 0, 0, tiled=True)  27 us
    all_to_all x2, starting transfers between devices, exchange(): return lax.all_to_all(blocks, axes, 0, 0, tiled=True)  20.6 us
    pallas_call x9, Pallas kernels, call(): pl.pallas_call(kernel, name=name, out_shape=outs, in_specs=specs, out_spe...  12.8 us
    unnamed x16, local copies, waits for them, and re-layouts  5.33 us
    ppermute x1, starting transfers between devices, on_device(): grad_pair = lax.ppermute(grad_send, 'core', swap)  4.56 us
    dot_general x1, matrix products, on_device(): lax.dot_general(grad, w_out, (((1,), (1,)), ((), ())), preferred_element_...  3.62 us
  transfers between devices with their start and end apart: 4, of which 4 were waited for; matrix products, arithmetic and copies ran while one was open for 4% of the time, Pallas kernels for 1%

profile of v5, /device:TPU:1, one launch (start us, length us, event | category | flops | bytes accessed | tf_op | source)
XLA Modules:
  0.0 154.3 jit_solution(3513676116442056528)
XLA Ops:
  0.6 0.0 copy-start
  0.6 0.0 copy-start.7
  0.7 3.0 %gather_rows.1 = bf16[384,1280]{1,0:T(8,128)(2,1)} custom-call(s32[1,80]{1,0:T(1,128)} %bitcast.14, bf16[80,4,1280]{2,1,0:T(4,128)(2,1)} %bitcast.13), custom_call_target="tpu_custom_call" | custom-call | flops 1000000 | bytes 1802560 | tf_op jit(solution)/shard_map/gather_rows/pallas_call | solution.py:28
  3.6 16.7 %all-to-all-start = ((bf16[24,16,1280]{2,1,0:T(8,128)(2,1)}), bf16[24,16,1280]{2,1,0:T(8,128)(2,1)}, u32[]{:S(2)}, u32[]{:S(2)}) async-start(bf16[24,16,1280]{2,1,0:T(8,128)(2,1)} %bitcast.12), calls=%async_computation | async-start | bytes 1966080 | tf_op jit(solution)/shard_map/all_to_all | solution.py:41
  20.4 2.2 %collective-permute-start = (bf16[96,4,1280]{2,1,0:T(4,128)(2,1)}, bf16[96,4,1280]{2,1,0:T(4,128)(2,1)}, u32[]{:S(2)}, u32[]{:S(2)}) collective-permute-start(bf16[96,4,1280]{2,1,0:T(4,128)(2,1)} %bitcast.10), channel_id=1, source_target_pairs={{0,1},{1,0},{2,3},{3,2},{4,5},{5,4},{6,7},{7,6},{8,9},{9,8},{10,11... | collective-permute-start | bytes 2949128 | tf_op jit(solution)/shard_map/ppermute | solution.py:253
  22.5 0.0 copy-done.7
  22.6 2.6 %collective-permute-done.pair_ref = bf16[96,4,1280]{2,1,0:T(4,128)(2,1)} collective-permute-done((bf16[96,4,1280]{2,1,0:T(4,128)(2,1)}, bf16[96,4,1280]{2,1,0:T(4,128)(2,1)}, u32[]{:S(2)}, u32[]{:S(2)}) %collective-permute-start) | collective-permute-done | bytes 983072 | tf_op jit(solution)/shard_map/ppermute | solution.py:253
  25.2 0.0 copy-start.1
  25.2 1.2 copy-done.1
  26.4 0.0 copy-start.2
  26.4 1.2 copy-done.2
  27.6 2.1 %prepare.1 = (bf16[384,1280]{1,0:T(8,128)(2,1)S(1)}, f32[384,1]{1,0:T(8,128)S(1)}, bf16[1280,384]{1,0:T(8,128)(2,1)S(1)}, bf16[1280,384]{1,0:T(8,128)(2,1)S(1)}) custom-call(bf16[96,4,1280]{2,1,0:T(4,128)(2,1)S(1)} %bitcast.9, bf16[96,4,1280]{2,1,0:T(4,128)(2,1)S(1)} %bitcast.11, bf16[96,4,1280]{2,1,0:T(4,128)(2,1)} %collective-permute-done.pair_ref), custom_call_target="tpu_custom_call" | custom-call | flops 1000000 | bytes 5899776 | tf_op jit(solution)/shard_map/prepare/pallas_call | solution.py:28
  29.6 0.0 copy-start.4
  29.7 1.0 copy-done.4
  30.6 0.0 copy-start.5
  30.6 1.0 copy-done.5
  31.6 0.0 copy-start.6
  31.6 1.0 copy-done.6
  32.6 24.5 %all-to-all-done = bf16[24,16,1280]{2,1,0:T(8,128)(2,1)} async-done(((bf16[24,16,1280]{2,1,0:T(8,128)(2,1)}), bf16[24,16,1280]{2,1,0:T(8,128)(2,1)}, u32[]{:S(2)}, u32[]{:S(2)}) %all-to-all-start) | async-done | bytes 983072 | tf_op jit(solution)/shard_map/all_to_all | solution.py:41
  57.1 3.5 %norm_backward.1 = (bf16[384,640]{1,0:T(8,128)(2,1)S(1)}, bf16[384,640]{1,0:T(8,128)(2,1)S(1)}, bf16[1280,384]{1,0:T(8,128)(2,1)S(1)}, bf16[1280,384]{1,0:T(8,128)(2,1)S(1)}, f32[1,1280]{1,0:T(1,128)S(1)}) custom-call(s32[1]{0:T(128)} %bitcast.core_ref, bf16[384,1280]{1,0:T(8,128)(2,1)} %bitcast.4.recv_ref, bf16[384,1280]{1,0:T(8,128)(2,1)} %copy-done.4, ...), custom_call_target="tpu_custom_call" | custom-call | flops 1000000 | bytes 6893060 | tf_op jit(solution)/shard_map/norm_backward/pallas_call | solution.py:28
  60.6 4.6 %collective-permute-start.1 = (bf16[384,640]{1,0:T(8,128)(2,1)S(1)}, bf16[384,640]{1,0:T(8,128)(2,1)S(1)}, u32[]{:S(2)}, u32[]{:S(2)}) collective-permute-start(bf16[384,640]{1,0:T(8,128)(2,1)S(1)} %get-tuple-element.23.send_ref), channel_id=1, source_target_pairs={{0,1},{1,0},{2,3},{3,2},{4,5},{5,4},{6,7},{7,6},{8,9},{9,8},{10,11... | collective-permute-start | bytes 1474568 | tf_op jit(solution)/shard_map/ppermute | solution.py:287
  65.2 0.1 whole_grad.1
  65.3 0.0 copy-start.3
  65.3 1.4 collective-permute-done.1.right_pair_ref
  66.7 2.0 %weight_pair.1 = bf16[8,168,640]{2,1,0:T(8,128)(2,1)S(1)} custom-call(bf16[1280,384]{1,0:T(8,128)(2,1)S(1)} %get-tuple-element.25.left_ref, bf16[1280,384]{1,0:T(8,128)(2,1)S(1)} %get-tuple-element.26.left_pair_ref, bf16[384,640]{1,0:T(8,128)(2,1)S(1)} %get-tuple-element.27.keep_ref.right_ref, bf16[384,640]{1,0:T(8,128)(2,1)S(1)} %collective-permute-done.1.right_pair_ref, ...), custom_call_target="tpu_custom_call" | custom-call | flops 1258291200 | bytes 4674560 | tf_op jit(solution)/shard_map/weight_pair/pallas_call | solution.py:28
  68.7 27.2 %all_to_all.25.in_ref = bf16[8,168,640]{2,1,0:T(8,128)(2,1)S(1)} all-to-all(bf16[8,168,640]{2,1,0:T(8,128)(2,1)S(1)} %weight_pair.1), channel_id=1, replica_groups=mesh['dp_0'=4,'dp_1'=4,'dp_2'=2,'z'=12,'core'=2] {'dp_0','dp_2'}, dimensions={0} | all-to-all | bytes 3440640 | tf_op jit(solution)/shard_map/all_to_all | solution.py:41
  95.9 0.0 copy-done.3
  95.9 0.2 sum_first.1
  96.1 24.4 %all_to_all.26.in_ref = bf16[48,4,640]{2,1,0:T(4,128)(2,1)S(1)} all-to-all(bf16[48,4,640]{2,1,0:T(4,128)(2,1)S(1)} %sum_first.1), channel_id=1, replica_groups=mesh['dp_0'=4,'dp_1'=4,'dp_2'=2,'z'=12,'core'=2] {'dp_1','z'}, dimensions={0} | all-to-all | bytes 491520 | tf_op jit(solution)/shard_map/all_to_all | solution.py:41
  120.5 0.1 sum_second.1
  120.7 19.3 %all_to_all.27.in_ref = bf16[24,4,640]{2,1,0:T(4,128)(2,1)S(1)} all-to-all(bf16[24,4,640]{2,1,0:T(4,128)(2,1)S(1)} %sum_second.1), channel_id=1, replica_groups=mesh['dp_0'=4,'dp_1'=4,'dp_2'=2,'z'=12,'core'=2] {'z','core'}, dimensions={0} | all-to-all | bytes 245760 | tf_op jit(solution)/shard_map/all_to_all | solution.py:41
  140.0 0.8 joined.1
  140.8 3.9 %all-to-all-start.4 = ((f32[32,1,256]{2,1,0:T(1,128)}), f32[32,1,256]{2,1,0:T(1,128)S(1)}, u32[]{:S(2)}, u32[]{:S(2)}) async-start(f32[32,1,256]{2,1,0:T(1,128)} %get-tuple-element.29), calls=%async_computation.4 | async-start | bytes 65536 | tf_op jit(solution)/shard_map/all_to_all | solution.py:41
  144.6 0.0 copy-done
  144.6 3.6 %convolution_convert_fusion = bf16[384,1280]{1,0:T(8,128)(2,1)} fusion(bf16[384,1280]{1,0:T(8,128)(2,1)} %copy-done.3, bf16[1280,1280]{1,0:T(8,128)(2,1)S(1)} %copy-done), kind=kOutput, calls=%fused_computation | convolution fusion | flops 1258782720 | bytes 5242880 | tf_op jit(solution)/shard_map/dot_general | solution.py:320
  148.3 2.6 %reshape.41 = bf16[1,1,96,4,1280]{4,3,2,1,0:T(4,128)(2,1)} reshape(bf16[384,1280]{1,0:T(8,128)(2,1)} %convolution_convert_fusion) | data formatting | bytes 1966080 | tf_op jit(solution)/shard_map/reshape | solution.py:322
  150.8 2.5 %all-to-all-done.4.note_ref = f32[32,1,256]{2,1,0:T(1,128)S(1)} async-done(((f32[32,1,256]{2,1,0:T(1,128)}), f32[32,1,256]{2,1,0:T(1,128)S(1)}, u32[]{:S(2)}, u32[]{:S(2)}) %all-to-all-start.4) | async-done | bytes 32800 | tf_op jit(solution)/shard_map/all_to_all | solution.py:41
  153.3 0.9 scaled.1
  (1 shorter events, 0.0 us)
Async XLA Ops:
  0.6 144.0 %copy-start = (bf16[1280,1280]{1,0:T(8,128)(2,1)S(1)}, bf16[1280,1280]{1,0:T(8,128)(2,1)}, u32[]{:S(2)}) copy-start(bf16[1280,1280]{1,0:T(8,128)(2,1)} %param.11) | copy-start | bytes 9830404
  0.6 21.9 %copy-start.7 = (f32[1280]{0:T(1024)S(1)}, f32[1280]{0:T(1024)}, u32[]{:S(2)}) copy-start(f32[1280]{0:T(1024)} %param.10) | copy-start | bytes 15364
  3.6 53.5 %all-to-all-start = ((bf16[24,16,1280]{2,1,0:T(8,128)(2,1)}), bf16[24,16,1280]{2,1,0:T(8,128)(2,1)}, u32[]{:S(2)}, u32[]{:S(2)}) async-start(bf16[24,16,1280]{2,1,0:T(8,128)(2,1)} %bitcast.12), calls=%async_computation | async-start | bytes 1966080 | tf_op jit(solution)/shard_map/all_to_all | solution.py:41
  20.4 4.8 %collective-permute-start = (bf16[96,4,1280]{2,1,0:T(4,128)(2,1)}, bf16[96,4,1280]{2,1,0:T(4,128)(2,1)}, u32[]{:S(2)}, u32[]{:S(2)}) collective-permute-start(bf16[96,4,1280]{2,1,0:T(4,128)(2,1)} %bitcast.10), channel_id=1, source_target_pairs={{0,1},{1,0},{2,3},{3,2},{4,5},{5,4},{6,7},{7,6},{8,9},{9,8},{10,11... | collective-permute-start | bytes 2949128 | tf_op jit(solution)/shard_map/ppermute | solution.py:253
  25.2 1.2 copy-start.1
  26.4 1.2 copy-start.2
  29.6 1.0 copy-start.4
  30.6 1.0 copy-start.5
  31.6 1.0 copy-start.6
  60.6 6.0 %collective-permute-start.1 = (bf16[384,640]{1,0:T(8,128)(2,1)S(1)}, bf16[384,640]{1,0:T(8,128)(2,1)S(1)}, u32[]{:S(2)}, u32[]{:S(2)}) collective-permute-start(bf16[384,640]{1,0:T(8,128)(2,1)S(1)} %get-tuple-element.23.send_ref), channel_id=1, source_target_pairs={{0,1},{1,0},{2,3},{3,2},{4,5},{5,4},{6,7},{7,6},{8,9},{9,8},{10,11... | collective-permute-start | bytes 1474568 | tf_op jit(solution)/shard_map/ppermute | solution.py:287
  65.3 30.6 %copy-start.3 = (bf16[384,1280]{1,0:T(8,128)(2,1)}, bf16[384,1280]{1,0:T(8,128)(2,1)S(1)}, u32[]{:S(2)}) copy-start(bf16[384,1280]{1,0:T(8,128)(2,1)S(1)} %whole_grad.1) | copy-start | bytes 2949124
  140.8 12.6 %all-to-all-start.4 = ((f32[32,1,256]{2,1,0:T(1,128)}), f32[32,1,256]{2,1,0:T(1,128)S(1)}, u32[]{:S(2)}, u32[]{:S(2)}) async-start(f32[32,1,256]{2,1,0:T(1,128)} %get-tuple-element.29), calls=%async_computation.4 | async-start | bytes 65536 | tf_op jit(solution)/shard_map/all_to_all | solution.py:41

commit v6 on v5

--- a/solution.py
+++ b/solution.py
@@ -1,4 +1,5 @@
 import functools
+import itertools
 
 import jax
 import jax.numpy as jnp
@@ -8,10 +9,9 @@
 from jax.sharding import Mesh
 from jax.sharding import PartitionSpec as P
 
-DP = ("dp_0", "dp_1", "dp_2")
-FIRST = ("dp_0", "dp_2")
-SECOND = ("dp_1", "z")
+DP = ("x", "y")
 SEQ = ("z", "core")
+ALL = (*DP, *SEQ)
 LANES = 128
 
 epsilon = 1e-06
@@ -37,8 +37,40 @@
     )(*ins)
 
 
-def exchange(blocks, axes):
-    return lax.all_to_all(blocks, axes, 0, 0, tiled=True)
+def exchange(blocks, axes, groups=None):
+    return lax.all_to_all(blocks, axes, 0, 0, axis_index_groups=groups, tiled=True)
+
+
+class Cells:
+    def __init__(self, counts, core):
+        x, y, z = self.counts = counts
+        self.core = core
+        self.near = list(itertools.product(range(2), repeat=3))
+        self.far = list(itertools.product(range(x // 2), range(y // 2), range(z // 2)))
+        self.far_xy = list(itertools.product(range(x // 2), range(y // 2)))
+
+    def chip(self, far, near):
+        return tuple((2 * f + n + self.core) % c for f, n, c in zip(far, near, self.counts))
+
+    def device(self, far, near):
+        x, y, z = self.chip(far, near)
+        return ((x * self.counts[1] + y) * self.counts[2] + z) * 2 + self.core
+
+    def inside(self):
+        return [[self.device(far, near) for near in self.near] for far in self.far]
+
+    def across(self):
+        return [[self.device(far, near) for far in self.far] for near in self.near]
+
+    def replicas(self, near):
+        chips = [self.chip((*far, 0), near) for far in self.far_xy]
+        return [x * self.counts[1] + y for x, y, _ in chips]
+
+    def order(self):
+        return [n * 2 + near[2] for near in self.near for n in self.replicas(near)]
+
+    def gain_rows(self, chunks):
+        return [[n if near[2] == 0 and n < chunks else None for n in self.replicas(near)] for near in self.near]
 
 
 def iota(shape, dim):
@@ -70,7 +102,14 @@
         copy.wait()
 
 
-def prepare_kernel(step, xact_ref, acts_ref, pair_ref, lines_ref, inverse_ref, left_ref, left_pair_ref):
+def in_order(target, lane, turned, order):
+    size = turned.shape[0] // len(order)
+    for place, first in enumerate(order):
+        rows = turned[first * size:(first + 1) * size]
+        target[place * size:(place + 1) * size, lane:lane + turned.shape[1]] = rows
+
+
+def prepare_kernel(step, orders, core_ref, xact_ref, acts_ref, pair_ref, lines_ref, inverse_ref, left_ref, left_pair_ref):
     slots, patches, features = xact_ref.shape
     height = step * patches
     for n in range(slots // step):
@@ -83,18 +122,22 @@
         width = LANES
         for n in range(slots * patches // width):
             block = source[n * width // patches:(n + 1) * width // patches].reshape(width, features)
-            target[:, n * width:(n + 1) * width] = block.T
+            turned = block.T
+            for core, order in enumerate(orders):
+                pl.when(core_ref[0] == core)(functools.partial(in_order, target, n * width, turned, order))
 
 
 def norm_kernel(
-    chunks, step, core_ref, recv_ref, lines_ref, left_ref, left_pair_ref, inverse_ref, gamma_ref,
-    keep_ref, send_ref, left_out_ref, left_pair_out_ref, gain_ref, hold_ref, values_ref, sems, left_sems,
+    chunks, step, core_ref, recv_ref, lines_ref, left_ref, left_pair_ref, far_ref, gamma_ref,
+    keep_ref, send_ref, left_out_ref, left_pair_out_ref, gain_ref, hold_ref, values_ref, inverse_ref, sems, left_sems,
 ):
     rows, features = recv_ref.shape
     half = features // 2
     height = rows // chunks
     first = core_ref[0] == 0
     gamma = gamma_ref[...]
+    scales = pltpu.make_async_copy(far_ref, inverse_ref, left_sems.at[2])
+    scales.start()
     incoming = []
     for n in range(chunks):
         at = pl.ds(n * height, height)
@@ -126,10 +169,11 @@
         return gain
 
     gain = jnp.zeros((8, features), f32)
+    scales.wait()
     for n in range(chunks):
         for copy in incoming[n]:
             copy.wait()
-        gain = lax.fori_loop(n * height // step, (n + 1) * height // step, body, gain, unroll=2)
+        gain = lax.fori_loop(n * height // step, (n + 1) * height // step, body, gain, unroll=3)
     gain_ref[...] = jnp.sum(gain, axis=0, keepdims=True)
     for copy in lefts:
         copy.wait()
@@ -143,44 +187,43 @@
     grad_ref[:, half:] = jnp.where(first, send, keep)
 
 
-def weight_kernel(shape, left_ref, left_pair_ref, right_ref, right_pair_ref, gain_ref, out_ref):
-    outer, middle, inner = shape
-    rows = (out_ref.shape[1] - 8) // middle
-    width = out_ref.shape[2]
+def gain_tiles(gain_rows, gain, out_ref):
+    rows = out_ref.shape[1] - 8
+    for b, numbers in enumerate(gain_rows):
+        if any(n is not None for n in numbers):
+            lines = [
+                jnp.zeros((1, LANES), f32) if n is None else gain[:, n * LANES:(n + 1) * LANES] for n in numbers
+            ]
+            lines += [jnp.zeros((1, LANES), f32)] * (8 - len(lines))
+            out_ref[b, rows:, :LANES] = jnp.concatenate(lines, axis=0).astype(bf16)
+
+
+def weight_kernel(gain_rows, core_ref, left_ref, left_pair_ref, right_ref, right_pair_ref, gain_ref, out_ref):
+    blocks, height, width = out_ref.shape
+    rows = height - 8
     gain = gain_ref[...]
-    chunks = gain.shape[1] // LANES
-    for b in range(outer):
-        at = slice(b * middle * inner * rows, (b + 1) * middle * inner * rows)
-        block = (
+    for b in range(blocks):
+        at = slice(b * rows, (b + 1) * rows)
+        out_ref[b, :rows, :] = (
             jnp.dot(left_ref[at, :], right_ref[...], preferred_element_type=f32)
             + jnp.dot(left_pair_ref[at, :], right_pair_ref[...], preferred_element_type=f32)
         ).astype(bf16)
-        for i in range(inner):
-            lines = []
-            for m in range(middle):
-                own = m * inner + i
-                out_ref[b * inner + i, m * rows:(m + 1) * rows, :] = block[own * rows:(own + 1) * rows, :]
-                n = b * middle * inner + own
-                if n < chunks:
-                    lines.append(gain[:, n * LANES:(n + 1) * LANES])
-            out_ref[b * inner + i, middle * rows:, :] = jnp.zeros((8, width), bf16)
-            if lines:
-                lines += [jnp.zeros((1, LANES), f32)] * (8 - len(lines))
-                out_ref[b * inner + i, middle * rows:, :LANES] = jnp.concatenate(lines, axis=0).astype(bf16)
+        out_ref[b, rows:, :] = jnp.zeros((8, width), bf16)
+    for core, numbers in enumerate(gain_rows):
+        pl.when(core_ref[0] == core)(functools.partial(gain_tiles, numbers, gain, out_ref))
 
 
 def first_sum_kernel(middle, in_ref, out_ref):
     pieces, height, width = out_ref.shape
     pieces //= middle
     rows = (in_ref.shape[1] - 8) // middle
-    lines = in_ref[:, middle * rows:, :].astype(f32).sum(0)
+    total = in_ref[...].astype(f32).sum(0)
     for m in range(middle):
-        total = in_ref[:, m * rows:(m + 1) * rows, :].astype(f32).sum(0)
         for p in range(pieces):
             if p * height < rows:
-                piece = total[p * height:(p + 1) * height, :]
+                piece = total[m * rows + p * height:m * rows + (p + 1) * height, :]
             elif p * height == rows:
-                piece = jnp.where(iota((height, width), 0) == 0, lines[m:m + 1, :], 0.0)
+                piece = jnp.where(iota((height, width), 0) == 0, total[middle * rows + m:middle * rows + m + 1, :], 0.0)
             else:
                 piece = jnp.zeros((height, width), f32)
             out_ref[m * pieces + p] = piece.astype(bf16)
@@ -195,16 +238,19 @@
 
 def joined_kernel(in_ref, weight_ref, note_ref):
     pieces, height, half = in_ref.shape
-    rows = weight_ref.shape[0]
+    part = weight_ref.shape[0] // 2
     squares = jnp.zeros((height, half), f32)
+    gain = jnp.zeros((1, LANES), f32)
     for p in range(pieces):
-        at = (p // 2) * height
-        if at < rows:
-            block = in_ref[p].astype(f32)
+        core = p % 2
+        far, near = divmod((p // 2 - core) % (pieces // 2), 2)
+        block = in_ref[p].astype(f32)
+        if far * height < part:
+            at = near * part + far * height
             squares += block * block
-            weight_ref[at:at + height, (p % 2) * half:(p % 2 + 1) * half] = block
-    p = 2 * (rows // height)
-    gain = (in_ref[p].astype(f32) + in_ref[p + 1].astype(f32))[:1, :LANES]
+            weight_ref[at:at + height, core * half:(core + 1) * half] = block
+        elif near == 0:
+            gain += block[:1, :LANES]
     line = jnp.concatenate([gain, jnp.full((1, LANES), jnp.sum(squares), f32)], axis=1)
     for d in range(note_ref.shape[0]):
         note_ref[d] = line
@@ -225,7 +271,10 @@
 
 def on_device(grad_rows, row_owner, acts, xact, gamma, w_out):
     seq_count = lax.axis_size(SEQ)
-    outer, middle, inner, z_count = (lax.axis_size(a) for a in (*DP, "z"))
+    counts = tuple(lax.axis_size(a) for a in (*DP, SEQ[0]))
+    cells = [Cells(counts, core) for core in range(2)]
+    inside = [group for c in cells for group in c.inside()]
+    across = [group for c in cells for group in c.across()]
     tokens = row_owner.shape[1]
     slot_count, patches, features = acts.shape[2:]
     capacity = slot_count // seq_count
@@ -252,7 +301,7 @@
     act_slots = acts.reshape(slot_count, patches, features)
     act_pair = lax.ppermute(act_slots, "core", swap)
     lines, inverse, left, left_pair = call(
-        functools.partial(prepare_kernel, 8),
+        functools.partial(prepare_kernel, 8, [c.order() for c in cells]),
         "prepare",
         (
             shaped(bf16, rows, features),
@@ -260,10 +309,10 @@
             shaped(bf16, features, rows),
             shaped(bf16, features, rows),
         ),
-        (xact.reshape(slot_count, patches, features), act_slots, act_pair),
-    )
-
-    chunks = 4
+        (core, xact.reshape(slot_count, patches, features), act_slots, act_pair),
+    )
+
+    chunks = 8
     grad_keep, grad_send, left, left_pair, gain_part = call(
         functools.partial(norm_kernel, chunks, 16),
         "norm_backward",
@@ -275,13 +324,14 @@
             shaped(f32, 1, features),
         ),
         (core, received.reshape(rows, features), lines, left, left_pair, inverse, gamma.reshape(1, features)),
-        far_in=(1, 2, 3, 4),
+        far_in=(1, 2, 3, 4, 5),
         limit=50,
         scratch=[
             pltpu.VMEM((rows, features), bf16),
             pltpu.VMEM((rows, features), bf16),
+            pltpu.VMEM((rows, 1), f32),
             pltpu.SemaphoreType.DMA((2 * chunks,)),
-            pltpu.SemaphoreType.DMA((2,)),
+            pltpu.SemaphoreType.DMA((3,)),
         ],
     )
     grad_pair = lax.ppermute(grad_send, "core", swap)
@@ -290,31 +340,32 @@
     )
     grad, grad_keep = lax.optimization_barrier((grad, grad_keep))
 
-    out_rows = features // (outer * middle * inner)
-    z_rows = (out_rows + 8) // z_count
+    replicas = counts[0] * counts[1]
+    out_rows = features // replicas
+    z_rows = out_rows // 2 // (counts[2] // 2 - 1)
     (weight_pair,) = call(
-        functools.partial(weight_kernel, (outer, middle, inner)),
+        functools.partial(weight_kernel, [c.gain_rows(features // LANES) for c in cells]),
         "weight_pair",
-        (shaped(bf16, outer * inner, middle * out_rows + 8, half),),
-        (left, left_pair, grad_keep, grad_pair, gain_part),
+        (shaped(bf16, 8, features // 8 + 8, half),),
+        (core, left, left_pair, grad_keep, grad_pair, gain_part),
         flops=4 * features * half * rows,
     )
     (weight_some,) = call(
-        functools.partial(first_sum_kernel, middle),
+        functools.partial(first_sum_kernel, replicas // 4),
         "sum_first",
-        (shaped(bf16, middle * z_count, z_rows, half),),
-        (exchange(weight_pair, FIRST),),
+        (shaped(bf16, replicas // 4 * counts[2] // 2, z_rows, half),),
+        (exchange(weight_pair, ALL, inside),),
     )
     (pieces,) = call(
         second_sum_kernel,
         "sum_second",
         (shaped(bf16, seq_count, z_rows, half),),
-        (exchange(weight_some, SECOND),),
+        (exchange(weight_some, ALL, across),),
     )
     weight_sum, note = call(
         joined_kernel,
         "joined",
-        (shaped(f32, out_rows, features), shaped(f32, outer * middle * inner, 1, 2 * LANES)),
+        (shaped(f32, out_rows, features), shaped(f32, replicas, 1, 2 * LANES)),
         (exchange(pieces, SEQ),),
     )
     attn_grad = lax.dot_general(
@@ -330,7 +381,7 @@
 
 
 def solution(mesh):
-    finer = Mesh(mesh.devices.reshape(4, 4, 2, mesh.shape["seq"] // 2, 2), (*DP, *SEQ))
+    finer = Mesh(mesh.devices.reshape(4, 8, mesh.shape["seq"] // 2, 2), ALL)
     placed = (
         P(DP, SEQ, None, None),
         P(DP, SEQ, None),

time: 155 us -> 150 us (0.968)
  blocking collectives: 70.9 us -> 65.9 us
    all_to_all x3, blocking collectives: 70.9 us -> 65.9 us  [exchange(): lax.all_to_all(blocks, axes, 0, 0, axis_index_groups=groups, tiled=True)]
  transfers between devices with their start and end apart: 4 -> 4, of which waited for: 4 -> 4; matrix products, arithmetic and copies ran while one was open for 4% -> 4% of each run, Pallas kernels for 1% -> 2%
where the time goes in v6:
time: 150 us
  blocking collectives  65.9 us (44%)
  waiting for transfers between devices  30.4 us (20%)
  starting transfers between devices  28 us (19%)
  Pallas kernels  13.1 us (9%)
  local copies, waits for them, and re-layouts  7.92 us (5%)
  matrix products  3.63 us (2%)
    all_to_all x3, blocking collectives, exchange(): lax.all_to_all(blocks, axes, 0, 0, axis_index_groups=groups, tiled=True)  65.9 us
    all_to_all x2, waiting for transfers between devices, exchange(): lax.all_to_all(blocks, axes, 0, 0, axis_index_groups=groups, tiled=True)  26.4 us
    all_to_all x2, starting transfers between devices, exchange(): lax.all_to_all(blocks, axes, 0, 0, axis_index_groups=groups, tiled=True)  21.3 us
    pallas_call x9, Pallas kernels, call(): pl.pallas_call(kernel, name=name, out_shape=outs, in_specs=specs, out_spe...  13.1 us
    unnamed x16, local copies, waits for them, and re-layouts  5.33 us
    ppermute x1, starting transfers between devices, on_device(): grad_pair = lax.ppermute(grad_send, 'core', swap)  4.56 us
    dot_general x1, matrix products, on_device(): lax.dot_general(grad, w_out, (((1,), (1,)), ((), ())), preferred_element_...  3.63 us
  transfers between devices with their start and end apart: 4, of which 4 were waited for; matrix products, arithmetic and copies ran while one was open for 4% of the time, Pallas kernels for 2%

profile of v6, /device:TPU:1, one launch (start us, length us, event | category | flops | bytes accessed | tf_op | source)
XLA Modules:
  0.0 149.7 jit_solution(5864149838494330211)
XLA Ops:
  0.6 0.0 copy-start
  0.6 0.0 copy-start.7
  0.7 3.0 %gather_rows.1 = bf16[384,1280]{1,0:T(8,128)(2,1)} custom-call(s32[1,80]{1,0:T(1,128)} %bitcast.14, bf16[80,4,1280]{2,1,0:T(4,128)(2,1)} %bitcast.13), custom_call_target="tpu_custom_call" | custom-call | flops 1000000 | bytes 1802560 | tf_op jit(solution)/shard_map/gather_rows/pallas_call | solution.py:28
  3.6 16.7 %all-to-all-start = ((bf16[24,16,1280]{2,1,0:T(8,128)(2,1)}), bf16[24,16,1280]{2,1,0:T(8,128)(2,1)}, u32[]{:S(2)}, u32[]{:S(2)}) async-start(bf16[24,16,1280]{2,1,0:T(8,128)(2,1)} %bitcast.12), calls=%async_computation | async-start | bytes 1966080 | tf_op jit(solution)/shard_map/all_to_all | solution.py:41
  20.4 2.2 %collective-permute-start = (bf16[96,4,1280]{2,1,0:T(4,128)(2,1)}, bf16[96,4,1280]{2,1,0:T(4,128)(2,1)}, u32[]{:S(2)}, u32[]{:S(2)}) collective-permute-start(bf16[96,4,1280]{2,1,0:T(4,128)(2,1)} %bitcast.10), channel_id=1, source_target_pairs={{0,1},{1,0},{2,3},{3,2},{4,5},{5,4},{6,7},{7,6},{8,9},{9,8},{10,11... | collective-permute-start | bytes 2949128 | tf_op jit(solution)/shard_map/ppermute | solution.py:302
  22.5 0.0 copy-done.7
  22.6 2.6 %collective-permute-done.pair_ref = bf16[96,4,1280]{2,1,0:T(4,128)(2,1)} collective-permute-done((bf16[96,4,1280]{2,1,0:T(4,128)(2,1)}, bf16[96,4,1280]{2,1,0:T(4,128)(2,1)}, u32[]{:S(2)}, u32[]{:S(2)}) %collective-permute-start) | collective-permute-done | bytes 983072 | tf_op jit(solution)/shard_map/ppermute | solution.py:302
  25.2 0.0 copy-start.1
  25.2 1.2 copy-done.1
  26.4 0.0 copy-start.2
  26.4 1.2 copy-done.2
  27.6 2.7 %prepare.1 = (bf16[384,1280]{1,0:T(8,128)(2,1)S(1)}, f32[384,1]{1,0:T(8,128)S(1)}, bf16[1280,384]{1,0:T(8,128)(2,1)S(1)}, bf16[1280,384]{1,0:T(8,128)(2,1)S(1)}) custom-call(s32[1]{0:T(128)} %bitcast.core_ref, bf16[96,4,1280]{2,1,0:T(4,128)(2,1)S(1)} %bitcast.9, bf16[96,4,1280]{2,1,0:T(4,128)(2,1)S(1)} %bitcast.11, ...), custom_call_target="tpu_custom_call" | custom-call | flops 1000000 | bytes 5899780 | tf_op jit(solution)/shard_map/prepare/pallas_call | solution.py:28
  30.3 0.0 copy-start.4
  30.3 1.0 copy-done.4
  31.3 0.0 copy-start.5
  31.3 1.0 copy-done.5
  32.3 0.0 copy-start.6
  32.3 1.0 copy-done.6
  33.2 23.9 %all-to-all-done = bf16[24,16,1280]{2,1,0:T(8,128)(2,1)} async-done(((bf16[24,16,1280]{2,1,0:T(8,128)(2,1)}), bf16[24,16,1280]{2,1,0:T(8,128)(2,1)}, u32[]{:S(2)}, u32[]{:S(2)}) %all-to-all-start) | async-done | bytes 983072 | tf_op jit(solution)/shard_map/all_to_all | solution.py:41
  57.1 3.0 %norm_backward.1 = (bf16[384,640]{1,0:T(8,128)(2,1)S(1)}, bf16[384,640]{1,0:T(8,128)(2,1)S(1)}, bf16[1280,384]{1,0:T(8,128)(2,1)S(1)}, bf16[1280,384]{1,0:T(8,128)(2,1)S(1)}, f32[1,1280]{1,0:T(1,128)S(1)}) custom-call(s32[1]{0:T(128)} %bitcast.core_ref, bf16[384,1280]{1,0:T(8,128)(2,1)} %bitcast.4.recv_ref, bf16[384,1280]{1,0:T(8,128)(2,1)} %copy-done.4, ...), custom_call_target="tpu_custom_call" | custom-call | flops 1000000 | bytes 6893060 | tf_op jit(solution)/shard_map/norm_backward/pallas_call | solution.py:28
  60.1 4.6 %collective-permute-start.1 = (bf16[384,640]{1,0:T(8,128)(2,1)S(1)}, bf16[384,640]{1,0:T(8,128)(2,1)S(1)}, u32[]{:S(2)}, u32[]{:S(2)}) collective-permute-start(bf16[384,640]{1,0:T(8,128)(2,1)S(1)} %get-tuple-element.23.send_ref), channel_id=1, source_target_pairs={{0,1},{1,0},{2,3},{3,2},{4,5},{5,4},{6,7},{7,6},{8,9},{9,8},{10,11... | collective-permute-start | bytes 1474568 | tf_op jit(solution)/shard_map/ppermute | solution.py:337
  64.7 0.1 whole_grad.1
  64.8 0.0 copy-start.3
  64.8 1.4 collective-permute-done.1.right_pair_ref
  66.2 2.2 %weight_pair.1 = bf16[8,168,640]{2,1,0:T(8,128)(2,1)S(1)} custom-call(s32[1]{0:T(128)} %bitcast.core_ref, bf16[1280,384]{1,0:T(8,128)(2,1)S(1)} %get-tuple-element.25.left_ref, bf16[1280,384]{1,0:T(8,128)(2,1)S(1)} %get-tuple-element.26.left_pair_ref, bf16[384,640]{1,0:T(8,128)(2,1)S(1)} %get-tuple-element.27.keep_ref.right_ref, ...), custom_call_target="tpu_custom_call" | custom-call | flops 1258291200 | bytes 4674564 | tf_op jit(solution)/shard_map/weight_pair/pallas_call | solution.py:28
  68.4 20.0 %all_to_all.25.in_ref = bf16[8,168,640]{2,1,0:T(8,128)(2,1)S(1)} all-to-all(bf16[8,168,640]{2,1,0:T(8,128)(2,1)S(1)} %weight_pair.1), channel_id=1, replica_groups={{0,2,24,26,192,194,216,218},{4,6,28,30,196,198,220,222},{8,10,32,34,200..., dimensions={0} | all-to-all | bytes 3440640 | tf_op jit(solution)/shard_map/all_to_all | solution.py:41
  88.4 0.0 copy-done.3
  88.4 0.3 sum_first.1
  88.6 24.8 %all_to_all.26.in_ref = bf16[48,4,640]{2,1,0:T(4,128)(2,1)S(1)} all-to-all(bf16[48,4,640]{2,1,0:T(4,128)(2,1)S(1)} %sum_first.1), channel_id=1, replica_groups={{0,4,8,12,16,20,48,52,56,60,64,68,96,100,104,108,112,116,144,148,152,15..., dimensions={0} | all-to-all | bytes 491520 | tf_op jit(solution)/shard_map/all_to_all | solution.py:41
  113.4 0.1 sum_second.1
  113.6 21.1 %all_to_all.27.in_ref = bf16[24,4,640]{2,1,0:T(4,128)(2,1)S(1)} all-to-all(bf16[24,4,640]{2,1,0:T(4,128)(2,1)S(1)} %sum_second.1), channel_id=1, replica_groups=mesh['x'=4,'y'=8,'z'=12,'core'=2] {'z','core'}, dimensions={0} | all-to-all | bytes 245760 | tf_op jit(solution)/shard_map/all_to_all | solution.py:41
  134.7 0.8 joined.1
  135.4 4.6 %all-to-all-start.4 = ((f32[32,1,256]{2,1,0:T(1,128)}), f32[32,1,256]{2,1,0:T(1,128)S(1)}, u32[]{:S(2)}, u32[]{:S(2)}) async-start(f32[32,1,256]{2,1,0:T(1,128)} %get-tuple-element.29), calls=%async_computation.4 | async-start | bytes 65536 | tf_op jit(solution)/shard_map/all_to_all | solution.py:41
  140.0 0.0 copy-done
  140.0 3.6 %convolution_convert_fusion = bf16[384,1280]{1,0:T(8,128)(2,1)} fusion(bf16[384,1280]{1,0:T(8,128)(2,1)} %copy-done.3, bf16[1280,1280]{1,0:T(8,128)(2,1)S(1)} %copy-done), kind=kOutput, calls=%fused_computation | convolution fusion | flops 1258782720 | bytes 5242880 | tf_op jit(solution)/shard_map/dot_general | solution.py:371
  143.7 2.6 %reshape.41 = bf16[1,1,96,4,1280]{4,3,2,1,0:T(4,128)(2,1)} reshape(bf16[384,1280]{1,0:T(8,128)(2,1)} %convolution_convert_fusion) | data formatting | bytes 1966080 | tf_op jit(solution)/shard_map/reshape | solution.py:373
  146.2 2.5 %all-to-all-done.4.note_ref = f32[32,1,256]{2,1,0:T(1,128)S(1)} async-done(((f32[32,1,256]{2,1,0:T(1,128)}), f32[32,1,256]{2,1,0:T(1,128)S(1)}, u32[]{:S(2)}, u32[]{:S(2)}) %all-to-all-start.4) | async-done | bytes 32800 | tf_op jit(solution)/shard_map/all_to_all | solution.py:41
  148.8 0.9 scaled.1
  (1 shorter events, 0.0 us)
Async XLA Ops:
  0.6 139.4 %copy-start = (bf16[1280,1280]{1,0:T(8,128)(2,1)S(1)}, bf16[1280,1280]{1,0:T(8,128)(2,1)}, u32[]{:S(2)}) copy-start(bf16[1280,1280]{1,0:T(8,128)(2,1)} %param.11) | copy-start | bytes 9830404
  0.6 21.9 %copy-start.7 = (f32[1280]{0:T(1024)S(1)}, f32[1280]{0:T(1024)}, u32[]{:S(2)}) copy-start(f32[1280]{0:T(1024)} %param.10) | copy-start | bytes 15364
  3.6 53.5 %all-to-all-start = ((bf16[24,16,1280]{2,1,0:T(8,128)(2,1)}), bf16[24,16,1280]{2,1,0:T(8,128)(2,1)}, u32[]{:S(2)}, u32[]{:S(2)}) async-start(bf16[24,16,1280]{2,1,0:T(8,128)(2,1)} %bitcast.12), calls=%async_computation | async-start | bytes 1966080 | tf_op jit(solution)/shard_map/all_to_all | solution.py:41
  20.4 4.8 %collective-permute-start = (bf16[96,4,1280]{2,1,0:T(4,128)(2,1)}, bf16[96,4,1280]{2,1,0:T(4,128)(2,1)}, u32[]{:S(2)}, u32[]{:S(2)}) collective-permute-start(bf16[96,4,1280]{2,1,0:T(4,128)(2,1)} %bitcast.10), channel_id=1, source_target_pairs={{0,1},{1,0},{2,3},{3,2},{4,5},{5,4},{6,7},{7,6},{8,9},{9,8},{10,11... | collective-permute-start | bytes 2949128 | tf_op jit(solution)/shard_map/ppermute | solution.py:302
  25.2 1.2 copy-start.1
  26.4 1.2 copy-start.2
  30.3 1.0 copy-start.4
  31.3 1.0 copy-start.5
  32.3 1.0 copy-start.6
  60.1 6.0 %collective-permute-start.1 = (bf16[384,640]{1,0:T(8,128)(2,1)S(1)}, bf16[384,640]{1,0:T(8,128)(2,1)S(1)}, u32[]{:S(2)}, u32[]{:S(2)}) collective-permute-start(bf16[384,640]{1,0:T(8,128)(2,1)S(1)} %get-tuple-element.23.send_ref), channel_id=1, source_target_pairs={{0,1},{1,0},{2,3},{3,2},{4,5},{5,4},{6,7},{7,6},{8,9},{9,8},{10,11... | collective-permute-start | bytes 1474568 | tf_op jit(solution)/shard_map/ppermute | solution.py:337
  64.8 23.6 %copy-start.3 = (bf16[384,1280]{1,0:T(8,128)(2,1)}, bf16[384,1280]{1,0:T(8,128)(2,1)S(1)}, u32[]{:S(2)}) copy-start(bf16[384,1280]{1,0:T(8,128)(2,1)S(1)} %whole_grad.1) | copy-start | bytes 2949124
  135.4 13.3 %all-to-all-start.4 = ((f32[32,1,256]{2,1,0:T(1,128)}), f32[32,1,256]{2,1,0:T(1,128)S(1)}, u32[]{:S(2)}, u32[]{:S(2)}) async-start(f32[32,1,256]{2,1,0:T(1,128)} %get-tuple-element.29), calls=%async_computation.4 | async-start | bytes 65536 | tf_op jit(solution)/shard_map/all_to_all | solution.py:41

commit v7 on v6

--- a/solution.py
+++ b/solution.py
@@ -198,14 +198,18 @@
             out_ref[b, rows:, :LANES] = jnp.concatenate(lines, axis=0).astype(bf16)
 
 
-def weight_kernel(gain_rows, core_ref, left_ref, left_pair_ref, right_ref, right_pair_ref, gain_ref, out_ref):
+def own_kernel(left_ref, right_ref, out_ref):
+    out_ref[...] = jnp.dot(left_ref[...], right_ref[...], preferred_element_type=f32)
+
+
+def weight_kernel(gain_rows, core_ref, own_ref, left_pair_ref, right_pair_ref, gain_ref, out_ref):
     blocks, height, width = out_ref.shape
     rows = height - 8
     gain = gain_ref[...]
     for b in range(blocks):
         at = slice(b * rows, (b + 1) * rows)
         out_ref[b, :rows, :] = (
-            jnp.dot(left_ref[at, :], right_ref[...], preferred_element_type=f32)
+            own_ref[at, :]
             + jnp.dot(left_pair_ref[at, :], right_pair_ref[...], preferred_element_type=f32)
         ).astype(bf16)
         out_ref[b, rows:, :] = jnp.zeros((8, width), bf16)
@@ -338,7 +342,8 @@
     (grad,) = call(
         whole_kernel, "whole_grad", (shaped(bf16, rows, features),), (core, grad_keep, grad_send), limit=52
     )
-    grad, grad_keep = lax.optimization_barrier((grad, grad_keep))
+    (own,) = call(own_kernel, "weight_own", (shaped(f32, features, half),), (left, grad_keep), flops=2 * features * half * rows, limit=20)
+    grad, own = lax.optimization_barrier((grad, own))
 
     replicas = counts[0] * counts[1]
     out_rows = features // replicas
@@ -347,7 +352,7 @@
         functools.partial(weight_kernel, [c.gain_rows(features // LANES) for c in cells]),
         "weight_pair",
         (shaped(bf16, 8, features // 8 + 8, half),),
-        (core, left, left_pair, grad_keep, grad_pair, gain_part),
+        (core, own, left_pair, grad_pair, gain_part),
         flops=4 * features * half * rows,
     )
     (weight_some,) = call(

time: 150 us -> 149 us (level)
    pallas_call x9 -> x10, Pallas kernels: 13.1 us -> 13.3 us  [call(): pl.pallas_call(kernel, name=name, out_shape=outs, in_specs=specs, out_spe...]
  transfers between devices with their start and end apart: 4 -> 4, of which waited for: 4 -> 4; matrix products, arithmetic and copies ran while one was open for 4% -> 4% of each run, Pallas kernels for 2% -> 3%
where the time goes in v7:
time: 149 us
  blocking collectives  65.9 us (44%)
  waiting for transfers between devices  29.3 us (20%)
  starting transfers between devices  28 us (19%)
  Pallas kernels  13.3 us (9%)
  local copies, waits for them, and re-layouts  7.92 us (5%)
  matrix products  3.63 us (2%)
    all_to_all x3, blocking collectives, exchange(): lax.all_to_all(blocks, axes, 0, 0, axis_index_groups=groups, tiled=True)  65.9 us
    all_to_all x2, waiting for transfers between devices, exchange(): lax.all_to_all(blocks, axes, 0, 0, axis_index_groups=groups, tiled=True)  26.4 us
    all_to_all x2, starting transfers between devices, exchange(): lax.all_to_all(blocks, axes, 0, 0, axis_index_groups=groups, tiled=True)  21.3 us
    pallas_call x10, Pallas kernels, call(): pl.pallas_call(kernel, name=name, out_shape=outs, in_specs=specs, out_spe...  13.3 us
    unnamed x16, local copies, waits for them, and re-layouts  5.33 us
    ppermute x1, starting transfers between devices, on_device(): grad_pair = lax.ppermute(grad_send, 'core', swap)  4.56 us
    dot_general x1, matrix products, on_device(): lax.dot_general(grad, w_out, (((1,), (1,)), ((), ())), preferred_element_...  3.63 us
  transfers between devices with their start and end apart: 4, of which 4 were waited for; matrix products, arithmetic and copies ran while one was open for 4% of the time, Pallas kernels for 3%

profile of v7, /device:TPU:1, one launch (start us, length us, event | category | flops | bytes accessed | tf_op | source)
XLA Modules:
  0.0 148.8 jit_solution(6313765321962841915)
XLA Ops:
  0.6 0.0 copy-start
  0.6 0.0 copy-start.7
  0.7 3.0 %gather_rows.1 = bf16[384,1280]{1,0:T(8,128)(2,1)} custom-call(s32[1,80]{1,0:T(1,128)} %bitcast.14, bf16[80,4,1280]{2,1,0:T(4,128)(2,1)} %bitcast.13), custom_call_target="tpu_custom_call" | custom-call | flops 1000000 | bytes 1802560 | tf_op jit(solution)/shard_map/gather_rows/pallas_call | solution.py:28
  3.6 16.7 %all-to-all-start = ((bf16[24,16,1280]{2,1,0:T(8,128)(2,1)}), bf16[24,16,1280]{2,1,0:T(8,128)(2,1)}, u32[]{:S(2)}, u32[]{:S(2)}) async-start(bf16[24,16,1280]{2,1,0:T(8,128)(2,1)} %bitcast.12), calls=%async_computation | async-start | bytes 1966080 | tf_op jit(solution)/shard_map/all_to_all | solution.py:41
  20.4 2.2 %collective-permute-start = (bf16[96,4,1280]{2,1,0:T(4,128)(2,1)}, bf16[96,4,1280]{2,1,0:T(4,128)(2,1)}, u32[]{:S(2)}, u32[]{:S(2)}) collective-permute-start(bf16[96,4,1280]{2,1,0:T(4,128)(2,1)} %bitcast.10), channel_id=1, source_target_pairs={{0,1},{1,0},{2,3},{3,2},{4,5},{5,4},{6,7},{7,6},{8,9},{9,8},{10,11... | collective-permute-start | bytes 2949128 | tf_op jit(solution)/shard_map/ppermute | solution.py:306
  22.5 0.0 copy-done.7
  22.6 2.6 %collective-permute-done.pair_ref = bf16[96,4,1280]{2,1,0:T(4,128)(2,1)} collective-permute-done((bf16[96,4,1280]{2,1,0:T(4,128)(2,1)}, bf16[96,4,1280]{2,1,0:T(4,128)(2,1)}, u32[]{:S(2)}, u32[]{:S(2)}) %collective-permute-start) | collective-permute-done | bytes 983072 | tf_op jit(solution)/shard_map/ppermute | solution.py:306
  25.2 0.0 copy-start.1
  25.2 1.2 copy-done.1
  26.4 0.0 copy-start.2
  26.4 1.2 copy-done.2
  27.6 2.7 %prepare.1 = (bf16[384,1280]{1,0:T(8,128)(2,1)S(1)}, f32[384,1]{1,0:T(8,128)S(1)}, bf16[1280,384]{1,0:T(8,128)(2,1)S(1)}, bf16[1280,384]{1,0:T(8,128)(2,1)S(1)}) custom-call(s32[1]{0:T(128)} %bitcast.core_ref, bf16[96,4,1280]{2,1,0:T(4,128)(2,1)S(1)} %bitcast.9, bf16[96,4,1280]{2,1,0:T(4,128)(2,1)S(1)} %bitcast.11, ...), custom_call_target="tpu_custom_call" | custom-call | flops 1000000 | bytes 5899780 | tf_op jit(solution)/shard_map/prepare/pallas_call | solution.py:28
  30.3 0.0 copy-start.4
  30.3 1.0 copy-done.4
  31.3 0.0 copy-start.5
  31.3 1.0 copy-done.5
  32.3 0.0 copy-start.6
  32.3 1.0 copy-done.6
  33.2 23.9 %all-to-all-done = bf16[24,16,1280]{2,1,0:T(8,128)(2,1)} async-done(((bf16[24,16,1280]{2,1,0:T(8,128)(2,1)}), bf16[24,16,1280]{2,1,0:T(8,128)(2,1)}, u32[]{:S(2)}, u32[]{:S(2)}) %all-to-all-start) | async-done | bytes 983072 | tf_op jit(solution)/shard_map/all_to_all | solution.py:41
  57.1 3.0 %norm_backward.1 = (bf16[384,640]{1,0:T(8,128)(2,1)S(1)}, bf16[384,640]{1,0:T(8,128)(2,1)S(1)}, bf16[1280,384]{1,0:T(8,128)(2,1)S(1)}, bf16[1280,384]{1,0:T(8,128)(2,1)S(1)}, f32[1,1280]{1,0:T(1,128)S(1)}) custom-call(s32[1]{0:T(128)} %bitcast.core_ref, bf16[384,1280]{1,0:T(8,128)(2,1)} %bitcast.4.recv_ref, bf16[384,1280]{1,0:T(8,128)(2,1)} %copy-done.4, ...), custom_call_target="tpu_custom_call" | custom-call | flops 1000000 | bytes 6893060 | tf_op jit(solution)/shard_map/norm_backward/pallas_call | solution.py:28
  60.1 4.6 %collective-permute-start.1 = (bf16[384,640]{1,0:T(8,128)(2,1)S(1)}, bf16[384,640]{1,0:T(8,128)(2,1)S(1)}, u32[]{:S(2)}, u32[]{:S(2)}) collective-permute-start(bf16[384,640]{1,0:T(8,128)(2,1)S(1)} %get-tuple-element.23.send_ref), channel_id=1, source_target_pairs={{0,1},{1,0},{2,3},{3,2},{4,5},{5,4},{6,7},{7,6},{8,9},{9,8},{10,11... | collective-permute-start | bytes 1474568 | tf_op jit(solution)/shard_map/ppermute | solution.py:341
  64.7 0.1 whole_grad.1
  64.8 0.0 copy-start.3
  64.8 1.1 weight_own.1.own_ref
  65.9 0.3 collective-permute-done.1.right_pair_ref
  66.2 1.3 weight_pair.1
  67.5 0.0 copy-done.3
  67.5 20.0 %all_to_all.25.in_ref = bf16[8,168,640]{2,1,0:T(8,128)(2,1)S(1)} all-to-all(bf16[8,168,640]{2,1,0:T(8,128)(2,1)S(1)} %weight_pair.1), channel_id=1, replica_groups={{0,2,24,26,192,194,216,218},{4,6,28,30,196,198,220,222},{8,10,32,34,200..., dimensions={0} | all-to-all | bytes 3440640 | tf_op jit(solution)/shard_map/all_to_all | solution.py:41
  87.5 0.3 sum_first.1
  87.8 24.8 %all_to_all.26.in_ref = bf16[48,4,640]{2,1,0:T(4,128)(2,1)S(1)} all-to-all(bf16[48,4,640]{2,1,0:T(4,128)(2,1)S(1)} %sum_first.1), channel_id=1, replica_groups={{0,4,8,12,16,20,48,52,56,60,64,68,96,100,104,108,112,116,144,148,152,15..., dimensions={0} | all-to-all | bytes 491520 | tf_op jit(solution)/shard_map/all_to_all | solution.py:41
  112.5 0.1 sum_second.1
  112.7 21.1 %all_to_all.27.in_ref = bf16[24,4,640]{2,1,0:T(4,128)(2,1)S(1)} all-to-all(bf16[24,4,640]{2,1,0:T(4,128)(2,1)S(1)} %sum_second.1), channel_id=1, replica_groups=mesh['x'=4,'y'=8,'z'=12,'core'=2] {'z','core'}, dimensions={0} | all-to-all | bytes 245760 | tf_op jit(solution)/shard_map/all_to_all | solution.py:41
  133.8 0.8 joined.1
  134.5 4.6 %all-to-all-start.4 = ((f32[32,1,256]{2,1,0:T(1,128)}), f32[32,1,256]{2,1,0:T(1,128)S(1)}, u32[]{:S(2)}, u32[]{:S(2)}) async-start(f32[32,1,256]{2,1,0:T(1,128)} %get-tuple-element.29), calls=%async_computation.4 | async-start | bytes 65536 | tf_op jit(solution)/shard_map/all_to_all | solution.py:41
  139.1 0.0 copy-done
  139.1 3.6 %convolution_convert_fusion = bf16[384,1280]{1,0:T(8,128)(2,1)} fusion(bf16[384,1280]{1,0:T(8,128)(2,1)} %copy-done.3, bf16[1280,1280]{1,0:T(8,128)(2,1)S(1)} %copy-done), kind=kOutput, calls=%fused_computation | convolution fusion | flops 1258782720 | bytes 5242880 | tf_op jit(solution)/shard_map/dot_general | solution.py:376
  142.8 2.6 %reshape.41 = bf16[1,1,96,4,1280]{4,3,2,1,0:T(4,128)(2,1)} reshape(bf16[384,1280]{1,0:T(8,128)(2,1)} %convolution_convert_fusion) | data formatting | bytes 1966080 | tf_op jit(solution)/shard_map/reshape | solution.py:378
  145.4 2.5 %all-to-all-done.4.note_ref = f32[32,1,256]{2,1,0:T(1,128)S(1)} async-done(((f32[32,1,256]{2,1,0:T(1,128)}), f32[32,1,256]{2,1,0:T(1,128)S(1)}, u32[]{:S(2)}, u32[]{:S(2)}) %all-to-all-start.4) | async-done | bytes 32800 | tf_op jit(solution)/shard_map/all_to_all | solution.py:41
  147.9 0.9 scaled.1
  (1 shorter events, 0.0 us)
Async XLA Ops:
  0.6 138.5 %copy-start = (bf16[1280,1280]{1,0:T(8,128)(2,1)S(1)}, bf16[1280,1280]{1,0:T(8,128)(2,1)}, u32[]{:S(2)}) copy-start(bf16[1280,1280]{1,0:T(8,128)(2,1)} %param.11) | copy-start | bytes 9830404
  0.6 21.9 %copy-start.7 = (f32[1280]{0:T(1024)S(1)}, f32[1280]{0:T(1024)}, u32[]{:S(2)}) copy-start(f32[1280]{0:T(1024)} %param.10) | copy-start | bytes 15364
  3.6 53.5 %all-to-all-start = ((bf16[24,16,1280]{2,1,0:T(8,128)(2,1)}), bf16[24,16,1280]{2,1,0:T(8,128)(2,1)}, u32[]{:S(2)}, u32[]{:S(2)}) async-start(bf16[24,16,1280]{2,1,0:T(8,128)(2,1)} %bitcast.12), calls=%async_computation | async-start | bytes 1966080 | tf_op jit(solution)/shard_map/all_to_all | solution.py:41
  20.4 4.8 %collective-permute-start = (bf16[96,4,1280]{2,1,0:T(4,128)(2,1)}, bf16[96,4,1280]{2,1,0:T(4,128)(2,1)}, u32[]{:S(2)}, u32[]{:S(2)}) collective-permute-start(bf16[96,4,1280]{2,1,0:T(4,128)(2,1)} %bitcast.10), channel_id=1, source_target_pairs={{0,1},{1,0},{2,3},{3,2},{4,5},{5,4},{6,7},{7,6},{8,9},{9,8},{10,11... | collective-permute-start | bytes 2949128 | tf_op jit(solution)/shard_map/ppermute | solution.py:306
  25.2 1.2 copy-start.1
  26.4 1.2 copy-start.2
  30.3 1.0 copy-start.4
  31.3 1.0 copy-start.5
  32.3 1.0 copy-start.6
  60.1 6.0 %collective-permute-start.1 = (bf16[384,640]{1,0:T(8,128)(2,1)S(1)}, bf16[384,640]{1,0:T(8,128)(2,1)S(1)}, u32[]{:S(2)}, u32[]{:S(2)}) collective-permute-start(bf16[384,640]{1,0:T(8,128)(2,1)S(1)} %get-tuple-element.23.send_ref), channel_id=1, source_target_pairs={{0,1},{1,0},{2,3},{3,2},{4,5},{5,4},{6,7},{7,6},{8,9},{9,8},{10,11... | collective-permute-start | bytes 1474568 | tf_op jit(solution)/shard_map/ppermute | solution.py:341
  64.8 2.7 %copy-start.3 = (bf16[384,1280]{1,0:T(8,128)(2,1)}, bf16[384,1280]{1,0:T(8,128)(2,1)S(1)}, u32[]{:S(2)}) copy-start(bf16[384,1280]{1,0:T(8,128)(2,1)S(1)} %whole_grad.1) | copy-start | bytes 2949124
  134.5 13.4 %all-to-all-start.4 = ((f32[32,1,256]{2,1,0:T(1,128)}), f32[32,1,256]{2,1,0:T(1,128)S(1)}, u32[]{:S(2)}, u32[]{:S(2)}) async-start(f32[32,1,256]{2,1,0:T(1,128)} %get-tuple-element.29), calls=%async_computation.4 | async-start | bytes 65536 | tf_op jit(solution)/shard_map/all_to_all | solution.py:41

commit v8 on v7

--- a/solution.py
+++ b/solution.py
@@ -32,7 +32,7 @@
         in_specs=specs,
         out_specs=tuple(FAR if n in far_out else VMEM for n in range(len(outs))),
         scratch_shapes=scratch,
-        compiler_params=pltpu.CompilerParams(vmem_limit_bytes=limit * 1024 * 1024),
+        compiler_params=pltpu.CompilerParams(vmem_limit_bytes=int(limit * 1024 * 1024)),
         cost_estimate=pl.CostEstimate(flops=max(flops, 1000000), bytes_accessed=moved, transcendentals=0),
     )(*ins)
 
@@ -128,15 +128,15 @@
 
 
 def norm_kernel(
-    chunks, step, core_ref, recv_ref, lines_ref, left_ref, left_pair_ref, far_ref, gamma_ref,
-    keep_ref, send_ref, left_out_ref, left_pair_out_ref, gain_ref, hold_ref, values_ref, inverse_ref, sems, left_sems,
+    chunks, step, core_ref, recv_ref, lines_ref, left_ref, far_ref, gamma_ref,
+    keep_ref, send_ref, left_out_ref, gain_ref, hold_ref, values_ref, inverse_ref, sems, left_sems,
 ):
     rows, features = recv_ref.shape
     half = features // 2
     height = rows // chunks
     first = core_ref[0] == 0
     gamma = gamma_ref[...]
-    scales = pltpu.make_async_copy(far_ref, inverse_ref, left_sems.at[2])
+    scales = pltpu.make_async_copy(far_ref, inverse_ref, left_sems.at[1])
     scales.start()
     incoming = []
     for n in range(chunks):
@@ -147,12 +147,8 @@
         ))
         for copy in incoming[-1]:
             copy.start()
-    lefts = (
-        pltpu.make_async_copy(left_ref, left_out_ref, left_sems.at[0]),
-        pltpu.make_async_copy(left_pair_ref, left_pair_out_ref, left_sems.at[1]),
-    )
-    for copy in lefts:
-        copy.start()
+    carried = pltpu.make_async_copy(left_ref, left_out_ref, left_sems.at[0])
+    carried.start()
 
     def body(i, gain):
         at = pl.ds(pl.multiple_of(i * step, step), step)
@@ -175,8 +171,7 @@
             copy.wait()
         gain = lax.fori_loop(n * height // step, (n + 1) * height // step, body, gain, unroll=3)
     gain_ref[...] = jnp.sum(gain, axis=0, keepdims=True)
-    for copy in lefts:
-        copy.wait()
+    carried.wait()
 
 
 def whole_kernel(core_ref, keep_ref, send_ref, grad_ref):
@@ -198,8 +193,11 @@
             out_ref[b, rows:, :LANES] = jnp.concatenate(lines, axis=0).astype(bf16)
 
 
-def own_kernel(left_ref, right_ref, out_ref):
+def own_kernel(left_ref, right_ref, far_ref, out_ref, pair_ref, sem):
+    carried = pltpu.make_async_copy(far_ref, pair_ref, sem)
+    carried.start()
     out_ref[...] = jnp.dot(left_ref[...], right_ref[...], preferred_element_type=f32)
+    carried.wait()
 
 
 def weight_kernel(gain_rows, core_ref, own_ref, left_pair_ref, right_pair_ref, gain_ref, out_ref):
@@ -317,32 +315,40 @@
     )
 
     chunks = 8
-    grad_keep, grad_send, left, left_pair, gain_part = call(
+    grad_keep, grad_send, left, gain_part = call(
         functools.partial(norm_kernel, chunks, 16),
         "norm_backward",
         (
             shaped(bf16, rows, half),
             shaped(bf16, rows, half),
             shaped(bf16, features, rows),
-            shaped(bf16, features, rows),
             shaped(f32, 1, features),
         ),
-        (core, received.reshape(rows, features), lines, left, left_pair, inverse, gamma.reshape(1, features)),
-        far_in=(1, 2, 3, 4, 5),
-        limit=50,
+        (core, received.reshape(rows, features), lines, left, inverse, gamma.reshape(1, features)),
+        far_in=(1, 2, 3, 4),
+        limit=51.5,
         scratch=[
             pltpu.VMEM((rows, features), bf16),
             pltpu.VMEM((rows, features), bf16),
             pltpu.VMEM((rows, 1), f32),
             pltpu.SemaphoreType.DMA((2 * chunks,)),
-            pltpu.SemaphoreType.DMA((3,)),
+            pltpu.SemaphoreType.DMA((2,)),
         ],
     )
     grad_pair = lax.ppermute(grad_send, "core", swap)
     (grad,) = call(
         whole_kernel, "whole_grad", (shaped(bf16, rows, features),), (core, grad_keep, grad_send), limit=52
     )
-    (own,) = call(own_kernel, "weight_own", (shaped(f32, features, half),), (left, grad_keep), flops=2 * features * half * rows, limit=20)
+    own, left_pair = call(
+        own_kernel,
+        "weight_own",
+        (shaped(f32, features, half), shaped(bf16, features, rows)),
+        (left, grad_keep, left_pair),
+        flops=2 * features * half * rows,
+        far_in=(2,),
+        limit=44,
+        scratch=[pltpu.SemaphoreType.DMA],
+    )
     grad, own = lax.optimization_barrier((grad, own))
 
     replicas = counts[0] * counts[1]

time: 149 us -> 150 us (level)
    unnamed x16 -> x18, local copies, waits for them, and re-layouts: 5.33 us -> 5.33 us
  transfers between devices with their start and end apart: 4 -> 4, of which waited for: 4 -> 3; matrix products, arithmetic and copies ran while one was open for 4% -> 4% of each run, Pallas kernels for 3% -> 3%
where the time goes in v8:
time: 150 us; the launch traced here: 149 us
  blocking collectives  65.8 us (44%)
  waiting for transfers between devices  29 us (19%)
  starting transfers between devices  28 us (19%)
  Pallas kernels  13.7 us (9%)
  local copies, waits for them, and re-layouts  7.92 us (5%)
  matrix products  3.64 us (2%)
    all_to_all x3, blocking collectives, exchange(): lax.all_to_all(blocks, axes, 0, 0, axis_index_groups=groups, tiled=True)  65.8 us
    all_to_all x2, waiting for transfers between devices, exchange(): lax.all_to_all(blocks, axes, 0, 0, axis_index_groups=groups, tiled=True)  26.4 us
    all_to_all x2, starting transfers between devices, exchange(): lax.all_to_all(blocks, axes, 0, 0, axis_index_groups=groups, tiled=True)  21.3 us
    pallas_call x10, Pallas kernels, call(): pl.pallas_call(kernel, name=name, out_shape=outs, in_specs=specs, out_spe...  13.7 us
    unnamed x18, local copies, waits for them, and re-layouts  5.33 us
    ppermute x1, starting transfers between devices, on_device(): grad_pair = lax.ppermute(grad_send, 'core', swap)  4.56 us
    dot_general x1, matrix products, on_device(): lax.dot_general(grad, w_out, (((1,), (1,)), ((), ())), preferred_element_...  3.64 us
  transfers between devices with their start and end apart: 4, of which 3 were waited for; matrix products, arithmetic and copies ran while one was open for 4% of the time, Pallas kernels for 3%

profile of v8, /device:TPU:1, one launch (start us, length us, event | category | flops | bytes accessed | tf_op | source)
XLA Modules:
  0.0 148.9 jit_solution(7499272935308229409)
XLA Ops:
  0.6 0.0 copy-start
  0.6 0.0 copy-start.8
  0.7 3.0 %gather_rows.1 = bf16[384,1280]{1,0:T(8,128)(2,1)} custom-call(s32[1,80]{1,0:T(1,128)} %bitcast.14, bf16[80,4,1280]{2,1,0:T(4,128)(2,1)} %bitcast.13), custom_call_target="tpu_custom_call" | custom-call | flops 1000000 | bytes 1802560 | tf_op jit(solution)/shard_map/gather_rows/pallas_call | solution.py:28
  3.6 16.7 %all-to-all-start = ((bf16[24,16,1280]{2,1,0:T(8,128)(2,1)}), bf16[24,16,1280]{2,1,0:T(8,128)(2,1)}, u32[]{:S(2)}, u32[]{:S(2)}) async-start(bf16[24,16,1280]{2,1,0:T(8,128)(2,1)} %bitcast.12), calls=%async_computation | async-start | bytes 1966080 | tf_op jit(solution)/shard_map/all_to_all | solution.py:41
  20.4 2.2 %collective-permute-start = (bf16[96,4,1280]{2,1,0:T(4,128)(2,1)}, bf16[96,4,1280]{2,1,0:T(4,128)(2,1)}, u32[]{:S(2)}, u32[]{:S(2)}) collective-permute-start(bf16[96,4,1280]{2,1,0:T(4,128)(2,1)} %bitcast.10), channel_id=1, source_target_pairs={{0,1},{1,0},{2,3},{3,2},{4,5},{5,4},{6,7},{7,6},{8,9},{9,8},{10,11... | collective-permute-start | bytes 2949128 | tf_op jit(solution)/shard_map/ppermute | solution.py:304
  22.5 0.0 copy-done.8
  22.6 2.6 %collective-permute-done.pair_ref = bf16[96,4,1280]{2,1,0:T(4,128)(2,1)} collective-permute-done((bf16[96,4,1280]{2,1,0:T(4,128)(2,1)}, bf16[96,4,1280]{2,1,0:T(4,128)(2,1)}, u32[]{:S(2)}, u32[]{:S(2)}) %collective-permute-start) | collective-permute-done | bytes 983072 | tf_op jit(solution)/shard_map/ppermute | solution.py:304
  25.2 0.0 copy-start.1
  25.2 1.2 copy-done.1
  26.4 0.0 copy-start.2
  26.4 1.2 copy-done.2
  27.6 2.7 %prepare.1 = (bf16[384,1280]{1,0:T(8,128)(2,1)S(1)}, f32[384,1]{1,0:T(8,128)S(1)}, bf16[1280,384]{1,0:T(8,128)(2,1)S(1)}, bf16[1280,384]{1,0:T(8,128)(2,1)S(1)}) custom-call(s32[1]{0:T(128)} %bitcast.core_ref, bf16[96,4,1280]{2,1,0:T(4,128)(2,1)S(1)} %bitcast.9, bf16[96,4,1280]{2,1,0:T(4,128)(2,1)S(1)} %bitcast.11, ...), custom_call_target="tpu_custom_call" | custom-call | flops 1000000 | bytes 5899780 | tf_op jit(solution)/shard_map/prepare/pallas_call | solution.py:28
  30.3 0.0 copy-start.4
  30.3 1.0 copy-done.4
  31.3 0.0 copy-start.6
  31.3 1.0 copy-done.6
  32.3 0.0 copy-start.7
  32.3 1.0 copy-done.7
  33.2 23.9 %all-to-all-done = bf16[24,16,1280]{2,1,0:T(8,128)(2,1)} async-done(((bf16[24,16,1280]{2,1,0:T(8,128)(2,1)}), bf16[24,16,1280]{2,1,0:T(8,128)(2,1)}, u32[]{:S(2)}, u32[]{:S(2)}) %all-to-all-start) | async-done | bytes 983072 | tf_op jit(solution)/shard_map/all_to_all | solution.py:41
  57.1 0.0 copy-start.5
  57.1 3.1 %norm_backward.1 = (bf16[384,640]{1,0:T(8,128)(2,1)S(1)}, bf16[384,640]{1,0:T(8,128)(2,1)S(1)}, bf16[1280,384]{1,0:T(8,128)(2,1)S(1)}, f32[1,1280]{1,0:T(1,128)S(1)}) custom-call(s32[1]{0:T(128)} %bitcast.core_ref, bf16[384,1280]{1,0:T(8,128)(2,1)} %bitcast.4.recv_ref, bf16[384,1280]{1,0:T(8,128)(2,1)} %copy-done.6, bf16[1280,384]{1,0:T(8,128)(2,1)} %copy-done.7, ...), custom_call_target="tpu_custom_call" | custom-call | flops 1000000 | bytes 4926980 | tf_op jit(solution)/shard_map/norm_backward/pallas_call | solution.py:28
  60.2 4.6 %collective-permute-start.1 = (bf16[384,640]{1,0:T(8,128)(2,1)S(1)}, bf16[384,640]{1,0:T(8,128)(2,1)S(1)}, u32[]{:S(2)}, u32[]{:S(2)}) collective-permute-start(bf16[384,640]{1,0:T(8,128)(2,1)S(1)} %get-tuple-element.23.send_ref), channel_id=1, source_target_pairs={{0,1},{1,0},{2,3},{3,2},{4,5},{5,4},{6,7},{7,6},{8,9},{9,8},{10,11... | collective-permute-start | bytes 1474568 | tf_op jit(solution)/shard_map/ppermute | solution.py:338
  64.8 0.1 whole_grad.1
  64.9 0.0 copy-start.3
  64.9 0.0 copy-done.5
  64.9 1.4 weight_own.1
  66.3 0.0 collective-permute-done.1.right_pair_ref
  66.3 1.3 weight_pair.1
  67.6 0.0 copy-done.3
  67.6 20.0 %all_to_all.25.in_ref = bf16[8,168,640]{2,1,0:T(8,128)(2,1)S(1)} all-to-all(bf16[8,168,640]{2,1,0:T(8,128)(2,1)S(1)} %weight_pair.1), channel_id=1, replica_groups={{0,2,24,26,192,194,216,218},{4,6,28,30,196,198,220,222},{8,10,32,34,200..., dimensions={0} | all-to-all | bytes 3440640 | tf_op jit(solution)/shard_map/all_to_all | solution.py:41
  87.6 0.3 sum_first.1
  87.9 24.7 %all_to_all.26.in_ref = bf16[48,4,640]{2,1,0:T(4,128)(2,1)S(1)} all-to-all(bf16[48,4,640]{2,1,0:T(4,128)(2,1)S(1)} %sum_first.1), channel_id=1, replica_groups={{0,4,8,12,16,20,48,52,56,60,64,68,96,100,104,108,112,116,144,148,152,15..., dimensions={0} | all-to-all | bytes 491520 | tf_op jit(solution)/shard_map/all_to_all | solution.py:41
  112.6 0.1 sum_second.1
  112.7 21.1 %all_to_all.27.in_ref = bf16[24,4,640]{2,1,0:T(4,128)(2,1)S(1)} all-to-all(bf16[24,4,640]{2,1,0:T(4,128)(2,1)S(1)} %sum_second.1), channel_id=1, replica_groups=mesh['x'=4,'y'=8,'z'=12,'core'=2] {'z','core'}, dimensions={0} | all-to-all | bytes 245760 | tf_op jit(solution)/shard_map/all_to_all | solution.py:41
  133.8 0.8 joined.1
  134.6 4.6 %all-to-all-start.4 = ((f32[32,1,256]{2,1,0:T(1,128)}), f32[32,1,256]{2,1,0:T(1,128)S(1)}, u32[]{:S(2)}, u32[]{:S(2)}) async-start(f32[32,1,256]{2,1,0:T(1,128)} %get-tuple-element.31), calls=%async_computation.4 | async-start | bytes 65536 | tf_op jit(solution)/shard_map/all_to_all | solution.py:41
  139.2 0.0 copy-done
  139.2 3.6 %convolution_convert_fusion = bf16[384,1280]{1,0:T(8,128)(2,1)} fusion(bf16[384,1280]{1,0:T(8,128)(2,1)} %copy-done.3, bf16[1280,1280]{1,0:T(8,128)(2,1)S(1)} %copy-done), kind=kOutput, calls=%fused_computation | convolution fusion | flops 1258782720 | bytes 5242880 | tf_op jit(solution)/shard_map/dot_general | solution.py:382
  142.9 2.6 %reshape.41 = bf16[1,1,96,4,1280]{4,3,2,1,0:T(4,128)(2,1)} reshape(bf16[384,1280]{1,0:T(8,128)(2,1)} %convolution_convert_fusion) | data formatting | bytes 1966080 | tf_op jit(solution)/shard_map/reshape | solution.py:384
  145.4 2.5 %all-to-all-done.4.note_ref = f32[32,1,256]{2,1,0:T(1,128)S(1)} async-done(((f32[32,1,256]{2,1,0:T(1,128)}), f32[32,1,256]{2,1,0:T(1,128)S(1)}, u32[]{:S(2)}, u32[]{:S(2)}) %all-to-all-start.4) | async-done | bytes 32800 | tf_op jit(solution)/shard_map/all_to_all | solution.py:41
  148.0 0.9 scaled.1
  (1 shorter events, 0.0 us)
Async XLA Ops:
  0.6 138.6 %copy-start = (bf16[1280,1280]{1,0:T(8,128)(2,1)S(1)}, bf16[1280,1280]{1,0:T(8,128)(2,1)}, u32[]{:S(2)}) copy-start(bf16[1280,1280]{1,0:T(8,128)(2,1)} %param.11) | copy-start | bytes 9830404
  0.6 21.9 %copy-start.8 = (f32[1280]{0:T(1024)S(1)}, f32[1280]{0:T(1024)}, u32[]{:S(2)}) copy-start(f32[1280]{0:T(1024)} %param.10) | copy-start | bytes 15364
  3.6 53.5 %all-to-all-start = ((bf16[24,16,1280]{2,1,0:T(8,128)(2,1)}), bf16[24,16,1280]{2,1,0:T(8,128)(2,1)}, u32[]{:S(2)}, u32[]{:S(2)}) async-start(bf16[24,16,1280]{2,1,0:T(8,128)(2,1)} %bitcast.12), calls=%async_computation | async-start | bytes 1966080 | tf_op jit(solution)/shard_map/all_to_all | solution.py:41
  20.4 4.8 %collective-permute-start = (bf16[96,4,1280]{2,1,0:T(4,128)(2,1)}, bf16[96,4,1280]{2,1,0:T(4,128)(2,1)}, u32[]{:S(2)}, u32[]{:S(2)}) collective-permute-start(bf16[96,4,1280]{2,1,0:T(4,128)(2,1)} %bitcast.10), channel_id=1, source_target_pairs={{0,1},{1,0},{2,3},{3,2},{4,5},{5,4},{6,7},{7,6},{8,9},{9,8},{10,11... | collective-permute-start | bytes 2949128 | tf_op jit(solution)/shard_map/ppermute | solution.py:304
  25.2 1.2 copy-start.1
  26.4 1.2 copy-start.2
  30.3 1.0 copy-start.4
  31.3 1.0 copy-start.6
  32.3 1.0 copy-start.7
  57.1 7.8 %copy-start.5 = (bf16[1280,384]{1,0:T(8,128)(2,1)S(1)}, bf16[1280,384]{1,0:T(8,128)(2,1)}, u32[]{:S(2)}) copy-start(bf16[1280,384]{1,0:T(8,128)(2,1)} %copy-done.4) | copy-start | bytes 2949124
  60.2 6.1 %collective-permute-start.1 = (bf16[384,640]{1,0:T(8,128)(2,1)S(1)}, bf16[384,640]{1,0:T(8,128)(2,1)S(1)}, u32[]{:S(2)}, u32[]{:S(2)}) collective-permute-start(bf16[384,640]{1,0:T(8,128)(2,1)S(1)} %get-tuple-element.23.send_ref), channel_id=1, source_target_pairs={{0,1},{1,0},{2,3},{3,2},{4,5},{5,4},{6,7},{7,6},{8,9},{9,8},{10,11... | collective-permute-start | bytes 1474568 | tf_op jit(solution)/shard_map/ppermute | solution.py:338
  64.9 2.7 %copy-start.3 = (bf16[384,1280]{1,0:T(8,128)(2,1)}, bf16[384,1280]{1,0:T(8,128)(2,1)S(1)}, u32[]{:S(2)}) copy-start(bf16[384,1280]{1,0:T(8,128)(2,1)S(1)} %whole_grad.1) | copy-start | bytes 2949124
  134.6 13.4 %all-to-all-start.4 = ((f32[32,1,256]{2,1,0:T(1,128)}), f32[32,1,256]{2,1,0:T(1,128)S(1)}, u32[]{:S(2)}, u32[]{:S(2)}) async-start(f32[32,1,256]{2,1,0:T(1,128)} %get-tuple-element.31), calls=%async_computation.4 | async-start | bytes 65536 | tf_op jit(solution)/shard_map/all_to_all | solution.py:41
